TPU v7x, 32 devices: a whole 2x2x4 slice. The times are simulated.
32 devices in a mesh: rep: 4 (over y, x), tile: 8 (over z, core).
Axes of the slice: x: 2, y: 2, z: 4, core: 2. Of those that a mesh axis runs over, the one named last changes fastest.
Arguments:
- feature_tiles: bfloat16 [64, 16, 128, 128], P(('rep', 'tile')), parts along dimension 0, may hold values from -6 to 6
- neighbours: int32 [64, 4], P('rep'), parts along dimension 0, may hold values from -1 to 15, as said below
- valid_rows: int32 [64], P('rep'), parts along dimension 0, may hold values from 4 to 16, as said below
- tile_image: int32 [64], P('rep'), parts along dimension 0, may hold values from 0 to 7, as said below
- gain_one: float32 [128], replicated, may hold values from 0.1 to 1.9
- shift_one: float32 [128], replicated, may hold values from -3 to 3
- kernel_one: bfloat16 [3, 3, 128, 128], replicated, may hold values from -0.1875 to 0.1875
- offset_one: float32 [128], replicated, may hold values from -3 to 3
- gain_two: float32 [128], replicated, may hold values from 0.1 to 1.9
- shift_two: float32 [128], replicated, may hold values from -3 to 3
- kernel_two: bfloat16 [3, 3, 128, 128], replicated, may hold values from -0.1875 to 0.1875
- offset_two: float32 [128], replicated, may hold values from -3 to 3
Outputs:
- block_out: bfloat16 [64, 16, 128, 128], P(('rep', 'tile')), parts along dimension 0
There are 4 independent parts, one for each index of `rep`. A program takes and returns all parts, laid end to end along the dimension named above; an argument that names none is the same for every part. Nothing has to cross between parts.
Inputs may be any that keep to these rules, and one draw needn't show every extreme that they name: Each image is a rectangle of tiles; neighbours name the adjacent tile of the same image in that direction, or -1 at the image's border. `valid_rows`: only tiles in the bottom row of tiles of an image have fewer than 16 rows; all tiles of that row have the same count. `tile_image`: image numbers need not be consecutive; some may be unused.
All inputs are finite; a program needn't handle non-finite values.
Results may differ from a plain program's by a relative error of at most 0.0075.
Values may be sent and summed in bfloat16 or wider, within the bound.
No kernel may reach another device: no remote copies, remote signals or barrier semaphores. Data moves between devices by JAX's collectives and lax.ppermute only.
A program may use at most 64 MiB of HBM per device.

v0:
```python
import functools

import jax
import jax.numpy as jnp
from jax import lax
from jax.experimental import pallas as pl
from jax.experimental.pallas import tpu as pltpu
from jax.sharding import PartitionSpec as P


G = 32
AXIS = "tile"
epsilon = 1e-06
f32 = jnp.float32
bf16 = jnp.bfloat16


VMEM = pl.BlockSpec(memory_space=pltpu.VMEM)
SMEM = pl.BlockSpec(memory_space=pltpu.SMEM)
HBM = pl.BlockSpec(memory_space=pltpu.HBM)


def round_up(value, step):
    return -(-value // step) * step


class Plan:
    def __init__(self, size, count, rows, cols, channels):
        self.size, self.count, self.rows, self.cols, self.channels = size, count, rows, cols, channels
        chips = size // 2
        fits = size % 2 == 0 and chips & (chips - 1) == 0 and cols % (16 * max(chips, 1)) == 0
        self.chunks = chips if fits and chips > 1 else 1
        self.width = cols // self.chunks
        self.stat_rows = round_up(6 * count, 16)
        self.row_base = self.stat_rows
        self.col_base = self.row_base + 2 * count * self.width
        self.buf_rows = self.col_base + 2 * count * rows
        self.slots = size

    def place(self):
        index = lax.axis_index(AXIS)
        return lax.div(index, 2), lax.rem(index, 2)

    def chunk(self, k):
        return lax.bitwise_xor(self.place()[0], k) if self.chunks > 1 else 0

    def slot_of(self, device):
        if self.chunks == 1:
            return device
        chip, core = self.place()
        other = lax.bitwise_xor(lax.rem(device, 2), core)
        return other * self.chunks + lax.bitwise_xor(lax.div(device, 2), chip)

    def device_of(self, slot):
        if self.chunks == 1:
            return slot
        chip, core = self.place()
        return lax.bitwise_xor(chip, slot % self.chunks) * 2 + lax.bitwise_xor(core, slot // self.chunks)

    def target(self, k):
        if self.chunks == 1:
            return lax.axis_index(AXIS)
        chip, core = self.place()
        return lax.bitwise_xor(chip, k) * 2 + core


def split_three(values):
    high = values.astype(bf16)
    rest = values - high.astype(f32)
    middle = rest.astype(bf16)
    low = (rest - middle.astype(f32)).astype(bf16)
    return high.astype(f32), middle.astype(f32), low.astype(f32)


def fold_rows(values):
    return values.reshape(-1, 8, values.shape[-1]).sum(axis=0)


def column_sums(values_of, rows, valid):
    pixels = jnp.int32(0)
    total = None
    for row in rows:
        values = values_of(row)
        inside = row < valid
        pixels = pixels + jnp.where(inside, values.shape[0], 0)
        part = jnp.where(inside, fold_rows(values), 0.0)
        total = part if total is None else total + part
    total = jnp.sum(total, axis=0, keepdims=True)
    mean = total / jnp.maximum(pixels, 1).astype(f32)
    spread = None
    for row in rows:
        apart = values_of(row) - mean
        part = jnp.where(row < valid, fold_rows(apart * apart), 0.0)
        spread = part if spread is None else spread + part
    return pixels.astype(f32), total, jnp.sum(spread, axis=0, keepdims=True)


def pack_stats(plan, sums, spreads):
    parts = list(split_three(jnp.concatenate(sums + spreads, axis=0)))
    padding = plan.stat_rows - 6 * plan.count
    if padding:
        parts.append(jnp.zeros((padding, plan.channels), f32))
    return jnp.concatenate(parts, axis=0).astype(bf16)


def fill_buffers(plan, stats, edge_of, columns, buf_refs):
    for k in range(plan.chunks):
        buf_refs[k][0 : plan.stat_rows, :] = stats
        start = plan.chunk(k) * plan.width
        if plan.chunks > 1:
            start = pl.multiple_of(start, 16)
        for tile in range(plan.count):
            for edge in range(2):
                at = plan.row_base + (2 * tile + edge) * plan.width
                buf_refs[k][at : at + plan.width, :] = edge_of(tile, edge, pl.ds(start, plan.width))
        for place, column in enumerate(columns):
            at = plan.col_base + place * plan.rows
            buf_refs[k][at : at + plan.rows, :] = column


def own_values(plan, ref):
    first = lax.axis_index(AXIS) * plan.count
    return [ref[first + tile] for tile in range(plan.count)]


def edges_kernel(plan, rows_hbm, x_hbm, *refs):
    buf_refs, (rows_ref, x_ref, sems) = refs[: plan.chunks], refs[plan.chunks :]
    counts = pltpu.make_async_copy(rows_hbm, rows_ref, sems.at[plan.count])
    counts.start()
    copies = [pltpu.make_async_copy(x_hbm.at[tile], x_ref.at[tile], sems.at[tile]) for tile in range(plan.count)]
    for copy in copies:
        copy.start()
    counts.wait()
    own_rows = own_values(plan, rows_ref)
    sums, spreads, columns = [], [], []
    for tile in range(plan.count):
        copies[tile].wait()
        _, total, spread = column_sums(lambda row: x_ref[tile, row].astype(f32), range(plan.rows), own_rows[tile])
        sums.append(total)
        spreads.append(spread)
        for column in (0, plan.cols - 1):
            picked = [x_ref[tile, row, column : column + 1, :].astype(f32) for row in range(plan.rows)]
            columns.append(jnp.concatenate(picked, axis=0).astype(bf16))

    def edge_of(tile, edge, window):
        return x_ref[tile, edge * (plan.rows - 1), window, :]

    fill_buffers(plan, pack_stats(plan, sums, spreads), edge_of, columns, buf_refs)


def group_total(values, group_width):
    lanes = values.shape[-1]
    lane = lax.broadcasted_iota(jnp.int32, values.shape, 1)
    step = 1
    while step < group_width:
        ahead = pltpu.roll(values, lanes - step, axis=1)
        behind = pltpu.roll(values, step, axis=1)
        values = values + jnp.where(lax.bitwise_and(lane, step) == 0, ahead, behind)
        step *= 2
    return values


class Held:
    def __init__(self, plan, bufs, held):
        self.plan = plan
        if plan.chunks > 1:
            for slot in range(plan.slots):
                held[slot] = bufs[slot][...]
            self.held = held
        else:
            self.held = bufs[0]

    def locate(self, tile):
        tile = jnp.maximum(tile, 0)
        return self.plan.slot_of(lax.div(tile, self.plan.count)), lax.rem(tile, self.plan.count)

    def edge_row(self, tile, edge):
        slot, local = self.locate(tile)
        at = pl.multiple_of(self.plan.row_base + (2 * local + edge) * self.plan.width, 16)
        return self.held[slot, pl.ds(at, self.plan.width), :]

    def edge_col(self, tile, edge):
        slot, local = self.locate(tile)
        at = pl.multiple_of(self.plan.col_base + (2 * local + edge) * self.plan.rows, 16)
        return self.held[slot, pl.ds(at, self.plan.rows), :]


def buffer_inputs(plan, refs):
    inputs = plan.slots if plan.chunks > 1 else 1
    return refs[:inputs], refs[inputs:]


def route_kernel(plan, links_ref, *refs):
    bufs, refs = buffer_inputs(plan, refs)
    send_refs, held = refs[:-1], Held(plan, bufs, refs[-1])
    for k in range(plan.chunks):
        first = plan.target(k) * plan.count
        for tile in range(plan.count):
            for edge in range(2):
                at = (2 * tile + edge) * plan.width
                wanted = links_ref[(first + tile) * 4 + edge]
                send_refs[k][at : at + plan.width, :] = held.edge_row(wanted, 1 - edge)


def image_norms(plan, rows_ref, image_ref, held):
    count, channels = plan.count, plan.channels
    group_width = channels // G
    first = lax.axis_index(AXIS) * count
    partial = []
    for slot in range(plan.slots):
        raw = held[slot, 0 : plan.stat_rows, :].astype(f32)
        span = 2 * count
        partial.append(raw[0:span] + raw[span : 2 * span] + raw[2 * span : 3 * span])
    means, inverses = [], []
    for tile in range(count):
        image = image_ref[first + tile]
        weights, pixels = [], []
        area = jnp.int32(0)
        for slot in range(plan.slots):
            base = plan.device_of(slot) * count
            for other in range(count):
                same = image_ref[base + other] == image
                weights.append(jnp.where(same, 1.0, 0.0).astype(f32))
                amount = rows_ref[base + other] * plan.cols
                pixels.append(jnp.maximum(amount, 1).astype(f32))
                area = area + jnp.where(same, amount, 0)
        total = jnp.zeros((1, channels), f32)
        for slot in range(plan.slots):
            for other in range(count):
                total = total + weights[slot * count + other] * partial[slot][other : other + 1]
        amount = jnp.maximum(area * group_width, 1).astype(f32)
        mean = group_total(jnp.broadcast_to(total, (8, channels)), group_width)[0:1] / amount
        total = jnp.zeros((1, channels), f32)
        for slot in range(plan.slots):
            for other in range(count):
                place = slot * count + other
                apart = partial[slot][other : other + 1] / pixels[place] - mean
                spread = partial[slot][count + other : count + other + 1] + pixels[place] * apart * apart
                total = total + weights[place] * spread
        variance = group_total(jnp.broadcast_to(total, (8, channels)), group_width)[0:1] / amount
        means.append(mean)
        inverses.append(lax.rsqrt(variance + epsilon))
    return means, inverses


def halves(mean, inverse, gain_ref, shift_ref):
    scale = inverse * (gain_ref[...] * 0.5)
    shift = shift_ref[...] * 0.5

    def activate(values):
        half = (values.astype(f32) - mean) * scale + shift
        return half + half * jnp.tanh(half)

    return activate


def taps(act, before, after):
    cols = act.shape[0]
    pixel = lax.broadcasted_iota(jnp.int32, act.shape, 0)
    back = jnp.where(pixel == 0, before, pltpu.roll(act, 1, axis=0))
    ahead = jnp.where(pixel == cols - 1, after, pltpu.roll(act, cols - 1, axis=0))
    return [values.astype(bf16) for values in (back, act, ahead)]


def middle_kernel(plan, last, links_ref, rows_ref, image_ref, *refs):
    bufs, refs = buffer_inputs(plan, refs)
    x_ref, gain_ref, shift_ref, offset_ref, weight_ref = refs[:5]
    refs = refs[5:]
    ends_ref = residual_ref = None
    if last:
        (ends_ref, residual_ref), refs = refs[:2], refs[2:]
    out_ref, partial_ref, norm_ref, side_ref, held_ref, wide = refs[:6]
    refs = refs[6:]
    count, rows, cols, channels = plan.count, plan.rows, plan.cols, plan.channels
    held = Held(plan, bufs, held_ref)
    means, inverses = image_norms(plan, rows_ref, image_ref, held.held)
    first = lax.axis_index(AXIS) * count
    own_rows = own_values(plan, rows_ref)
    offset = offset_ref[...]
    norm_ref[0 : 2 * count, :] = jnp.concatenate(means + inverses, axis=0)
    copies = []
    for tile in range(count):
        valid = own_rows[tile]
        link = [links_ref[(first + tile) * 4 + column] for column in range(4)]
        activate = halves(means[tile], inverses[tile], gain_ref, shift_ref)
        left = jnp.where(link[2] >= 0, activate(held.edge_col(link[2], 1)), 0.0)
        right = jnp.where(link[3] >= 0, activate(held.edge_col(link[3], 0)), 0.0)
        corners = []
        for place in range(4):
            beside = links_ref[jnp.maximum(link[place // 2], 0) * 4 + 2 + place % 2]
            beside = jnp.where(link[place // 2] >= 0, beside, -1)
            row = 0 if place // 2 else rows - 1
            corner = activate(held.edge_col(beside, 1 - place % 2))[row : row + 1]
            corners.append(jnp.where(beside >= 0, corner, 0.0))
        side_ref[8 * tile : 8 * tile + 4, :] = jnp.concatenate(corners, axis=0)

        depth = 3 * channels
        nothing = jnp.zeros((cols, depth), bf16)
        wide[tile, 0, :, 0:depth] = nothing
        wide[tile, rows // 2, :, depth : 2 * depth] = nothing
        for row in range(rows):
            if ends_ref is not None and row in (0, rows - 1):
                source = ends_ref[2 * tile + (row > 0)]
            else:
                source = x_ref[tile, row]
            act = jnp.where(row < valid, activate(source), 0.0)
            before = jnp.where(row < valid, left[row : row + 1], 0.0)
            after = jnp.where(row < valid, right[row : row + 1], 0.0)
            lane = ((row + 1) % 2) * depth
            for tap, values in enumerate(taps(act, before, after)):
                at = lane + tap * channels
                wide[tile, (row + 1) // 2, :, at : at + channels] = values

        pairs = rows // 2
        upper = wide[tile, 0:pairs].reshape(pairs * cols, 2 * depth)
        lower = wide[tile, 1 : pairs + 1].reshape(pairs * cols, 2 * depth)
        summed = jnp.dot(upper, weight_ref[0 : 2 * depth, :], preferred_element_type=f32)
        summed = summed + jnp.dot(lower, weight_ref[2 * depth : 4 * depth, :], preferred_element_type=f32)
        for row in range(rows):
            at, lane = (row // 2) * cols, (row % 2) * channels
            part = summed[at : at + cols, lane : lane + channels] + offset
            if last:
                part = part + residual_ref[tile, row].astype(f32)
            if row in (0, rows - 1):
                partial_ref[2 * tile + (row > 0)] = part
            elif last:
                refs[0][tile, row] = jnp.where(row < valid, part, 0.0).astype(bf16)
            else:
                out_ref[tile, row] = jnp.where(row < valid, part, 0.0).astype(bf16)
        if last:
            window = pl.ds(1, rows - 2)
            copy = pltpu.make_async_copy(refs[0].at[tile, window], out_ref.at[tile, window], refs[1].at[tile])
            copy.start()
            copies.append(copy)
        else:
            _, total, spread = column_sums(
                lambda row: out_ref[tile, row].astype(f32), range(1, rows - 1), valid
            )
            norm_ref[(2 * count + tile) : (2 * count + tile) + 1, :] = total
            norm_ref[(3 * count + tile) : (3 * count + tile) + 1, :] = spread
            for side, column in enumerate((0, cols - 1)):
                picked = [out_ref[tile, row, column : column + 1, :].astype(f32) for row in range(1, rows - 1)]
                at = 8 * count + (2 * tile + side) * rows
                side_ref[at + 1 : at + rows - 1, :] = jnp.concatenate(picked, axis=0)
    for copy in copies:
        copy.wait()


def ends_kernel(plan, last, links_ref, rows_ref, *refs):
    halo_refs, refs = refs[: plan.chunks], refs[plan.chunks :]
    partial_ref, norm_ref, side_ref, gain_ref, shift_ref, weight_ref = refs[:6]
    refs = refs[6:]
    count, rows, cols, channels = plan.count, plan.rows, plan.cols, plan.channels
    if last:
        _, out_ref, halo, ends_ref, sems = refs
    else:
        ends_ref, buf_refs, halo = refs[0], refs[1:-1], refs[-1]
    first = lax.axis_index(AXIS) * count
    own_rows = own_values(plan, rows_ref)
    for k in range(plan.chunks):
        start = plan.chunk(k) * plan.width
        if plan.chunks > 1:
            start = pl.multiple_of(start, 16)
        for place in range(2 * count):
            at = place * plan.width
            halo[place, pl.ds(start, plan.width), :] = halo_refs[k][at : at + plan.width, :]
    depth = 3 * channels
    copies, sums, spreads, columns = [], [], [], []
    for tile in range(count):
        valid = own_rows[tile]
        activate = halves(
            norm_ref[tile : tile + 1, :], norm_ref[count + tile : count + tile + 1, :], gain_ref, shift_ref
        )
        values = []
        for edge, row in enumerate((0, rows - 1)):
            place = 2 * tile + edge
            present = links_ref[(first + tile) * 4 + edge] >= 0
            act = jnp.where(present, activate(halo[place]), 0.0)
            at = 8 * tile + 2 * edge
            wide = jnp.concatenate(taps(act, side_ref[at : at + 1, :], side_ref[at + 1 : at + 2, :]), axis=1)
            weight = weight_ref[3 * edge * depth : (3 * edge + 1) * depth, edge * channels : (edge + 1) * channels]
            part = partial_ref[place] + jnp.dot(wide, weight, preferred_element_type=f32)
            result = jnp.where(row < valid, part, 0.0).astype(bf16)
            ends_ref[place] = result
            values.append(result.astype(f32))
            if last:
                copies.append(pltpu.make_async_copy(ends_ref.at[place], out_ref.at[tile, row], sems.at[place]))
                copies[-1].start()
        if last:
            continue
        amount, total, spread = column_sums(lambda row: values[row > 0], (0, rows - 1), valid)
        inner_total = norm_ref[2 * count + tile : 2 * count + tile + 1, :]
        inner_spread = norm_ref[3 * count + tile : 3 * count + tile + 1, :]
        inner = jnp.maximum((jnp.minimum(valid, rows - 1) - 1) * cols, 1).astype(f32)
        amount = jnp.maximum(amount, 1.0)
        apart = inner_total / inner - total / amount
        sums.append(inner_total + total)
        spreads.append(inner_spread + spread + apart * apart * (inner * amount / (inner + amount)))
        line = lax.broadcasted_iota(jnp.int32, (rows, channels), 0)
        for side, column in enumerate((0, cols - 1)):
            at = 8 * count + (2 * tile + side) * rows
            picked = side_ref[at : at + rows, :]
            picked = jnp.where(line == 0, values[0][column : column + 1], picked)
            picked = jnp.where(line == rows - 1, values[1][column : column + 1], picked)
            columns.append(picked.astype(bf16))
    if not last:

        def edge_of(tile, edge, window):
            return ends_ref[2 * tile + edge, window, :]

        fill_buffers(plan, pack_stats(plan, sums, spreads), edge_of, columns, buf_refs)
    for copy in copies:
        copy.wait()


def paired_weights(kernel):
    upper = jnp.pad(kernel, ((0, 1), (0, 0), (0, 0), (0, 0)))
    lower = jnp.pad(kernel, ((1, 0), (0, 0), (0, 0), (0, 0)))
    both = jnp.concatenate([upper, lower], axis=-1)
    return both.reshape(-1, both.shape[-1])


def shards(
    feature_tiles,
    neighbours,
    valid_rows,
    tile_image,
    gain_one,
    shift_one,
    kernel_one,
    offset_one,
    gain_two,
    shift_two,
    kernel_two,
    offset_two,
    *,
    size,
):
    count, rows, cols, channels = feature_tiles.shape
    plan = Plan(size, count, rows, cols, channels)
    links = neighbours.reshape(-1)
    scalars = (links, valid_rows, tile_image)
    buf_shape = [jax.ShapeDtypeStruct((plan.buf_rows, channels), bf16)] * plan.chunks
    limit = 24 * 1024 * 1024
    params = pltpu.CompilerParams(vmem_limit_bytes=limit)

    def swap(array, distance):
        return lax.ppermute(array, AXIS, [(i, i ^ distance) for i in range(size)])

    def spread(arrays):
        result = [arrays[0]]
        for k in range(1, plan.chunks):
            result.append(swap(arrays[k], 2 * k))
        return result

    def exchange(bufs):
        if plan.chunks == 1:
            return [lax.all_gather(bufs[0], AXIS)]
        own = spread(bufs)
        return own + [swap(array, 1) for array in own]

    def shape(dims, dtype=f32):
        return jax.ShapeDtypeStruct(dims, dtype)

    held = pltpu.VMEM((plan.slots, plan.buf_rows, channels) if plan.chunks > 1 else (1, 16, channels), bf16)
    partial_shape = shape((2 * count, cols, channels))
    norm_shape = shape((round_up(4 * count, 8), channels))
    side_shape = shape((8 * count + 2 * count * rows, channels))
    ends_shape = shape((2 * count, cols, channels), bf16)
    tiles_shape = shape(feature_tiles.shape, bf16)

    def stage(last, source, ends, bufs, gain, shift, kernel, offset):
        arrays = exchange(bufs)
        send = pl.pallas_call(
            functools.partial(route_kernel, plan),
            out_shape=[shape((2 * count * plan.width, channels), bf16)] * plan.chunks,
            in_specs=[SMEM] + [VMEM] * len(arrays),
            out_specs=[VMEM] * plan.chunks,
            scratch_shapes=[held],
            compiler_params=params,
        )(links, *arrays)
        halo = spread(send)
        weights = paired_weights(kernel)
        gain, shift, offset = gain[None], shift[None], offset[None]
        operands = arrays + [source, gain, shift, offset, weights] + ([ends, feature_tiles] if last else [])
        flops = 2 * count * rows * cols * 9 * channels * channels
        tiles, partial, norm, side = pl.pallas_call(
            functools.partial(middle_kernel, plan, last),
            out_shape=[tiles_shape, partial_shape, norm_shape, side_shape],
            in_specs=[SMEM] * 3 + [VMEM] * len(operands),
            out_specs=[HBM if last else VMEM] + [VMEM] * 3,
            scratch_shapes=[held, pltpu.VMEM((count, rows // 2 + 1, cols, 6 * channels), bf16)]
            + ([pltpu.VMEM(feature_tiles.shape, bf16), pltpu.SemaphoreType.DMA((count,))] if last else []),
            compiler_params=params,
            cost_estimate=pl.CostEstimate(flops=flops, bytes_accessed=4 * feature_tiles.size, transcendentals=0),
        )(*scalars, *operands)
        operands = halo + [partial, norm, side, gain, shift, weights]
        scratch = [pltpu.VMEM((2 * count, cols, channels), bf16)]
        if last:
            return pl.pallas_call(
                functools.partial(ends_kernel, plan, last),
                out_shape=tiles_shape,
                in_specs=[SMEM] * 2 + [VMEM] * len(operands) + [HBM],
                out_specs=HBM,
                input_output_aliases={2 + len(operands): 0},
                scratch_shapes=scratch + scratch + [pltpu.SemaphoreType.DMA((2 * count,))],
                compiler_params=params,
            )(links, valid_rows, *operands, tiles)
        ends, *bufs = pl.pallas_call(
            functools.partial(ends_kernel, plan, last),
            out_shape=[ends_shape] + buf_shape,
            in_specs=[SMEM] * 2 + [VMEM] * len(operands),
            out_specs=[VMEM] * (1 + plan.chunks),
            scratch_shapes=scratch,
            compiler_params=params,
        )(links, valid_rows, *operands)
        return tiles, ends, bufs

    bufs = pl.pallas_call(
        functools.partial(edges_kernel, plan),
        out_shape=buf_shape,
        in_specs=[HBM, HBM],
        out_specs=[VMEM] * plan.chunks,
        scratch_shapes=[
            pltpu.SMEM(valid_rows.shape, jnp.int32),
            pltpu.VMEM(feature_tiles.shape, bf16),
            pltpu.SemaphoreType.DMA((count + 1,)),
        ],
        compiler_params=params,
        name="edges",
    )(valid_rows, feature_tiles)
    hidden, ends, bufs = stage(False, feature_tiles, None, bufs, gain_one, shift_one, kernel_one, offset_one)
    return stage(True, hidden, ends, bufs, gain_two, shift_two, kernel_two, offset_two)


def solution(mesh):
    in_specs = (
        P(("rep", "tile"), None, None, None),
        P("rep", None),
        P("rep"),
        P("rep"),
        P(),
        P(),
        P(),
        P(),
        P(),
        P(),
        P(),
        P(),
    )
    out_specs = P(("rep", "tile"), None, None, None)

    def body(*args):
        return shards(*args, size=mesh.shape[AXIS])

    return jax.shard_map(body, mesh=mesh, in_specs=in_specs, out_specs=out_specs, check_vma=False)
```

profile of v0, /device:TPU:0, one launch (start us, length us, event | category | flops | bytes accessed | tf_op | source)
XLA Modules:
  0.0 46.6 jit_solution(11088057778493192019)
XLA Ops:
  0.0 1.2 %copy-done = bf16[2,16,128,128]{3,2,1,0:T(8,128)(2,1)S(1)} copy-done((bf16[2,16,128,128]{3,2,1,0:T(8,128)(2,1)S(1)}, bf16[2,16,128,128]{3,2,1,0:T(8,128)(2,1)}, u32[]{:S(2)}) %copy-start) | copy-done | bytes 1048600
  1.2 0.7 %copy-done.2 = s32[16]{0:T(128)S(1)} copy-done((s32[16]{0:T(128)S(1)}, s32[16]{0:T(128)}, u32[]{:S(2)}) %copy-start.2) | copy-done | bytes 88
  1.9 0.0 copy-start.5
  1.9 0.0 copy-start.8
  1.9 0.0 copy-start.9
  1.9 1.0 %edges.1 = (bf16[208,128]{1,0:T(8,128)(2,1)S(1)}, bf16[208,128]{1,0:T(8,128)(2,1)S(1)}, bf16[208,128]{1,0:T(8,128)(2,1)S(1)}, bf16[208,128]{1,0:T(8,128)(2,1)S(1)}) custom-call(s32[16]{0:T(128)S(1)} %copy-done.2, bf16[2,16,128,128]{3,2,1,0:T(8,128)(2,1)S(1)} %copy-done), custom_call_target="tpu_custom_call" | custom-call | tf_op jit(solution)/shard_map/edges/pallas_call | solution.py:519
  2.9 3.1 %collective-permute-start = (bf16[208,128]{1,0:T(8,128)(2,1)S(1)}, bf16[208,128]{1,0:T(8,128)(2,1)S(1)}, u32[]{:S(2)}, u32[]{:S(2)}) collective-permute-start(bf16[208,128]{1,0:T(8,128)(2,1)S(1)} %get-tuple-element.31), channel_id=1, source_target_pairs={{0,2},{1,3},{2,0},{3,1},{4,6},{5,7},{6,4},{7,5},{8,10},{9,11},{10,... | collective-permute-start | bytes 159752 | tf_op jit(solution)/shard_map/ppermute | solution.py:448
  6.1 2.6 %collective-permute-start.1 = (bf16[208,128]{1,0:T(8,128)(2,1)S(1)}, bf16[208,128]{1,0:T(8,128)(2,1)S(1)}, u32[]{:S(2)}, u32[]{:S(2)}) collective-permute-start(bf16[208,128]{1,0:T(8,128)(2,1)S(1)} %get-tuple-element.32), channel_id=1, source_target_pairs={{0,4},{1,5},{2,6},{3,7},{4,0},{5,1},{6,2},{7,3},{8,12},{9,13},{10,... | collective-permute-start | bytes 159752 | tf_op jit(solution)/shard_map/ppermute | solution.py:448
  8.6 0.0 collective-permute-start.2
  8.7 0.0 collective-permute-start.3
  8.7 0.0 collective-permute-done.refs_1_
  8.7 0.5 %collective-permute-start.4 = (bf16[208,128]{1,0:T(8,128)(2,1)S(1)}, bf16[208,128]{1,0:T(8,128)(2,1)S(1)}, u32[]{:S(2)}, u32[]{:S(2)}) collective-permute-start(bf16[208,128]{1,0:T(8,128)(2,1)S(1)} %collective-permute-done.refs_1_), channel_id=1, source_target_pairs={{0,1},{1,0},{2,3},{3,2},{4,5},{5,4},{6,7},{7,6},{8,9},{9,8},{10,11... | collective-permute-start | bytes 159752 | tf_op jit(solution)/shard_map/ppermute | solution.py:448
  9.2 2.9 %collective-permute-done.1.refs_2_ = bf16[208,128]{1,0:T(8,128)(2,1)S(1)} collective-permute-done((bf16[208,128]{1,0:T(8,128)(2,1)S(1)}, bf16[208,128]{1,0:T(8,128)(2,1)S(1)}, u32[]{:S(2)}, u32[]{:S(2)}) %collective-permute-start.1) | collective-permute-done | bytes 53280 | tf_op jit(solution)/shard_map/ppermute | solution.py:448
  12.1 0.0 collective-permute-start.5
  12.1 2.5 %collective-permute-done.2.refs_3_ = bf16[208,128]{1,0:T(8,128)(2,1)S(1)} collective-permute-done((bf16[208,128]{1,0:T(8,128)(2,1)S(1)}, bf16[208,128]{1,0:T(8,128)(2,1)S(1)}, u32[]{:S(2)}, u32[]{:S(2)}) %collective-permute-start.2) | collective-permute-done | bytes 53280 | tf_op jit(solution)/shard_map/ppermute | solution.py:448
  14.6 0.0 collective-permute-start.6
  14.6 1.1 %fusion.4 = bf16[4,3,128,256]{3,2,1,0:T(8,128)(2,1)S(1)} fusion(bf16[3,3,128,128]{3,2,1,0:T(8,128)(2,1)} %param.18), kind=kLoop, calls=%fused_computation.6 | loop fusion | flops 3145728 | bytes 1081344 | tf_op jit(solution)/shard_map/concatenate | solution.py:419
  15.7 0.0 copy-done.12
  15.7 0.1 copy.15
  15.8 0.1 reshape.9.links_ref
  15.9 0.0 collective-permute-done.3.refs_4_
  15.9 0.0 collective-permute-done.4.refs_5_
  15.9 0.0 collective-permute-done.5.refs_6_
  15.9 0.0 collective-permute-done.6.refs_7_
  15.9 0.7 %shard_map.118 = (bf16[128,128]{1,0:T(8,128)(2,1)S(1)}, bf16[128,128]{1,0:T(8,128)(2,1)S(1)}, bf16[128,128]{1,0:T(8,128)(2,1)S(1)}, bf16[128,128]{1,0:T(8,128)(2,1)S(1)}) custom-call(s32[64]{0:T(128)S(1)} %reshape.9.links_ref, bf16[208,128]{1,0:T(8,128)(2,1)S(1)} %get-tuple-element.30.refs_0_, bf16[208,128]{1,0:T(8,128)(2,1)S(1)} %collective-permute-done.refs_1_, ...), custom_call_target="tpu_custom_call" | custom-call | tf_op jit(solution)/shard_map/pallas_call | solution.py:474
  16.6 0.1 collective-permute-start.7
  16.7 2.1 %collective-permute-start.8 = (bf16[128,128]{1,0:T(8,128)(2,1)S(1)}, bf16[128,128]{1,0:T(8,128)(2,1)S(1)}, u32[]{:S(2)}, u32[]{:S(2)}) collective-permute-start(bf16[128,128]{1,0:T(8,128)(2,1)S(1)} %get-tuple-element.36), channel_id=1, source_target_pairs={{0,4},{1,5},{2,6},{3,7},{4,0},{5,1},{6,2},{7,3},{8,12},{9,13},{10,... | collective-permute-start | bytes 98312 | tf_op jit(solution)/shard_map/ppermute | solution.py:448
  18.7 2.3 %collective-permute-start.9 = (bf16[128,128]{1,0:T(8,128)(2,1)S(1)}, bf16[128,128]{1,0:T(8,128)(2,1)S(1)}, u32[]{:S(2)}, u32[]{:S(2)}) collective-permute-start(bf16[128,128]{1,0:T(8,128)(2,1)S(1)} %get-tuple-element.37), channel_id=1, source_target_pairs={{0,6},{1,7},{2,4},{3,5},{4,2},{5,3},{6,0},{7,1},{8,14},{9,15},{10,... | collective-permute-start | bytes 98312 | tf_op jit(solution)/shard_map/ppermute | solution.py:448
  21.0 0.0 copy-done.1
  21.1 0.0 copy-done.3
  21.1 0.0 copy-done.4
  21.1 3.8 %shard_map.119 = (bf16[2,16,128,128]{3,2,1,0:T(8,128)(2,1)S(1)}, f32[4,128,128]{2,1,0:T(8,128)S(1)}, f32[8,128]{1,0:T(8,128)S(1)}, f32[80,128]{1,0:T(8,128)S(1)}) custom-call(s32[64]{0:T(128)S(1)} %reshape.9.links_ref, s32[16]{0:T(128)S(1)} %copy-done.3, s32[16]{0:T(128)S(1)} %copy-done.9, bf16[208,128]{1,0:T(8,128)(2,1)S(1)} %get-tuple-element.30.refs_0_, ...), custom_call_target="tpu_custom_call" | custom-call | flops 1207959552 | bytes 2097152 | tf_op jit(solution)/shard_map/pallas_call | solution.py:487
  24.9 0.0 copy-start.11
  24.9 0.0 collective-permute-done.7.refs_1_
  24.9 0.0 collective-permute-done.8.refs_2_
  24.9 0.0 collective-permute-done.9.refs_3_
  24.9 0.9 %shard_map.120 = (bf16[4,128,128]{2,1,0:T(8,128)(2,1)S(1)}, bf16[208,128]{1,0:T(8,128)(2,1)S(1)}, bf16[208,128]{1,0:T(8,128)(2,1)S(1)}, bf16[208,128]{1,0:T(8,128)(2,1)S(1)}, bf16[208,128]{1,0:T(8,128)(2,1)S(1)}) custom-call(s32[64]{0:T(128)S(1)} %reshape.9.links_ref, s32[16]{0:T(128)S(1)} %copy-done.3, bf16[128,128]{1,0:T(8,128)(2,1)S(1)} %get-tuple-element.34.refs_0_, ...), custom_call_target="tpu_custom_call" | custom-call | tf_op jit(solution)/shard_map/pallas_call | solution.py:509
  25.9 0.0 copy-start.7
  25.9 0.0 copy-start.10
  25.9 0.1 collective-permute-start.10
  26.0 2.4 %collective-permute-start.11 = (bf16[208,128]{1,0:T(8,128)(2,1)S(1)}, bf16[208,128]{1,0:T(8,128)(2,1)S(1)}, u32[]{:S(2)}, u32[]{:S(2)}) collective-permute-start(bf16[208,128]{1,0:T(8,128)(2,1)S(1)} %get-tuple-element.43), channel_id=1, source_target_pairs={{0,4},{1,5},{2,6},{3,7},{4,0},{5,1},{6,2},{7,3},{8,12},{9,13},{10,... | collective-permute-start | bytes 159752 | tf_op jit(solution)/shard_map/ppermute | solution.py:448
  28.3 2.0 %collective-permute-start.12 = (bf16[208,128]{1,0:T(8,128)(2,1)S(1)}, bf16[208,128]{1,0:T(8,128)(2,1)S(1)}, u32[]{:S(2)}, u32[]{:S(2)}) collective-permute-start(bf16[208,128]{1,0:T(8,128)(2,1)S(1)} %get-tuple-element.44), channel_id=1, source_target_pairs={{0,6},{1,7},{2,4},{3,5},{4,2},{5,3},{6,0},{7,1},{8,14},{9,15},{10,... | collective-permute-start | bytes 159752 | tf_op jit(solution)/shard_map/ppermute | solution.py:448
  30.3 0.0 collective-permute-start.13
  30.3 0.0 collective-permute-done.10.refs_1_
  30.3 0.5 %collective-permute-start.14 = (bf16[208,128]{1,0:T(8,128)(2,1)S(1)}, bf16[208,128]{1,0:T(8,128)(2,1)S(1)}, u32[]{:S(2)}, u32[]{:S(2)}) collective-permute-start(bf16[208,128]{1,0:T(8,128)(2,1)S(1)} %collective-permute-done.10.refs_1_), channel_id=1, source_target_pairs={{0,1},{1,0},{2,3},{3,2},{4,5},{5,4},{6,7},{7,6},{8,9},{9,8},{10,11... | collective-permute-start | bytes 159752 | tf_op jit(solution)/shard_map/ppermute | solution.py:448
  30.8 1.8 %collective-permute-done.11.refs_2_ = bf16[208,128]{1,0:T(8,128)(2,1)S(1)} collective-permute-done((bf16[208,128]{1,0:T(8,128)(2,1)S(1)}, bf16[208,128]{1,0:T(8,128)(2,1)S(1)}, u32[]{:S(2)}, u32[]{:S(2)}) %collective-permute-start.11) | collective-permute-done | bytes 53280 | tf_op jit(solution)/shard_map/ppermute | solution.py:448
  32.6 0.0 collective-permute-start.15
  32.6 1.6 %collective-permute-done.12.refs_3_ = bf16[208,128]{1,0:T(8,128)(2,1)S(1)} collective-permute-done((bf16[208,128]{1,0:T(8,128)(2,1)S(1)}, bf16[208,128]{1,0:T(8,128)(2,1)S(1)}, u32[]{:S(2)}, u32[]{:S(2)}) %collective-permute-start.12) | collective-permute-done | bytes 53280 | tf_op jit(solution)/shard_map/ppermute | solution.py:448
  34.3 0.0 collective-permute-start.16
  34.3 0.0 copy-done.11
  34.3 0.1 fusion.5
  34.3 0.0 collective-permute-done.13.refs_4_
  34.4 0.0 collective-permute-done.14.refs_5_
  34.4 0.0 collective-permute-done.15.refs_6_
  34.4 1.1 %collective-permute-done.16.refs_7_ = bf16[208,128]{1,0:T(8,128)(2,1)S(1)} collective-permute-done((bf16[208,128]{1,0:T(8,128)(2,1)S(1)}, bf16[208,128]{1,0:T(8,128)(2,1)S(1)}, u32[]{:S(2)}, u32[]{:S(2)}) %collective-permute-start.16) | collective-permute-done | bytes 53280 | tf_op jit(solution)/shard_map/ppermute | solution.py:448
  35.5 0.6 %shard_map.121 = (bf16[128,128]{1,0:T(8,128)(2,1)S(1)}, bf16[128,128]{1,0:T(8,128)(2,1)S(1)}, bf16[128,128]{1,0:T(8,128)(2,1)S(1)}, bf16[128,128]{1,0:T(8,128)(2,1)S(1)}) custom-call(s32[64]{0:T(128)S(1)} %reshape.9.links_ref, bf16[208,128]{1,0:T(8,128)(2,1)S(1)} %get-tuple-element.41.refs_0_, bf16[208,128]{1,0:T(8,128)(2,1)S(1)} %collective-permute-done.10.refs_1_, ...), custom_call_target="tpu_custom_call" | custom-call | tf_op jit(solution)/shard_map/pallas_call | solution.py:474
  36.2 0.1 collective-permute-start.17
  36.2 2.6 %collective-permute-start.18 = (bf16[128,128]{1,0:T(8,128)(2,1)S(1)}, bf16[128,128]{1,0:T(8,128)(2,1)S(1)}, u32[]{:S(2)}, u32[]{:S(2)}) collective-permute-start(bf16[128,128]{1,0:T(8,128)(2,1)S(1)} %get-tuple-element.47), channel_id=1, source_target_pairs={{0,4},{1,5},{2,6},{3,7},{4,0},{5,1},{6,2},{7,3},{8,12},{9,13},{10,... | collective-permute-start | bytes 98312 | tf_op jit(solution)/shard_map/ppermute | solution.py:448
  38.8 1.8 %collective-permute-start.19 = (bf16[128,128]{1,0:T(8,128)(2,1)S(1)}, bf16[128,128]{1,0:T(8,128)(2,1)S(1)}, u32[]{:S(2)}, u32[]{:S(2)}) collective-permute-start(bf16[128,128]{1,0:T(8,128)(2,1)S(1)} %get-tuple-element.48), channel_id=1, source_target_pairs={{0,6},{1,7},{2,4},{3,5},{4,2},{5,3},{6,0},{7,1},{8,14},{9,15},{10,... | collective-permute-start | bytes 98312 | tf_op jit(solution)/shard_map/ppermute | solution.py:448
  40.6 4.4 %shard_map.122 = (bf16[2,16,128,128]{3,2,1,0:T(8,128)(2,1)}, f32[4,128,128]{2,1,0:T(8,128)S(1)}, f32[8,128]{1,0:T(8,128)S(1)}, f32[80,128]{1,0:T(8,128)S(1)}) custom-call(s32[64]{0:T(128)S(1)} %reshape.9.links_ref, s32[16]{0:T(128)S(1)} %copy-done.3, s32[16]{0:T(128)S(1)} %copy-done.9, bf16[208,128]{1,0:T(8,128)(2,1)S(1)} %get-tuple-element.41.refs_0_, ...), custom_call_target="tpu_custom_call" | custom-call | flops 1207959552 | bytes 2097152 | tf_op jit(solution)/shard_map/pallas_call | solution.py:487
  45.0 0.0 collective-permute-done.17.refs_1_
  45.1 0.0 collective-permute-done.18.refs_2_
  45.1 0.0 collective-permute-done.19.refs_3_
  45.1 1.5 %shard_map.123 = bf16[2,16,128,128]{3,2,1,0:T(8,128)(2,1)} custom-call(s32[64]{0:T(128)S(1)} %reshape.9.links_ref, s32[16]{0:T(128)S(1)} %copy-done.3, bf16[128,128]{1,0:T(8,128)(2,1)S(1)} %get-tuple-element.45.refs_0_, bf16[128,128]{1,0:T(8,128)(2,1)S(1)} %collective-permute-done.17.refs_1_, ...), custom_call_target="tpu_custom_call", output_to_operand_aliasing={{}: (12, {})} | custom-call | tf_op jit(solution)/shard_map/pallas_call | solution.py:500
  (13 shorter events, 0.0 us)
Async XLA Ops:
  0.0 1.2 %copy-start = (bf16[2,16,128,128]{3,2,1,0:T(8,128)(2,1)S(1)}, bf16[2,16,128,128]{3,2,1,0:T(8,128)(2,1)}, u32[]{:S(2)}) copy-start(bf16[2,16,128,128]{3,2,1,0:T(8,128)(2,1)} %refs_14_.1) | copy-start | bytes 3145732
  1.2 0.7 %copy-start.2 = (s32[16]{0:T(128)S(1)}, s32[16]{0:T(128)}, u32[]{:S(2)}) copy-start(s32[16]{0:T(128)} %rows_ref.7) | copy-start | bytes 196
  1.9 13.8 %copy-start.12 = (s32[16,4]{0,1:T(4,128)S(1)}, s32[16,4]{0,1:T(4,128)}, u32[]{:S(2)}) copy-start(s32[16,4]{0,1:T(4,128)} %param.13) | copy-start | bytes 772
  1.9 19.2 %copy-start.1 = (bf16[2,16,128,128]{3,2,1,0:T(8,128)(2,1)S(1)}, bf16[2,16,128,128]{3,2,1,0:T(8,128)(2,1)}, u32[]{:S(2)}) copy-start(bf16[2,16,128,128]{3,2,1,0:T(8,128)(2,1)} %refs_14_.1) | copy-start | bytes 3145732
  1.9 19.2 %copy-start.3 = (s32[16]{0:T(128)S(1)}, s32[16]{0:T(128)}, u32[]{:S(2)}) copy-start(s32[16]{0:T(128)} %rows_ref.7) | copy-start | bytes 196
  1.9 19.2 %copy-start.4 = (f32[128]{0:T(128)S(1)}, f32[128]{0:T(128)}, u32[]{:S(2)}) copy-start(f32[128]{0:T(128)} %param.16) | copy-start | bytes 1540
  1.9 19.2 %copy-start.5 = (f32[128]{0:T(128)S(1)}, f32[128]{0:T(128)}, u32[]{:S(2)}) copy-start(f32[128]{0:T(128)} %param.17) | copy-start | bytes 1540
  1.9 19.2 %copy-start.8 = (f32[128]{0:T(128)S(1)}, f32[128]{0:T(128)}, u32[]{:S(2)}) copy-start(f32[128]{0:T(128)} %param.19) | copy-start | bytes 1540
  1.9 19.2 %copy-start.9 = (s32[16]{0:T(128)S(1)}, s32[16]{0:T(128)}, u32[]{:S(2)}) copy-start(s32[16]{0:T(128)} %image_ref.3) | copy-start | bytes 196
  2.9 5.7 %collective-permute-start = (bf16[208,128]{1,0:T(8,128)(2,1)S(1)}, bf16[208,128]{1,0:T(8,128)(2,1)S(1)}, u32[]{:S(2)}, u32[]{:S(2)}) collective-permute-start(bf16[208,128]{1,0:T(8,128)(2,1)S(1)} %get-tuple-element.31), channel_id=1, source_target_pairs={{0,2},{1,3},{2,0},{3,1},{4,6},{5,7},{6,4},{7,5},{8,10},{9,11},{10,... | collective-permute-start | bytes 159752 | tf_op jit(solution)/shard_map/ppermute | solution.py:448
  6.1 6.1 %collective-permute-start.1 = (bf16[208,128]{1,0:T(8,128)(2,1)S(1)}, bf16[208,128]{1,0:T(8,128)(2,1)S(1)}, u32[]{:S(2)}, u32[]{:S(2)}) collective-permute-start(bf16[208,128]{1,0:T(8,128)(2,1)S(1)} %get-tuple-element.32), channel_id=1, source_target_pairs={{0,4},{1,5},{2,6},{3,7},{4,0},{5,1},{6,2},{7,3},{8,12},{9,13},{10,... | collective-permute-start | bytes 159752 | tf_op jit(solution)/shard_map/ppermute | solution.py:448
  8.6 5.9 %collective-permute-start.2 = (bf16[208,128]{1,0:T(8,128)(2,1)S(1)}, bf16[208,128]{1,0:T(8,128)(2,1)S(1)}, u32[]{:S(2)}, u32[]{:S(2)}) collective-permute-start(bf16[208,128]{1,0:T(8,128)(2,1)S(1)} %get-tuple-element.33), channel_id=1, source_target_pairs={{0,6},{1,7},{2,4},{3,5},{4,2},{5,3},{6,0},{7,1},{8,14},{9,15},{10,... | collective-permute-start | bytes 159752 | tf_op jit(solution)/shard_map/ppermute | solution.py:448
  8.7 7.2 %collective-permute-start.3 = (bf16[208,128]{1,0:T(8,128)(2,1)S(1)}, bf16[208,128]{1,0:T(8,128)(2,1)S(1)}, u32[]{:S(2)}, u32[]{:S(2)}) collective-permute-start(bf16[208,128]{1,0:T(8,128)(2,1)S(1)} %get-tuple-element.30.refs_0_), channel_id=1, source_target_pairs={{0,1},{1,0},{2,3},{3,2},{4,5},{5,4},{6,7},{7,6},{8,9},{9,8},{10,11... | collective-permute-start | bytes 159752 | tf_op jit(solution)/shard_map/ppermute | solution.py:448
  8.7 7.2 %collective-permute-start.4 = (bf16[208,128]{1,0:T(8,128)(2,1)S(1)}, bf16[208,128]{1,0:T(8,128)(2,1)S(1)}, u32[]{:S(2)}, u32[]{:S(2)}) collective-permute-start(bf16[208,128]{1,0:T(8,128)(2,1)S(1)} %collective-permute-done.refs_1_), channel_id=1, source_target_pairs={{0,1},{1,0},{2,3},{3,2},{4,5},{5,4},{6,7},{7,6},{8,9},{9,8},{10,11... | collective-permute-start | bytes 159752 | tf_op jit(solution)/shard_map/ppermute | solution.py:448
  12.1 3.8 %collective-permute-start.5 = (bf16[208,128]{1,0:T(8,128)(2,1)S(1)}, bf16[208,128]{1,0:T(8,128)(2,1)S(1)}, u32[]{:S(2)}, u32[]{:S(2)}) collective-permute-start(bf16[208,128]{1,0:T(8,128)(2,1)S(1)} %collective-permute-done.1.refs_2_), channel_id=1, source_target_pairs={{0,1},{1,0},{2,3},{3,2},{4,5},{5,4},{6,7},{7,6},{8,9},{9,8},{10,11... | collective-permute-start | bytes 159752 | tf_op jit(solution)/shard_map/ppermute | solution.py:448
  14.6 1.3 %collective-permute-start.6 = (bf16[208,128]{1,0:T(8,128)(2,1)S(1)}, bf16[208,128]{1,0:T(8,128)(2,1)S(1)}, u32[]{:S(2)}, u32[]{:S(2)}) collective-permute-start(bf16[208,128]{1,0:T(8,128)(2,1)S(1)} %collective-permute-done.2.refs_3_), channel_id=1, source_target_pairs={{0,1},{1,0},{2,3},{3,2},{4,5},{5,4},{6,7},{7,6},{8,9},{9,8},{10,11... | collective-permute-start | bytes 159752 | tf_op jit(solution)/shard_map/ppermute | solution.py:448
  16.6 8.3 %collective-permute-start.7 = (bf16[128,128]{1,0:T(8,128)(2,1)S(1)}, bf16[128,128]{1,0:T(8,128)(2,1)S(1)}, u32[]{:S(2)}, u32[]{:S(2)}) collective-permute-start(bf16[128,128]{1,0:T(8,128)(2,1)S(1)} %get-tuple-element.35), channel_id=1, source_target_pairs={{0,2},{1,3},{2,0},{3,1},{4,6},{5,7},{6,4},{7,5},{8,10},{9,11},{10,... | collective-permute-start | bytes 98312 | tf_op jit(solution)/shard_map/ppermute | solution.py:448
  16.7 8.2 %collective-permute-start.8 = (bf16[128,128]{1,0:T(8,128)(2,1)S(1)}, bf16[128,128]{1,0:T(8,128)(2,1)S(1)}, u32[]{:S(2)}, u32[]{:S(2)}) collective-permute-start(bf16[128,128]{1,0:T(8,128)(2,1)S(1)} %get-tuple-element.36), channel_id=1, source_target_pairs={{0,4},{1,5},{2,6},{3,7},{4,0},{5,1},{6,2},{7,3},{8,12},{9,13},{10,... | collective-permute-start | bytes 98312 | tf_op jit(solution)/shard_map/ppermute | solution.py:448
  18.7 6.2 %collective-permute-start.9 = (bf16[128,128]{1,0:T(8,128)(2,1)S(1)}, bf16[128,128]{1,0:T(8,128)(2,1)S(1)}, u32[]{:S(2)}, u32[]{:S(2)}) collective-permute-start(bf16[128,128]{1,0:T(8,128)(2,1)S(1)} %get-tuple-element.37), channel_id=1, source_target_pairs={{0,6},{1,7},{2,4},{3,5},{4,2},{5,3},{6,0},{7,1},{8,14},{9,15},{10,... | collective-permute-start | bytes 98312 | tf_op jit(solution)/shard_map/ppermute | solution.py:448
  24.9 9.4 %copy-start.11 = (bf16[3,3,128,128]{3,2,1,0:T(8,128)(2,1)S(1)}, bf16[3,3,128,128]{3,2,1,0:T(8,128)(2,1)}, u32[]{:S(2)}) copy-start(bf16[3,3,128,128]{3,2,1,0:T(8,128)(2,1)} %param.22) | copy-start | bytes 884740
  25.8 14.8 %copy-start.6 = (f32[128]{0:T(128)S(1)}, f32[128]{0:T(128)}, u32[]{:S(2)}) copy-start(f32[128]{0:T(128)} %param.20) | copy-start | bytes 1540
  25.9 14.8 %copy-start.7 = (f32[128]{0:T(128)S(1)}, f32[128]{0:T(128)}, u32[]{:S(2)}) copy-start(f32[128]{0:T(128)} %param.21) | copy-start | bytes 1540
  25.9 14.7 %copy-start.10 = (f32[128]{0:T(128)S(1)}, f32[128]{0:T(128)}, u32[]{:S(2)}) copy-start(f32[128]{0:T(128)} %param.23) | copy-start | bytes 1540
  25.9 4.5 %collective-permute-start.10 = (bf16[208,128]{1,0:T(8,128)(2,1)S(1)}, bf16[208,128]{1,0:T(8,128)(2,1)S(1)}, u32[]{:S(2)}, u32[]{:S(2)}) collective-permute-start(bf16[208,128]{1,0:T(8,128)(2,1)S(1)} %get-tuple-element.42), channel_id=1, source_target_pairs={{0,2},{1,3},{2,0},{3,1},{4,6},{5,7},{6,4},{7,5},{8,10},{9,11},{10,... | collective-permute-start | bytes 159752 | tf_op jit(solution)/shard_map/ppermute | solution.py:448
  26.0 6.6 %collective-permute-start.11 = (bf16[208,128]{1,0:T(8,128)(2,1)S(1)}, bf16[208,128]{1,0:T(8,128)(2,1)S(1)}, u32[]{:S(2)}, u32[]{:S(2)}) collective-permute-start(bf16[208,128]{1,0:T(8,128)(2,1)S(1)} %get-tuple-element.43), channel_id=1, source_target_pairs={{0,4},{1,5},{2,6},{3,7},{4,0},{5,1},{6,2},{7,3},{8,12},{9,13},{10,... | collective-permute-start | bytes 159752 | tf_op jit(solution)/shard_map/ppermute | solution.py:448
  28.3 5.9 %collective-permute-start.12 = (bf16[208,128]{1,0:T(8,128)(2,1)S(1)}, bf16[208,128]{1,0:T(8,128)(2,1)S(1)}, u32[]{:S(2)}, u32[]{:S(2)}) collective-permute-start(bf16[208,128]{1,0:T(8,128)(2,1)S(1)} %get-tuple-element.44), channel_id=1, source_target_pairs={{0,6},{1,7},{2,4},{3,5},{4,2},{5,3},{6,0},{7,1},{8,14},{9,15},{10,... | collective-permute-start | bytes 159752 | tf_op jit(solution)/shard_map/ppermute | solution.py:448
  30.3 4.0 %collective-permute-start.13 = (bf16[208,128]{1,0:T(8,128)(2,1)S(1)}, bf16[208,128]{1,0:T(8,128)(2,1)S(1)}, u32[]{:S(2)}, u32[]{:S(2)}) collective-permute-start(bf16[208,128]{1,0:T(8,128)(2,1)S(1)} %get-tuple-element.41.refs_0_), channel_id=1, source_target_pairs={{0,1},{1,0},{2,3},{3,2},{4,5},{5,4},{6,7},{7,6},{8,9},{9,8},{10,11... | collective-permute-start | bytes 159752 | tf_op jit(solution)/shard_map/ppermute | solution.py:448
  30.3 4.0 %collective-permute-start.14 = (bf16[208,128]{1,0:T(8,128)(2,1)S(1)}, bf16[208,128]{1,0:T(8,128)(2,1)S(1)}, u32[]{:S(2)}, u32[]{:S(2)}) collective-permute-start(bf16[208,128]{1,0:T(8,128)(2,1)S(1)} %collective-permute-done.10.refs_1_), channel_id=1, source_target_pairs={{0,1},{1,0},{2,3},{3,2},{4,5},{5,4},{6,7},{7,6},{8,9},{9,8},{10,11... | collective-permute-start | bytes 159752 | tf_op jit(solution)/shard_map/ppermute | solution.py:448
  32.6 1.8 %collective-permute-start.15 = (bf16[208,128]{1,0:T(8,128)(2,1)S(1)}, bf16[208,128]{1,0:T(8,128)(2,1)S(1)}, u32[]{:S(2)}, u32[]{:S(2)}) collective-permute-start(bf16[208,128]{1,0:T(8,128)(2,1)S(1)} %collective-permute-done.11.refs_2_), channel_id=1, source_target_pairs={{0,1},{1,0},{2,3},{3,2},{4,5},{5,4},{6,7},{7,6},{8,9},{9,8},{10,11... | collective-permute-start | bytes 159752 | tf_op jit(solution)/shard_map/ppermute | solution.py:448
  34.3 1.2 %collective-permute-start.16 = (bf16[208,128]{1,0:T(8,128)(2,1)S(1)}, bf16[208,128]{1,0:T(8,128)(2,1)S(1)}, u32[]{:S(2)}, u32[]{:S(2)}) collective-permute-start(bf16[208,128]{1,0:T(8,128)(2,1)S(1)} %collective-permute-done.12.refs_3_), channel_id=1, source_target_pairs={{0,1},{1,0},{2,3},{3,2},{4,5},{5,4},{6,7},{7,6},{8,9},{9,8},{10,11... | collective-permute-start | bytes 159752 | tf_op jit(solution)/shard_map/ppermute | solution.py:448
  36.2 8.9 %collective-permute-start.17 = (bf16[128,128]{1,0:T(8,128)(2,1)S(1)}, bf16[128,128]{1,0:T(8,128)(2,1)S(1)}, u32[]{:S(2)}, u32[]{:S(2)}) collective-permute-start(bf16[128,128]{1,0:T(8,128)(2,1)S(1)} %get-tuple-element.46), channel_id=1, source_target_pairs={{0,2},{1,3},{2,0},{3,1},{4,6},{5,7},{6,4},{7,5},{8,10},{9,11},{10,... | collective-permute-start | bytes 98312 | tf_op jit(solution)/shard_map/ppermute | solution.py:448
  36.2 8.8 %collective-permute-start.18 = (bf16[128,128]{1,0:T(8,128)(2,1)S(1)}, bf16[128,128]{1,0:T(8,128)(2,1)S(1)}, u32[]{:S(2)}, u32[]{:S(2)}) collective-permute-start(bf16[128,128]{1,0:T(8,128)(2,1)S(1)} %get-tuple-element.47), channel_id=1, source_target_pairs={{0,4},{1,5},{2,6},{3,7},{4,0},{5,1},{6,2},{7,3},{8,12},{9,13},{10,... | collective-permute-start | bytes 98312 | tf_op jit(solution)/shard_map/ppermute | solution.py:448
  38.8 6.3 %collective-permute-start.19 = (bf16[128,128]{1,0:T(8,128)(2,1)S(1)}, bf16[128,128]{1,0:T(8,128)(2,1)S(1)}, u32[]{:S(2)}, u32[]{:S(2)}) collective-permute-start(bf16[128,128]{1,0:T(8,128)(2,1)S(1)} %get-tuple-element.48), channel_id=1, source_target_pairs={{0,6},{1,7},{2,4},{3,5},{4,2},{5,3},{6,0},{7,1},{8,14},{9,15},{10,... | collective-permute-start | bytes 98312 | tf_op jit(solution)/shard_map/ppermute | solution.py:448
where the time goes:
time: 46.8 us; the launch traced here: 46.6 us
  starting transfers between devices  20.1 us (43%)
  Pallas kernels  13 us (28%)
  waiting for transfers between devices  9.97 us (21%)
  local copies, waits for them, and re-layouts  2.1 us (4%)
  other arithmetic  1.19 us (3%)
    ppermute x20, starting transfers between devices, swap(): return lax.ppermute(array, AXIS, [(i, i ^ distance) for i in range(size)])  20.1 us
    ppermute x20, waiting for transfers between devices, swap(): return lax.ppermute(array, AXIS, [(i, i ^ distance) for i in range(size)])  9.97 us
    pallas_call x2, Pallas kernels, stage(): pl.pallas_call(functools.partial(middle_kernel, plan, last), out_shape=[t...  8.24 us
    unnamed x27, local copies, waits for them, and re-layouts  2.01 us
    pallas_call x1, Pallas kernels, stage(): pl.pallas_call(functools.partial(ends_kernel, plan, last), out_shape=tile...  1.5 us
    pallas_call x2, Pallas kernels, stage(): pl.pallas_call(functools.partial(route_kernel, plan), out_shape=[shape((2...  1.3 us
    concatenate x2, other arithmetic, paired_weights(): both = jnp.concatenate([upper, lower], axis=-1)  1.19 us
    pallas_call x1, Pallas kernels, shards(): pl.pallas_call(functools.partial(edges_kernel, plan), out_shape=buf_shape...  1.01 us
  transfers between devices with their start and end apart: 20, of which 5 were waited for; matrix products, arithmetic and copies ran while one was open for 3% of the time, Pallas kernels for 18%

commit v1 on v0

--- a/solution.py
+++ b/solution.py
@@ -95,6 +95,13 @@
     return pixels.astype(f32), total, jnp.sum(spread, axis=0, keepdims=True)
 
 
+def merge_sums(one, two):
+    pixels, other = jnp.maximum(one[0], 1.0), jnp.maximum(two[0], 1.0)
+    apart = one[1] / pixels - two[1] / other
+    weight = jnp.where(jnp.minimum(one[0], two[0]) > 0, pixels * other / (pixels + other), 0.0)
+    return one[0] + two[0], one[1] + two[1], one[2] + two[2] + apart * apart * weight
+
+
 def pack_stats(plan, sums, spreads):
     parts = list(split_three(jnp.concatenate(sums + spreads, axis=0)))
     padding = plan.stat_rows - 6 * plan.count
@@ -123,14 +130,19 @@
     return [ref[first + tile] for tile in range(plan.count)]
 
 
-def edges_kernel(plan, rows_hbm, x_hbm, *refs):
-    buf_refs, (rows_ref, x_ref, sems) = refs[: plan.chunks], refs[plan.chunks :]
-    counts = pltpu.make_async_copy(rows_hbm, rows_ref, sems.at[plan.count])
-    counts.start()
+def edges_kernel(plan, links_hbm, rows_hbm, image_hbm, x_hbm, links_ref, rows_ref, image_ref, *refs):
+    buf_refs, (x_ref, sems) = refs[: plan.chunks], refs[plan.chunks :]
+    tables = [
+        pltpu.make_async_copy(source, target, sems.at[plan.count + place])
+        for place, (source, target) in enumerate(
+            ((rows_hbm, rows_ref), (links_hbm, links_ref), (image_hbm, image_ref))
+        )
+    ]
     copies = [pltpu.make_async_copy(x_hbm.at[tile], x_ref.at[tile], sems.at[tile]) for tile in range(plan.count)]
-    for copy in copies:
+    for copy in tables[:1] + copies + tables[1:]:
         copy.start()
-    counts.wait()
+    for copy in tables:
+        copy.wait()
     own_rows = own_values(plan, rows_ref)
     sums, spreads, columns = [], [], []
     for tile in range(plan.count):
@@ -161,14 +173,19 @@
 
 
 class Held:
-    def __init__(self, plan, bufs, held):
+    def __init__(self, plan, bufs, held, part):
         self.plan = plan
+        self.row_base, self.col_base = plan.row_base, plan.col_base
+        self.held = bufs[0]
         if plan.chunks > 1:
+            self.held = held
+            self.row_base, self.col_base = 0, plan.stat_rows
             for slot in range(plan.slots):
-                held[slot] = bufs[slot][...]
-            self.held = held
-        else:
-            self.held = bufs[0]
+                if part == "rows":
+                    held[slot] = bufs[slot][plan.row_base : plan.col_base, :]
+                else:
+                    held[slot, 0 : plan.stat_rows, :] = bufs[slot][0 : plan.stat_rows, :]
+                    held[slot, plan.stat_rows :, :] = bufs[slot][plan.col_base :, :]
 
     def locate(self, tile):
         tile = jnp.maximum(tile, 0)
@@ -176,13 +193,18 @@
 
     def edge_row(self, tile, edge):
         slot, local = self.locate(tile)
-        at = pl.multiple_of(self.plan.row_base + (2 * local + edge) * self.plan.width, 16)
+        at = pl.multiple_of(self.row_base + (2 * local + edge) * self.plan.width, 16)
         return self.held[slot, pl.ds(at, self.plan.width), :]
 
     def edge_col(self, tile, edge):
         slot, local = self.locate(tile)
-        at = pl.multiple_of(self.plan.col_base + (2 * local + edge) * self.plan.rows, 16)
+        at = pl.multiple_of(self.col_base + (2 * local + edge) * self.plan.rows, 16)
         return self.held[slot, pl.ds(at, self.plan.rows), :]
+
+
+def held_scratch(plan, part):
+    rows = plan.col_base - plan.row_base if part == "rows" else plan.buf_rows - plan.col_base + plan.stat_rows
+    return pltpu.VMEM((plan.slots, rows, plan.channels) if plan.chunks > 1 else (1, 16, plan.channels), bf16)
 
 
 def buffer_inputs(plan, refs):
@@ -192,13 +214,13 @@
 
 def route_kernel(plan, links_ref, *refs):
     bufs, refs = buffer_inputs(plan, refs)
-    send_refs, held = refs[:-1], Held(plan, bufs, refs[-1])
+    send_refs, held = refs[:-1], Held(plan, bufs, refs[-1], "rows")
     for k in range(plan.chunks):
         first = plan.target(k) * plan.count
         for tile in range(plan.count):
             for edge in range(2):
                 at = (2 * tile + edge) * plan.width
-                wanted = links_ref[(first + tile) * 4 + edge]
+                wanted = links_ref[edge, first + tile]
                 send_refs[k][at : at + plan.width, :] = held.edge_row(wanted, 1 - edge)
 
 
@@ -272,7 +294,7 @@
     out_ref, partial_ref, norm_ref, side_ref, held_ref, wide = refs[:6]
     refs = refs[6:]
     count, rows, cols, channels = plan.count, plan.rows, plan.cols, plan.channels
-    held = Held(plan, bufs, held_ref)
+    held = Held(plan, bufs, held_ref, "rest")
     means, inverses = image_norms(plan, rows_ref, image_ref, held.held)
     first = lax.axis_index(AXIS) * count
     own_rows = own_values(plan, rows_ref)
@@ -281,13 +303,13 @@
     copies = []
     for tile in range(count):
         valid = own_rows[tile]
-        link = [links_ref[(first + tile) * 4 + column] for column in range(4)]
+        link = [links_ref[column, first + tile] for column in range(4)]
         activate = halves(means[tile], inverses[tile], gain_ref, shift_ref)
         left = jnp.where(link[2] >= 0, activate(held.edge_col(link[2], 1)), 0.0)
         right = jnp.where(link[3] >= 0, activate(held.edge_col(link[3], 0)), 0.0)
         corners = []
         for place in range(4):
-            beside = links_ref[jnp.maximum(link[place // 2], 0) * 4 + 2 + place % 2]
+            beside = links_ref[2 + place % 2, jnp.maximum(link[place // 2], 0)]
             beside = jnp.where(link[place // 2] >= 0, beside, -1)
             row = 0 if place // 2 else rows - 1
             corner = activate(held.edge_col(beside, 1 - place % 2))[row : row + 1]
@@ -312,32 +334,40 @@
                 wide[tile, (row + 1) // 2, :, at : at + channels] = values
 
         pairs = rows // 2
-        upper = wide[tile, 0:pairs].reshape(pairs * cols, 2 * depth)
-        lower = wide[tile, 1 : pairs + 1].reshape(pairs * cols, 2 * depth)
-        summed = jnp.dot(upper, weight_ref[0 : 2 * depth, :], preferred_element_type=f32)
-        summed = summed + jnp.dot(lower, weight_ref[2 * depth : 4 * depth, :], preferred_element_type=f32)
-        for row in range(rows):
-            at, lane = (row // 2) * cols, (row % 2) * channels
-            part = summed[at : at + cols, lane : lane + channels] + offset
+        step = 2 if pairs % 2 == 0 else 1
+        gathered = None
+        for pair in range(0, pairs, step):
+            upper = wide[tile, pair : pair + step].reshape(step * cols, 2 * depth)
+            lower = wide[tile, pair + 1 : pair + step + 1].reshape(step * cols, 2 * depth)
+            window = jnp.concatenate([upper, lower], axis=1)
+            summed = jnp.dot(window, weight_ref[...], preferred_element_type=f32)
+            inner = {}
+            for row in range(2 * pair, 2 * (pair + step)):
+                at, lane = (row // 2 - pair) * cols, (row % 2) * channels
+                part = summed[at : at + cols, lane : lane + channels] + offset
+                if last:
+                    part = part + residual_ref[tile, row].astype(f32)
+                if row in (0, rows - 1):
+                    partial_ref[2 * tile + (row > 0)] = part
+                    continue
+                part = jnp.where(row < valid, part, 0.0).astype(bf16)
+                if last:
+                    refs[0][tile, row] = part
+                else:
+                    out_ref[tile, row] = part
+                inner[row] = part.astype(f32)
             if last:
-                part = part + residual_ref[tile, row].astype(f32)
-            if row in (0, rows - 1):
-                partial_ref[2 * tile + (row > 0)] = part
-            elif last:
-                refs[0][tile, row] = jnp.where(row < valid, part, 0.0).astype(bf16)
+                band = pl.ds(min(inner), len(inner))
+                sem = refs[1].at[tile * pairs + pair]
+                copy = pltpu.make_async_copy(refs[0].at[tile, band], out_ref.at[tile, band], sem)
+                copy.start()
+                copies.append(copy)
             else:
-                out_ref[tile, row] = jnp.where(row < valid, part, 0.0).astype(bf16)
-        if last:
-            window = pl.ds(1, rows - 2)
-            copy = pltpu.make_async_copy(refs[0].at[tile, window], out_ref.at[tile, window], refs[1].at[tile])
-            copy.start()
-            copies.append(copy)
-        else:
-            _, total, spread = column_sums(
-                lambda row: out_ref[tile, row].astype(f32), range(1, rows - 1), valid
-            )
-            norm_ref[(2 * count + tile) : (2 * count + tile) + 1, :] = total
-            norm_ref[(3 * count + tile) : (3 * count + tile) + 1, :] = spread
+                found = column_sums(lambda row: inner[row], sorted(inner), valid)
+                gathered = found if gathered is None else merge_sums(gathered, found)
+        if not last:
+            norm_ref[(2 * count + tile) : (2 * count + tile) + 1, :] = gathered[1]
+            norm_ref[(3 * count + tile) : (3 * count + tile) + 1, :] = gathered[2]
             for side, column in enumerate((0, cols - 1)):
                 picked = [out_ref[tile, row, column : column + 1, :].astype(f32) for row in range(1, rows - 1)]
                 at = 8 * count + (2 * tile + side) * rows
@@ -374,7 +404,7 @@
         values = []
         for edge, row in enumerate((0, rows - 1)):
             place = 2 * tile + edge
-            present = links_ref[(first + tile) * 4 + edge] >= 0
+            present = links_ref[edge, first + tile] >= 0
             act = jnp.where(present, activate(halo[place]), 0.0)
             at = 8 * tile + 2 * edge
             wide = jnp.concatenate(taps(act, side_ref[at : at + 1, :], side_ref[at + 1 : at + 2, :]), axis=1)
@@ -388,14 +418,15 @@
                 copies[-1].start()
         if last:
             continue
-        amount, total, spread = column_sums(lambda row: values[row > 0], (0, rows - 1), valid)
-        inner_total = norm_ref[2 * count + tile : 2 * count + tile + 1, :]
-        inner_spread = norm_ref[3 * count + tile : 3 * count + tile + 1, :]
-        inner = jnp.maximum((jnp.minimum(valid, rows - 1) - 1) * cols, 1).astype(f32)
-        amount = jnp.maximum(amount, 1.0)
-        apart = inner_total / inner - total / amount
-        sums.append(inner_total + total)
-        spreads.append(inner_spread + spread + apart * apart * (inner * amount / (inner + amount)))
+        found = column_sums(lambda row: values[row > 0], (0, rows - 1), valid)
+        inner = (
+            jnp.maximum((jnp.minimum(valid, rows - 1) - 1) * cols, 0).astype(f32),
+            norm_ref[2 * count + tile : 2 * count + tile + 1, :],
+            norm_ref[3 * count + tile : 3 * count + tile + 1, :],
+        )
+        _, total, spread = merge_sums(inner, found)
+        sums.append(total)
+        spreads.append(spread)
         line = lax.broadcasted_iota(jnp.int32, (rows, channels), 0)
         for side, column in enumerate((0, cols - 1)):
             at = 8 * count + (2 * tile + side) * rows
@@ -438,8 +469,6 @@
 ):
     count, rows, cols, channels = feature_tiles.shape
     plan = Plan(size, count, rows, cols, channels)
-    links = neighbours.reshape(-1)
-    scalars = (links, valid_rows, tile_image)
     buf_shape = [jax.ShapeDtypeStruct((plan.buf_rows, channels), bf16)] * plan.chunks
     limit = 24 * 1024 * 1024
     params = pltpu.CompilerParams(vmem_limit_bytes=limit)
@@ -462,7 +491,6 @@
     def shape(dims, dtype=f32):
         return jax.ShapeDtypeStruct(dims, dtype)
 
-    held = pltpu.VMEM((plan.slots, plan.buf_rows, channels) if plan.chunks > 1 else (1, 16, channels), bf16)
     partial_shape = shape((2 * count, cols, channels))
     norm_shape = shape((round_up(4 * count, 8), channels))
     side_shape = shape((8 * count + 2 * count * rows, channels))
@@ -476,9 +504,9 @@
             out_shape=[shape((2 * count * plan.width, channels), bf16)] * plan.chunks,
             in_specs=[SMEM] + [VMEM] * len(arrays),
             out_specs=[VMEM] * plan.chunks,
-            scratch_shapes=[held],
+            scratch_shapes=[held_scratch(plan, "rows")],
             compiler_params=params,
-        )(links, *arrays)
+        )(scalars[0], *arrays)
         halo = spread(send)
         weights = paired_weights(kernel)
         gain, shift, offset = gain[None], shift[None], offset[None]
@@ -489,8 +517,8 @@
             out_shape=[tiles_shape, partial_shape, norm_shape, side_shape],
             in_specs=[SMEM] * 3 + [VMEM] * len(operands),
             out_specs=[HBM if last else VMEM] + [VMEM] * 3,
-            scratch_shapes=[held, pltpu.VMEM((count, rows // 2 + 1, cols, 6 * channels), bf16)]
-            + ([pltpu.VMEM(feature_tiles.shape, bf16), pltpu.SemaphoreType.DMA((count,))] if last else []),
+            scratch_shapes=[held_scratch(plan, "rest"), pltpu.VMEM((count, rows // 2 + 1, cols, 6 * channels), bf16)]
+            + ([pltpu.VMEM(feature_tiles.shape, bf16), pltpu.SemaphoreType.DMA((count * rows // 2,))] if last else []),
             compiler_params=params,
             cost_estimate=pl.CostEstimate(flops=flops, bytes_accessed=4 * feature_tiles.size, transcendentals=0),
         )(*scalars, *operands)
@@ -505,7 +533,7 @@
                 input_output_aliases={2 + len(operands): 0},
                 scratch_shapes=scratch + scratch + [pltpu.SemaphoreType.DMA((2 * count,))],
                 compiler_params=params,
-            )(links, valid_rows, *operands, tiles)
+            )(*scalars[:2], *operands, tiles)
         ends, *bufs = pl.pallas_call(
             functools.partial(ends_kernel, plan, last),
             out_shape=[ends_shape] + buf_shape,
@@ -513,22 +541,21 @@
             out_specs=[VMEM] * (1 + plan.chunks),
             scratch_shapes=scratch,
             compiler_params=params,
-        )(links, valid_rows, *operands)
+        )(*scalars[:2], *operands)
         return tiles, ends, bufs
 
-    bufs = pl.pallas_call(
+    tables = (neighbours.T, valid_rows, tile_image)
+    inputs = [pltpu.with_memory_space_constraint(array, pltpu.HBM) for array in (*tables, feature_tiles)]
+    found = pl.pallas_call(
         functools.partial(edges_kernel, plan),
-        out_shape=buf_shape,
-        in_specs=[HBM, HBM],
-        out_specs=[VMEM] * plan.chunks,
-        scratch_shapes=[
-            pltpu.SMEM(valid_rows.shape, jnp.int32),
-            pltpu.VMEM(feature_tiles.shape, bf16),
-            pltpu.SemaphoreType.DMA((count + 1,)),
-        ],
+        out_shape=[pltpu.SMEM(table.shape, jnp.int32) for table in tables] + buf_shape,
+        in_specs=[HBM] * 4,
+        out_specs=[SMEM] * 3 + [VMEM] * plan.chunks,
+        scratch_shapes=[pltpu.VMEM(feature_tiles.shape, bf16), pltpu.SemaphoreType.DMA((count + 3,))],
         compiler_params=params,
         name="edges",
-    )(valid_rows, feature_tiles)
+    )(*inputs)
+    scalars, bufs = found[:3], found[3:]
     hidden, ends, bufs = stage(False, feature_tiles, None, bufs, gain_one, shift_one, kernel_one, offset_one)
     return stage(True, hidden, ends, bufs, gain_two, shift_two, kernel_two, offset_two)
 

time: 46.8 us -> 42.2 us (0.902)
  Pallas kernels: 13 us -> 9.51 us
  local copies, waits for them, and re-layouts: 2.1 us -> 0.04 us
  waiting for transfers between devices: 9.97 us -> 12 us
  other arithmetic: 1.19 us -> 0.15 us
    ppermute x20, waiting for transfers between devices: 9.97 us -> 12 us  [swap(): return lax.ppermute(array, AXIS, [(i, i ^ distance) for i in range(size)])]
    unnamed x27 -> x18, local copies, waits for them, and re-layouts: 2.01 us -> 0.04 us
    pallas_call x2, Pallas kernels: 8.24 us -> 6.36 us  [stage(): pl.pallas_call(functools.partial(middle_kernel, plan, last), out_shape=[t...]
    pallas_call x2, Pallas kernels: 1.3 us -> 0.21 us  [stage(): pl.pallas_call(functools.partial(route_kernel, plan), out_shape=[shape((2...]
    concatenate x2, other arithmetic: 1.19 us -> 0.15 us  [paired_weights(): both = jnp.concatenate([upper, lower], axis=-1)]
    pallas_call x1, Pallas kernels: 1.01 us -> 1.62 us  [shards(): pl.pallas_call(functools.partial(edges_kernel, plan), out_shape=[pltpu.SM...]
    pallas_call x1, Pallas kernels: 0.91 us -> 0.37 us  [stage(): pl.pallas_call(functools.partial(ends_kernel, plan, last), out_shape=[end...]
    pallas_call x1, Pallas kernels: 1.5 us -> 0.95 us  [stage(): pl.pallas_call(functools.partial(ends_kernel, plan, last), out_shape=tile...]
  transfers between devices with their start and end apart: 20 -> 20, of which waited for: 5 -> 7; matrix products, arithmetic and copies ran while one was open for 3% -> 0% of each run, Pallas kernels for 18% -> 15%
where the time goes in v1:
time: 42.2 us; the launch traced here: 42 us
  starting transfers between devices  20.1 us (48%)
  waiting for transfers between devices  12 us (28%)
  Pallas kernels  9.51 us (23%)
    ppermute x20, starting transfers between devices, swap(): return lax.ppermute(array, AXIS, [(i, i ^ distance) for i in range(size)])  20.1 us
    ppermute x20, waiting for transfers between devices, swap(): return lax.ppermute(array, AXIS, [(i, i ^ distance) for i in range(size)])  12 us
    pallas_call x2, Pallas kernels, stage(): pl.pallas_call(functools.partial(middle_kernel, plan, last), out_shape=[t...  6.36 us
    pallas_call x1, Pallas kernels, shards(): pl.pallas_call(functools.partial(edges_kernel, plan), out_shape=[pltpu.SM...  1.62 us
    pallas_call x1, Pallas kernels, stage(): pl.pallas_call(functools.partial(ends_kernel, plan, last), out_shape=tile...  0.95 us
  transfers between devices with their start and end apart: 20, of which 7 were waited for; matrix products, arithmetic and copies ran while one was open for 0% of the time, Pallas kernels for 15%

profile of v1, /device:TPU:0, one launch (start us, length us, event | category | flops | bytes accessed | tf_op | source)
XLA Modules:
  0.0 42.0 jit_solution(9366778840713622516)
XLA Ops:
  0.0 0.0 copy-start.7
  0.0 0.0 copy-start
  0.0 0.0 copy-start.1
  0.0 1.6 %edges.1 = (s32[4,16]{1,0:T(4,128)S(4)}, s32[16]{0:T(128)S(4)}, s32[16]{0:T(128)S(4)}, bf16[208,128]{1,0:T(8,128)(2,1)S(1)}, bf16[208,128]{1,0:T(8,128)(2,1)S(1)...) custom-call(s32[4,16]{1,0:T(4,128)} %bitcast.23, s32[16]{0:T(128)} %rows_hbm.1, s32[16]{0:T(128)} %image_hbm.1, ...), custom_call_target="tpu_custom_call" | custom-call | tf_op jit(solution)/shard_map/edges/pallas_call | solution.py:549
  1.6 3.1 %collective-permute-start = (bf16[208,128]{1,0:T(8,128)(2,1)S(1)}, bf16[208,128]{1,0:T(8,128)(2,1)S(1)}, u32[]{:S(2)}, u32[]{:S(2)}) collective-permute-start(bf16[208,128]{1,0:T(8,128)(2,1)S(1)} %get-tuple-element.36), channel_id=1, source_target_pairs={{0,2},{1,3},{2,0},{3,1},{4,6},{5,7},{6,4},{7,5},{8,10},{9,11},{10,... | collective-permute-start | bytes 159752 | tf_op jit(solution)/shard_map/ppermute | solution.py:477
  4.8 2.6 %collective-permute-start.1 = (bf16[208,128]{1,0:T(8,128)(2,1)S(1)}, bf16[208,128]{1,0:T(8,128)(2,1)S(1)}, u32[]{:S(2)}, u32[]{:S(2)}) collective-permute-start(bf16[208,128]{1,0:T(8,128)(2,1)S(1)} %get-tuple-element.37), channel_id=1, source_target_pairs={{0,4},{1,5},{2,6},{3,7},{4,0},{5,1},{6,2},{7,3},{8,12},{9,13},{10,... | collective-permute-start | bytes 159752 | tf_op jit(solution)/shard_map/ppermute | solution.py:477
  7.4 0.0 collective-permute-start.2
  7.4 0.0 collective-permute-start.3
  7.4 0.0 collective-permute-done.refs_1_
  7.4 0.5 %collective-permute-start.4 = (bf16[208,128]{1,0:T(8,128)(2,1)S(1)}, bf16[208,128]{1,0:T(8,128)(2,1)S(1)}, u32[]{:S(2)}, u32[]{:S(2)}) collective-permute-start(bf16[208,128]{1,0:T(8,128)(2,1)S(1)} %collective-permute-done.refs_1_), channel_id=1, source_target_pairs={{0,1},{1,0},{2,3},{3,2},{4,5},{5,4},{6,7},{7,6},{8,9},{9,8},{10,11... | collective-permute-start | bytes 159752 | tf_op jit(solution)/shard_map/ppermute | solution.py:477
  7.9 2.9 %collective-permute-done.1.refs_2_ = bf16[208,128]{1,0:T(8,128)(2,1)S(1)} collective-permute-done((bf16[208,128]{1,0:T(8,128)(2,1)S(1)}, bf16[208,128]{1,0:T(8,128)(2,1)S(1)}, u32[]{:S(2)}, u32[]{:S(2)}) %collective-permute-start.1) | collective-permute-done | bytes 53280 | tf_op jit(solution)/shard_map/ppermute | solution.py:477
  10.8 0.0 collective-permute-start.5
  10.8 2.5 %collective-permute-done.2.refs_3_ = bf16[208,128]{1,0:T(8,128)(2,1)S(1)} collective-permute-done((bf16[208,128]{1,0:T(8,128)(2,1)S(1)}, bf16[208,128]{1,0:T(8,128)(2,1)S(1)}, u32[]{:S(2)}, u32[]{:S(2)}) %collective-permute-start.2) | collective-permute-done | bytes 53280 | tf_op jit(solution)/shard_map/ppermute | solution.py:477
  13.3 0.0 collective-permute-start.6
  13.3 0.0 copy-done.7
  13.3 0.1 fusion.4
  13.4 0.0 collective-permute-done.3.refs_4_
  13.4 0.0 collective-permute-done.4.refs_5_
  13.4 0.0 collective-permute-done.5.refs_6_
  13.4 1.1 %collective-permute-done.6.refs_7_ = bf16[208,128]{1,0:T(8,128)(2,1)S(1)} collective-permute-done((bf16[208,128]{1,0:T(8,128)(2,1)S(1)}, bf16[208,128]{1,0:T(8,128)(2,1)S(1)}, u32[]{:S(2)}, u32[]{:S(2)}) %collective-permute-start.6) | collective-permute-done | bytes 53280 | tf_op jit(solution)/shard_map/ppermute | solution.py:477
  14.5 0.1 shard_map.118
  14.7 0.1 collective-permute-start.7
  14.7 1.7 %collective-permute-start.8 = (bf16[128,128]{1,0:T(8,128)(2,1)S(1)}, bf16[128,128]{1,0:T(8,128)(2,1)S(1)}, u32[]{:S(2)}, u32[]{:S(2)}) collective-permute-start(bf16[128,128]{1,0:T(8,128)(2,1)S(1)} %get-tuple-element.41), channel_id=1, source_target_pairs={{0,4},{1,5},{2,6},{3,7},{4,0},{5,1},{6,2},{7,3},{8,12},{9,13},{10,... | collective-permute-start | bytes 98312 | tf_op jit(solution)/shard_map/ppermute | solution.py:477
  16.4 2.7 %collective-permute-start.9 = (bf16[128,128]{1,0:T(8,128)(2,1)S(1)}, bf16[128,128]{1,0:T(8,128)(2,1)S(1)}, u32[]{:S(2)}, u32[]{:S(2)}) collective-permute-start(bf16[128,128]{1,0:T(8,128)(2,1)S(1)} %get-tuple-element.42), channel_id=1, source_target_pairs={{0,6},{1,7},{2,4},{3,5},{4,2},{5,3},{6,0},{7,1},{8,14},{9,15},{10,... | collective-permute-start | bytes 98312 | tf_op jit(solution)/shard_map/ppermute | solution.py:477
  19.1 0.0 copy-done
  19.1 0.0 copy-done.1
  19.1 0.0 copy-done.2
  19.1 0.0 copy-done.5
  19.1 2.9 %shard_map.119 = (bf16[2,16,128,128]{3,2,1,0:T(8,128)(2,1)S(1)}, f32[4,128,128]{2,1,0:T(8,128)S(1)}, f32[8,128]{1,0:T(8,128)S(1)}, f32[80,128]{1,0:T(8,128)S(1)}) custom-call(s32[4,16]{1,0:T(4,128)S(4)} %get-tuple-element.33.links_ref, s32[16]{0:T(128)S(4)} %get-tuple-element.34.rows_ref, s32[16]{0:T(128)S(4)} %get-tuple-element.43.image_ref, ...), custom_call_target="tpu_custom_call" | custom-call | flops 1207959552 | bytes 2097152 | tf_op jit(solution)/shard_map/pallas_call | solution.py:515
  22.0 0.0 copy-start.8
  22.0 0.0 collective-permute-done.7.refs_1_
  22.0 0.0 collective-permute-done.8.refs_2_
  22.1 0.1 collective-permute-done.9.refs_3_
  22.2 0.4 shard_map.120
  22.5 0.0 copy-start.4
  22.5 0.0 copy-start.6
  22.6 0.1 collective-permute-start.10
  22.6 3.2 %collective-permute-start.11 = (bf16[208,128]{1,0:T(8,128)(2,1)S(1)}, bf16[208,128]{1,0:T(8,128)(2,1)S(1)}, u32[]{:S(2)}, u32[]{:S(2)}) collective-permute-start(bf16[208,128]{1,0:T(8,128)(2,1)S(1)} %get-tuple-element.49), channel_id=1, source_target_pairs={{0,4},{1,5},{2,6},{3,7},{4,0},{5,1},{6,2},{7,3},{8,12},{9,13},{10,... | collective-permute-start | bytes 159752 | tf_op jit(solution)/shard_map/ppermute | solution.py:477
  25.8 1.2 %collective-permute-start.12 = (bf16[208,128]{1,0:T(8,128)(2,1)S(1)}, bf16[208,128]{1,0:T(8,128)(2,1)S(1)}, u32[]{:S(2)}, u32[]{:S(2)}) collective-permute-start(bf16[208,128]{1,0:T(8,128)(2,1)S(1)} %get-tuple-element.50), channel_id=1, source_target_pairs={{0,6},{1,7},{2,4},{3,5},{4,2},{5,3},{6,0},{7,1},{8,14},{9,15},{10,... | collective-permute-start | bytes 159752 | tf_op jit(solution)/shard_map/ppermute | solution.py:477
  27.0 0.0 collective-permute-start.13
  27.0 0.0 collective-permute-done.10.refs_1_
  27.0 0.5 %collective-permute-start.14 = (bf16[208,128]{1,0:T(8,128)(2,1)S(1)}, bf16[208,128]{1,0:T(8,128)(2,1)S(1)}, u32[]{:S(2)}, u32[]{:S(2)}) collective-permute-start(bf16[208,128]{1,0:T(8,128)(2,1)S(1)} %collective-permute-done.10.refs_1_), channel_id=1, source_target_pairs={{0,1},{1,0},{2,3},{3,2},{4,5},{5,4},{6,7},{7,6},{8,9},{9,8},{10,11... | collective-permute-start | bytes 159752 | tf_op jit(solution)/shard_map/ppermute | solution.py:477
  27.5 0.4 %collective-permute-done.11.refs_2_ = bf16[208,128]{1,0:T(8,128)(2,1)S(1)} collective-permute-done((bf16[208,128]{1,0:T(8,128)(2,1)S(1)}, bf16[208,128]{1,0:T(8,128)(2,1)S(1)}, u32[]{:S(2)}, u32[]{:S(2)}) %collective-permute-start.11) | collective-permute-done | bytes 53280 | tf_op jit(solution)/shard_map/ppermute | solution.py:477
  28.0 0.0 collective-permute-start.15
  28.0 3.8 %collective-permute-done.12.refs_3_ = bf16[208,128]{1,0:T(8,128)(2,1)S(1)} collective-permute-done((bf16[208,128]{1,0:T(8,128)(2,1)S(1)}, bf16[208,128]{1,0:T(8,128)(2,1)S(1)}, u32[]{:S(2)}, u32[]{:S(2)}) %collective-permute-start.12) | collective-permute-done | bytes 53280 | tf_op jit(solution)/shard_map/ppermute | solution.py:477
  31.8 0.0 collective-permute-start.16
  31.8 0.0 copy-done.8
  31.8 0.1 fusion.5
  31.9 0.0 collective-permute-done.13.refs_4_
  31.9 0.0 collective-permute-done.14.refs_5_
  31.9 0.0 collective-permute-done.15.refs_6_
  31.9 1.1 %collective-permute-done.16.refs_7_ = bf16[208,128]{1,0:T(8,128)(2,1)S(1)} collective-permute-done((bf16[208,128]{1,0:T(8,128)(2,1)S(1)}, bf16[208,128]{1,0:T(8,128)(2,1)S(1)}, u32[]{:S(2)}, u32[]{:S(2)}) %collective-permute-start.16) | collective-permute-done | bytes 53280 | tf_op jit(solution)/shard_map/ppermute | solution.py:477
  33.0 0.1 shard_map.121
  33.1 0.1 collective-permute-start.17
  33.2 1.7 %collective-permute-start.18 = (bf16[128,128]{1,0:T(8,128)(2,1)S(1)}, bf16[128,128]{1,0:T(8,128)(2,1)S(1)}, u32[]{:S(2)}, u32[]{:S(2)}) collective-permute-start(bf16[128,128]{1,0:T(8,128)(2,1)S(1)} %get-tuple-element.53), channel_id=1, source_target_pairs={{0,4},{1,5},{2,6},{3,7},{4,0},{5,1},{6,2},{7,3},{8,12},{9,13},{10,... | collective-permute-start | bytes 98312 | tf_op jit(solution)/shard_map/ppermute | solution.py:477
  34.9 2.7 %collective-permute-start.19 = (bf16[128,128]{1,0:T(8,128)(2,1)S(1)}, bf16[128,128]{1,0:T(8,128)(2,1)S(1)}, u32[]{:S(2)}, u32[]{:S(2)}) collective-permute-start(bf16[128,128]{1,0:T(8,128)(2,1)S(1)} %get-tuple-element.54), channel_id=1, source_target_pairs={{0,6},{1,7},{2,4},{3,5},{4,2},{5,3},{6,0},{7,1},{8,14},{9,15},{10,... | collective-permute-start | bytes 98312 | tf_op jit(solution)/shard_map/ppermute | solution.py:477
  37.6 0.0 copy-done.3
  37.6 0.0 copy-done.4
  37.6 0.0 copy-done.6
  37.6 3.5 %shard_map.122 = (bf16[2,16,128,128]{3,2,1,0:T(8,128)(2,1)}, f32[4,128,128]{2,1,0:T(8,128)S(1)}, f32[8,128]{1,0:T(8,128)S(1)}, f32[80,128]{1,0:T(8,128)S(1)}) custom-call(s32[4,16]{1,0:T(4,128)S(4)} %get-tuple-element.33.links_ref, s32[16]{0:T(128)S(4)} %get-tuple-element.34.rows_ref, s32[16]{0:T(128)S(4)} %get-tuple-element.43.image_ref, ...), custom_call_target="tpu_custom_call" | custom-call | flops 1207959552 | bytes 2097152 | tf_op jit(solution)/shard_map/pallas_call | solution.py:515
  41.1 0.0 collective-permute-done.17.refs_1_
  41.1 0.0 collective-permute-done.18.refs_2_
  41.1 0.0 collective-permute-done.19.refs_3_
  41.1 1.0 %shard_map.123 = bf16[2,16,128,128]{3,2,1,0:T(8,128)(2,1)} custom-call(s32[4,16]{1,0:T(4,128)S(4)} %get-tuple-element.33.links_ref, s32[16]{0:T(128)S(4)} %get-tuple-element.34.rows_ref, bf16[128,128]{1,0:T(8,128)(2,1)S(1)} %get-tuple-element.51.refs_0_, bf16[128,128]{1,0:T(8,128)(2,1)S(1)} %collective-permute-done.17.refs_1_, ...), custom_call_target="tpu_custom_call", output_to_operand_aliasing={{}: (12, {})} | custom-call | tf_op jit(solution)/shard_map/pallas_call | solution.py:528
  (3 shorter events, 0.0 us)
Async XLA Ops:
  0.0 13.3 %copy-start.7 = (bf16[3,3,128,128]{3,2,1,0:T(8,128)(2,1)S(1)}, bf16[3,3,128,128]{3,2,1,0:T(8,128)(2,1)}, u32[]{:S(2)}) copy-start(bf16[3,3,128,128]{3,2,1,0:T(8,128)(2,1)} %param.18) | copy-start | bytes 884740
  0.0 19.1 %copy-start = (bf16[2,16,128,128]{3,2,1,0:T(8,128)(2,1)S(1)}, bf16[2,16,128,128]{3,2,1,0:T(8,128)(2,1)}, u32[]{:S(2)}) copy-start(bf16[2,16,128,128]{3,2,1,0:T(8,128)(2,1)} %refs_14_.1) | copy-start | bytes 3145732
  0.0 19.1 %copy-start.1 = (f32[128]{0:T(128)S(1)}, f32[128]{0:T(128)}, u32[]{:S(2)}) copy-start(f32[128]{0:T(128)} %param.16) | copy-start | bytes 1540
  0.0 19.1 %copy-start.2 = (f32[128]{0:T(128)S(1)}, f32[128]{0:T(128)}, u32[]{:S(2)}) copy-start(f32[128]{0:T(128)} %param.17) | copy-start | bytes 1540
  0.0 19.1 %copy-start.5 = (f32[128]{0:T(128)S(1)}, f32[128]{0:T(128)}, u32[]{:S(2)}) copy-start(f32[128]{0:T(128)} %param.19) | copy-start | bytes 1540
  1.6 5.7 %collective-permute-start = (bf16[208,128]{1,0:T(8,128)(2,1)S(1)}, bf16[208,128]{1,0:T(8,128)(2,1)S(1)}, u32[]{:S(2)}, u32[]{:S(2)}) collective-permute-start(bf16[208,128]{1,0:T(8,128)(2,1)S(1)} %get-tuple-element.36), channel_id=1, source_target_pairs={{0,2},{1,3},{2,0},{3,1},{4,6},{5,7},{6,4},{7,5},{8,10},{9,11},{10,... | collective-permute-start | bytes 159752 | tf_op jit(solution)/shard_map/ppermute | solution.py:477
  4.8 6.1 %collective-permute-start.1 = (bf16[208,128]{1,0:T(8,128)(2,1)S(1)}, bf16[208,128]{1,0:T(8,128)(2,1)S(1)}, u32[]{:S(2)}, u32[]{:S(2)}) collective-permute-start(bf16[208,128]{1,0:T(8,128)(2,1)S(1)} %get-tuple-element.37), channel_id=1, source_target_pairs={{0,4},{1,5},{2,6},{3,7},{4,0},{5,1},{6,2},{7,3},{8,12},{9,13},{10,... | collective-permute-start | bytes 159752 | tf_op jit(solution)/shard_map/ppermute | solution.py:477
  7.4 5.9 %collective-permute-start.2 = (bf16[208,128]{1,0:T(8,128)(2,1)S(1)}, bf16[208,128]{1,0:T(8,128)(2,1)S(1)}, u32[]{:S(2)}, u32[]{:S(2)}) collective-permute-start(bf16[208,128]{1,0:T(8,128)(2,1)S(1)} %get-tuple-element.38), channel_id=1, source_target_pairs={{0,6},{1,7},{2,4},{3,5},{4,2},{5,3},{6,0},{7,1},{8,14},{9,15},{10,... | collective-permute-start | bytes 159752 | tf_op jit(solution)/shard_map/ppermute | solution.py:477
  7.4 6.0 %collective-permute-start.3 = (bf16[208,128]{1,0:T(8,128)(2,1)S(1)}, bf16[208,128]{1,0:T(8,128)(2,1)S(1)}, u32[]{:S(2)}, u32[]{:S(2)}) collective-permute-start(bf16[208,128]{1,0:T(8,128)(2,1)S(1)} %get-tuple-element.35.refs_0_), channel_id=1, source_target_pairs={{0,1},{1,0},{2,3},{3,2},{4,5},{5,4},{6,7},{7,6},{8,9},{9,8},{10,11... | collective-permute-start | bytes 159752 | tf_op jit(solution)/shard_map/ppermute | solution.py:477
  7.4 6.0 %collective-permute-start.4 = (bf16[208,128]{1,0:T(8,128)(2,1)S(1)}, bf16[208,128]{1,0:T(8,128)(2,1)S(1)}, u32[]{:S(2)}, u32[]{:S(2)}) collective-permute-start(bf16[208,128]{1,0:T(8,128)(2,1)S(1)} %collective-permute-done.refs_1_), channel_id=1, source_target_pairs={{0,1},{1,0},{2,3},{3,2},{4,5},{5,4},{6,7},{7,6},{8,9},{9,8},{10,11... | collective-permute-start | bytes 159752 | tf_op jit(solution)/shard_map/ppermute | solution.py:477
  10.8 2.6 %collective-permute-start.5 = (bf16[208,128]{1,0:T(8,128)(2,1)S(1)}, bf16[208,128]{1,0:T(8,128)(2,1)S(1)}, u32[]{:S(2)}, u32[]{:S(2)}) collective-permute-start(bf16[208,128]{1,0:T(8,128)(2,1)S(1)} %collective-permute-done.1.refs_2_), channel_id=1, source_target_pairs={{0,1},{1,0},{2,3},{3,2},{4,5},{5,4},{6,7},{7,6},{8,9},{9,8},{10,11... | collective-permute-start | bytes 159752 | tf_op jit(solution)/shard_map/ppermute | solution.py:477
  13.3 1.2 %collective-permute-start.6 = (bf16[208,128]{1,0:T(8,128)(2,1)S(1)}, bf16[208,128]{1,0:T(8,128)(2,1)S(1)}, u32[]{:S(2)}, u32[]{:S(2)}) collective-permute-start(bf16[208,128]{1,0:T(8,128)(2,1)S(1)} %collective-permute-done.2.refs_3_), channel_id=1, source_target_pairs={{0,1},{1,0},{2,3},{3,2},{4,5},{5,4},{6,7},{7,6},{8,9},{9,8},{10,11... | collective-permute-start | bytes 159752 | tf_op jit(solution)/shard_map/ppermute | solution.py:477
  14.7 7.4 %collective-permute-start.7 = (bf16[128,128]{1,0:T(8,128)(2,1)S(1)}, bf16[128,128]{1,0:T(8,128)(2,1)S(1)}, u32[]{:S(2)}, u32[]{:S(2)}) collective-permute-start(bf16[128,128]{1,0:T(8,128)(2,1)S(1)} %get-tuple-element.40), channel_id=1, source_target_pairs={{0,2},{1,3},{2,0},{3,1},{4,6},{5,7},{6,4},{7,5},{8,10},{9,11},{10,... | collective-permute-start | bytes 98312 | tf_op jit(solution)/shard_map/ppermute | solution.py:477
  14.7 7.3 %collective-permute-start.8 = (bf16[128,128]{1,0:T(8,128)(2,1)S(1)}, bf16[128,128]{1,0:T(8,128)(2,1)S(1)}, u32[]{:S(2)}, u32[]{:S(2)}) collective-permute-start(bf16[128,128]{1,0:T(8,128)(2,1)S(1)} %get-tuple-element.41), channel_id=1, source_target_pairs={{0,4},{1,5},{2,6},{3,7},{4,0},{5,1},{6,2},{7,3},{8,12},{9,13},{10,... | collective-permute-start | bytes 98312 | tf_op jit(solution)/shard_map/ppermute | solution.py:477
  16.4 5.7 %collective-permute-start.9 = (bf16[128,128]{1,0:T(8,128)(2,1)S(1)}, bf16[128,128]{1,0:T(8,128)(2,1)S(1)}, u32[]{:S(2)}, u32[]{:S(2)}) collective-permute-start(bf16[128,128]{1,0:T(8,128)(2,1)S(1)} %get-tuple-element.42), channel_id=1, source_target_pairs={{0,6},{1,7},{2,4},{3,5},{4,2},{5,3},{6,0},{7,1},{8,14},{9,15},{10,... | collective-permute-start | bytes 98312 | tf_op jit(solution)/shard_map/ppermute | solution.py:477
  22.0 9.8 %copy-start.8 = (bf16[3,3,128,128]{3,2,1,0:T(8,128)(2,1)S(1)}, bf16[3,3,128,128]{3,2,1,0:T(8,128)(2,1)}, u32[]{:S(2)}) copy-start(bf16[3,3,128,128]{3,2,1,0:T(8,128)(2,1)} %param.22) | copy-start | bytes 884740
  22.5 15.1 %copy-start.3 = (f32[128]{0:T(128)S(1)}, f32[128]{0:T(128)}, u32[]{:S(2)}) copy-start(f32[128]{0:T(128)} %param.20) | copy-start | bytes 1540
  22.5 15.1 %copy-start.4 = (f32[128]{0:T(128)S(1)}, f32[128]{0:T(128)}, u32[]{:S(2)}) copy-start(f32[128]{0:T(128)} %param.21) | copy-start | bytes 1540
  22.5 15.1 %copy-start.6 = (f32[128]{0:T(128)S(1)}, f32[128]{0:T(128)}, u32[]{:S(2)}) copy-start(f32[128]{0:T(128)} %param.23) | copy-start | bytes 1540
  22.6 4.5 %collective-permute-start.10 = (bf16[208,128]{1,0:T(8,128)(2,1)S(1)}, bf16[208,128]{1,0:T(8,128)(2,1)S(1)}, u32[]{:S(2)}, u32[]{:S(2)}) collective-permute-start(bf16[208,128]{1,0:T(8,128)(2,1)S(1)} %get-tuple-element.48), channel_id=1, source_target_pairs={{0,2},{1,3},{2,0},{3,1},{4,6},{5,7},{6,4},{7,5},{8,10},{9,11},{10,... | collective-permute-start | bytes 159752 | tf_op jit(solution)/shard_map/ppermute | solution.py:477
  22.6 5.3 %collective-permute-start.11 = (bf16[208,128]{1,0:T(8,128)(2,1)S(1)}, bf16[208,128]{1,0:T(8,128)(2,1)S(1)}, u32[]{:S(2)}, u32[]{:S(2)}) collective-permute-start(bf16[208,128]{1,0:T(8,128)(2,1)S(1)} %get-tuple-element.49), channel_id=1, source_target_pairs={{0,4},{1,5},{2,6},{3,7},{4,0},{5,1},{6,2},{7,3},{8,12},{9,13},{10,... | collective-permute-start | bytes 159752 | tf_op jit(solution)/shard_map/ppermute | solution.py:477
  25.8 5.9 %collective-permute-start.12 = (bf16[208,128]{1,0:T(8,128)(2,1)S(1)}, bf16[208,128]{1,0:T(8,128)(2,1)S(1)}, u32[]{:S(2)}, u32[]{:S(2)}) collective-permute-start(bf16[208,128]{1,0:T(8,128)(2,1)S(1)} %get-tuple-element.50), channel_id=1, source_target_pairs={{0,6},{1,7},{2,4},{3,5},{4,2},{5,3},{6,0},{7,1},{8,14},{9,15},{10,... | collective-permute-start | bytes 159752 | tf_op jit(solution)/shard_map/ppermute | solution.py:477
  27.0 4.9 %collective-permute-start.13 = (bf16[208,128]{1,0:T(8,128)(2,1)S(1)}, bf16[208,128]{1,0:T(8,128)(2,1)S(1)}, u32[]{:S(2)}, u32[]{:S(2)}) collective-permute-start(bf16[208,128]{1,0:T(8,128)(2,1)S(1)} %get-tuple-element.47.refs_0_), channel_id=1, source_target_pairs={{0,1},{1,0},{2,3},{3,2},{4,5},{5,4},{6,7},{7,6},{8,9},{9,8},{10,11... | collective-permute-start | bytes 159752 | tf_op jit(solution)/shard_map/ppermute | solution.py:477
  27.0 4.9 %collective-permute-start.14 = (bf16[208,128]{1,0:T(8,128)(2,1)S(1)}, bf16[208,128]{1,0:T(8,128)(2,1)S(1)}, u32[]{:S(2)}, u32[]{:S(2)}) collective-permute-start(bf16[208,128]{1,0:T(8,128)(2,1)S(1)} %collective-permute-done.10.refs_1_), channel_id=1, source_target_pairs={{0,1},{1,0},{2,3},{3,2},{4,5},{5,4},{6,7},{7,6},{8,9},{9,8},{10,11... | collective-permute-start | bytes 159752 | tf_op jit(solution)/shard_map/ppermute | solution.py:477
  28.0 3.9 %collective-permute-start.15 = (bf16[208,128]{1,0:T(8,128)(2,1)S(1)}, bf16[208,128]{1,0:T(8,128)(2,1)S(1)}, u32[]{:S(2)}, u32[]{:S(2)}) collective-permute-start(bf16[208,128]{1,0:T(8,128)(2,1)S(1)} %collective-permute-done.11.refs_2_), channel_id=1, source_target_pairs={{0,1},{1,0},{2,3},{3,2},{4,5},{5,4},{6,7},{7,6},{8,9},{9,8},{10,11... | collective-permute-start | bytes 159752 | tf_op jit(solution)/shard_map/ppermute | solution.py:477
  31.8 1.2 %collective-permute-start.16 = (bf16[208,128]{1,0:T(8,128)(2,1)S(1)}, bf16[208,128]{1,0:T(8,128)(2,1)S(1)}, u32[]{:S(2)}, u32[]{:S(2)}) collective-permute-start(bf16[208,128]{1,0:T(8,128)(2,1)S(1)} %collective-permute-done.12.refs_3_), channel_id=1, source_target_pairs={{0,1},{1,0},{2,3},{3,2},{4,5},{5,4},{6,7},{7,6},{8,9},{9,8},{10,11... | collective-permute-start | bytes 159752 | tf_op jit(solution)/shard_map/ppermute | solution.py:477
  33.1 7.9 %collective-permute-start.17 = (bf16[128,128]{1,0:T(8,128)(2,1)S(1)}, bf16[128,128]{1,0:T(8,128)(2,1)S(1)}, u32[]{:S(2)}, u32[]{:S(2)}) collective-permute-start(bf16[128,128]{1,0:T(8,128)(2,1)S(1)} %get-tuple-element.52), channel_id=1, source_target_pairs={{0,2},{1,3},{2,0},{3,1},{4,6},{5,7},{6,4},{7,5},{8,10},{9,11},{10,... | collective-permute-start | bytes 98312 | tf_op jit(solution)/shard_map/ppermute | solution.py:477
  33.2 7.9 %collective-permute-start.18 = (bf16[128,128]{1,0:T(8,128)(2,1)S(1)}, bf16[128,128]{1,0:T(8,128)(2,1)S(1)}, u32[]{:S(2)}, u32[]{:S(2)}) collective-permute-start(bf16[128,128]{1,0:T(8,128)(2,1)S(1)} %get-tuple-element.53), channel_id=1, source_target_pairs={{0,4},{1,5},{2,6},{3,7},{4,0},{5,1},{6,2},{7,3},{8,12},{9,13},{10,... | collective-permute-start | bytes 98312 | tf_op jit(solution)/shard_map/ppermute | solution.py:477
  34.9 6.2 %collective-permute-start.19 = (bf16[128,128]{1,0:T(8,128)(2,1)S(1)}, bf16[128,128]{1,0:T(8,128)(2,1)S(1)}, u32[]{:S(2)}, u32[]{:S(2)}) collective-permute-start(bf16[128,128]{1,0:T(8,128)(2,1)S(1)} %get-tuple-element.54), channel_id=1, source_target_pairs={{0,6},{1,7},{2,4},{3,5},{4,2},{5,3},{6,0},{7,1},{8,14},{9,15},{10,... | collective-permute-start | bytes 98312 | tf_op jit(solution)/shard_map/ppermute | solution.py:477

commit v2 on v1

--- a/solution.py
+++ b/solution.py
@@ -28,9 +28,10 @@
     def __init__(self, size, count, rows, cols, channels):
         self.size, self.count, self.rows, self.cols, self.channels = size, count, rows, cols, channels
         chips = size // 2
-        fits = size % 2 == 0 and chips & (chips - 1) == 0 and cols % (16 * max(chips, 1)) == 0
-        self.chunks = chips if fits and chips > 1 else 1
-        self.width = cols // self.chunks
+        self.direct = size % 2 == 0 and chips in (2, 4, 8) and cols % 32 == 0
+        self.targets = chips if self.direct else 1
+        self.parts = 2 if self.direct else 1
+        self.width = cols // self.parts
         self.stat_rows = round_up(6 * count, 16)
         self.row_base = self.stat_rows
         self.col_base = self.row_base + 2 * count * self.width
@@ -41,24 +42,27 @@
         index = lax.axis_index(AXIS)
         return lax.div(index, 2), lax.rem(index, 2)
 
-    def chunk(self, k):
-        return lax.bitwise_xor(self.place()[0], k) if self.chunks > 1 else 0
+    def window(self, k):
+        if not self.direct:
+            return pl.ds(0, self.width)
+        part = lax.bitwise_and(lax.bitwise_xor(self.place()[0], k), 1)
+        return pl.ds(pl.multiple_of(part * self.width, 16), self.width)
 
     def slot_of(self, device):
-        if self.chunks == 1:
+        if not self.direct:
             return device
         chip, core = self.place()
         other = lax.bitwise_xor(lax.rem(device, 2), core)
-        return other * self.chunks + lax.bitwise_xor(lax.div(device, 2), chip)
+        return other * self.targets + lax.bitwise_xor(lax.div(device, 2), chip)
 
     def device_of(self, slot):
-        if self.chunks == 1:
+        if not self.direct:
             return slot
         chip, core = self.place()
-        return lax.bitwise_xor(chip, slot % self.chunks) * 2 + lax.bitwise_xor(core, slot // self.chunks)
+        return lax.bitwise_xor(chip, slot % self.targets) * 2 + lax.bitwise_xor(core, slot // self.targets)
 
     def target(self, k):
-        if self.chunks == 1:
+        if not self.direct:
             return lax.axis_index(AXIS)
         chip, core = self.place()
         return lax.bitwise_xor(chip, k) * 2 + core
@@ -111,15 +115,13 @@
 
 
 def fill_buffers(plan, stats, edge_of, columns, buf_refs):
-    for k in range(plan.chunks):
+    for k in range(plan.targets):
         buf_refs[k][0 : plan.stat_rows, :] = stats
-        start = plan.chunk(k) * plan.width
-        if plan.chunks > 1:
-            start = pl.multiple_of(start, 16)
+        window = plan.window(k)
         for tile in range(plan.count):
             for edge in range(2):
                 at = plan.row_base + (2 * tile + edge) * plan.width
-                buf_refs[k][at : at + plan.width, :] = edge_of(tile, edge, pl.ds(start, plan.width))
+                buf_refs[k][at : at + plan.width, :] = edge_of(tile, edge, window)
         for place, column in enumerate(columns):
             at = plan.col_base + place * plan.rows
             buf_refs[k][at : at + plan.rows, :] = column
@@ -131,7 +133,7 @@
 
 
 def edges_kernel(plan, links_hbm, rows_hbm, image_hbm, x_hbm, links_ref, rows_ref, image_ref, *refs):
-    buf_refs, (x_ref, sems) = refs[: plan.chunks], refs[plan.chunks :]
+    buf_refs, (x_ref, sems) = refs[: plan.targets], refs[plan.targets :]
     tables = [
         pltpu.make_async_copy(source, target, sems.at[plan.count + place])
         for place, (source, target) in enumerate(
@@ -177,7 +179,7 @@
         self.plan = plan
         self.row_base, self.col_base = plan.row_base, plan.col_base
         self.held = bufs[0]
-        if plan.chunks > 1:
+        if plan.direct:
             self.held = held
             self.row_base, self.col_base = 0, plan.stat_rows
             for slot in range(plan.slots):
@@ -204,18 +206,18 @@
 
 def held_scratch(plan, part):
     rows = plan.col_base - plan.row_base if part == "rows" else plan.buf_rows - plan.col_base + plan.stat_rows
-    return pltpu.VMEM((plan.slots, rows, plan.channels) if plan.chunks > 1 else (1, 16, plan.channels), bf16)
+    return pltpu.VMEM((plan.slots, rows, plan.channels) if plan.direct else (1, 16, plan.channels), bf16)
 
 
 def buffer_inputs(plan, refs):
-    inputs = plan.slots if plan.chunks > 1 else 1
+    inputs = plan.slots if plan.direct else 1
     return refs[:inputs], refs[inputs:]
 
 
 def route_kernel(plan, links_ref, *refs):
     bufs, refs = buffer_inputs(plan, refs)
     send_refs, held = refs[:-1], Held(plan, bufs, refs[-1], "rows")
-    for k in range(plan.chunks):
+    for k in range(plan.parts):
         first = plan.target(k) * plan.count
         for tile in range(plan.count):
             for edge in range(2):
@@ -377,7 +379,7 @@
 
 
 def ends_kernel(plan, last, links_ref, rows_ref, *refs):
-    halo_refs, refs = refs[: plan.chunks], refs[plan.chunks :]
+    halo_refs, refs = refs[: plan.parts], refs[plan.parts :]
     partial_ref, norm_ref, side_ref, gain_ref, shift_ref, weight_ref = refs[:6]
     refs = refs[6:]
     count, rows, cols, channels = plan.count, plan.rows, plan.cols, plan.channels
@@ -387,13 +389,10 @@
         ends_ref, buf_refs, halo = refs[0], refs[1:-1], refs[-1]
     first = lax.axis_index(AXIS) * count
     own_rows = own_values(plan, rows_ref)
-    for k in range(plan.chunks):
-        start = plan.chunk(k) * plan.width
-        if plan.chunks > 1:
-            start = pl.multiple_of(start, 16)
+    for k in range(plan.parts):
         for place in range(2 * count):
             at = place * plan.width
-            halo[place, pl.ds(start, plan.width), :] = halo_refs[k][at : at + plan.width, :]
+            halo[place, plan.window(k), :] = halo_refs[k][at : at + plan.width, :]
     depth = 3 * channels
     copies, sums, spreads, columns = [], [], [], []
     for tile in range(count):
@@ -469,7 +468,7 @@
 ):
     count, rows, cols, channels = feature_tiles.shape
     plan = Plan(size, count, rows, cols, channels)
-    buf_shape = [jax.ShapeDtypeStruct((plan.buf_rows, channels), bf16)] * plan.chunks
+    buf_shape = [jax.ShapeDtypeStruct((plan.buf_rows, channels), bf16)] * plan.targets
     limit = 24 * 1024 * 1024
     params = pltpu.CompilerParams(vmem_limit_bytes=limit)
 
@@ -478,12 +477,12 @@
 
     def spread(arrays):
         result = [arrays[0]]
-        for k in range(1, plan.chunks):
+        for k in range(1, len(arrays)):
             result.append(swap(arrays[k], 2 * k))
         return result
 
     def exchange(bufs):
-        if plan.chunks == 1:
+        if not plan.direct:
             return [lax.all_gather(bufs[0], AXIS)]
         own = spread(bufs)
         return own + [swap(array, 1) for array in own]
@@ -501,9 +500,9 @@
         arrays = exchange(bufs)
         send = pl.pallas_call(
             functools.partial(route_kernel, plan),
-            out_shape=[shape((2 * count * plan.width, channels), bf16)] * plan.chunks,
+            out_shape=[shape((2 * count * plan.width, channels), bf16)] * plan.parts,
             in_specs=[SMEM] + [VMEM] * len(arrays),
-            out_specs=[VMEM] * plan.chunks,
+            out_specs=[VMEM] * plan.parts,
             scratch_shapes=[held_scratch(plan, "rows")],
             compiler_params=params,
         )(scalars[0], *arrays)
@@ -538,7 +537,7 @@
             functools.partial(ends_kernel, plan, last),
             out_shape=[ends_shape] + buf_shape,
             in_specs=[SMEM] * 2 + [VMEM] * len(operands),
-            out_specs=[VMEM] * (1 + plan.chunks),
+            out_specs=[VMEM] * (1 + plan.targets),
             scratch_shapes=scratch,
             compiler_params=params,
         )(*scalars[:2], *operands)
@@ -550,7 +549,7 @@
         functools.partial(edges_kernel, plan),
         out_shape=[pltpu.SMEM(table.shape, jnp.int32) for table in tables] + buf_shape,
         in_specs=[HBM] * 4,
-        out_specs=[SMEM] * 3 + [VMEM] * plan.chunks,
+        out_specs=[SMEM] * 3 + [VMEM] * plan.targets,
         scratch_shapes=[pltpu.VMEM(feature_tiles.shape, bf16), pltpu.SemaphoreType.DMA((count + 3,))],
         compiler_params=params,
         name="edges",

time: 42.2 us -> 38.5 us (0.912)
  starting transfers between devices: 20.1 us -> 14.5 us
  waiting for transfers between devices: 12 us -> 14.1 us
    ppermute x20 -> x16, starting transfers between devices: 20.1 us -> 14.5 us  [swap(): return lax.ppermute(array, AXIS, [(i, i ^ distance) for i in range(size)])]
    ppermute x20 -> x16, waiting for transfers between devices: 12 us -> 14.1 us  [swap(): return lax.ppermute(array, AXIS, [(i, i ^ distance) for i in range(size)])]
  transfers between devices with their start and end apart: 20 -> 16, of which waited for: 7 -> 8; matrix products, arithmetic and copies ran while one was open for 0% -> 0% of each run, Pallas kernels for 15% -> 17%
where the time goes in v2:
time: 38.5 us; the launch traced here: 38.3 us
  starting transfers between devices  14.5 us (38%)
  waiting for transfers between devices  14.1 us (37%)
  Pallas kernels  9.37 us (24%)
    ppermute x16, starting transfers between devices, swap(): return lax.ppermute(array, AXIS, [(i, i ^ distance) for i in range(size)])  14.5 us
    ppermute x16, waiting for transfers between devices, swap(): return lax.ppermute(array, AXIS, [(i, i ^ distance) for i in range(size)])  14.1 us
    pallas_call x2, Pallas kernels, stage(): pl.pallas_call(functools.partial(middle_kernel, plan, last), out_shape=[t...  6.35 us
    pallas_call x1, Pallas kernels, shards(): pl.pallas_call(functools.partial(edges_kernel, plan), out_shape=[pltpu.SM...  1.57 us
    pallas_call x1, Pallas kernels, stage(): pl.pallas_call(functools.partial(ends_kernel, plan, last), out_shape=tile...  0.95 us
  transfers between devices with their start and end apart: 16, of which 8 were waited for; matrix products, arithmetic and copies ran while one was open for 0% of the time, Pallas kernels for 17%

profile of v2, /device:TPU:0, one launch (start us, length us, event | category | flops | bytes accessed | tf_op | source)
XLA Modules:
  0.0 38.3 jit_solution(6419171919163761816)
XLA Ops:
  0.0 0.0 copy-start.7
  0.0 1.6 %edges.1 = (s32[4,16]{1,0:T(4,128)S(4)}, s32[16]{0:T(128)S(4)}, s32[16]{0:T(128)S(4)}, bf16[336,128]{1,0:T(8,128)(2,1)S(1)}, bf16[336,128]{1,0:T(8,128)(2,1)S(1)...) custom-call(s32[4,16]{1,0:T(4,128)} %bitcast.23, s32[16]{0:T(128)} %rows_hbm.1, s32[16]{0:T(128)} %image_hbm.1, ...), custom_call_target="tpu_custom_call" | custom-call | tf_op jit(solution)/shard_map/edges/pallas_call | solution.py:548
  1.6 0.0 copy-start
  1.6 0.0 copy-start.1
  1.6 0.0 copy-start.2
  1.6 0.0 copy-start.5
  1.6 3.1 %collective-permute-start = (bf16[336,128]{1,0:T(8,128)(2,1)S(1)}, bf16[336,128]{1,0:T(8,128)(2,1)S(1)}, u32[]{:S(2)}, u32[]{:S(2)}) collective-permute-start(bf16[336,128]{1,0:T(8,128)(2,1)S(1)} %get-tuple-element.32), channel_id=1, source_target_pairs={{0,2},{1,3},{2,0},{3,1},{4,6},{5,7},{6,4},{7,5},{8,10},{9,11},{10,... | collective-permute-start | bytes 258056 | tf_op jit(solution)/shard_map/ppermute | solution.py:476
  4.7 2.6 %collective-permute-start.1 = (bf16[336,128]{1,0:T(8,128)(2,1)S(1)}, bf16[336,128]{1,0:T(8,128)(2,1)S(1)}, u32[]{:S(2)}, u32[]{:S(2)}) collective-permute-start(bf16[336,128]{1,0:T(8,128)(2,1)S(1)} %get-tuple-element.33), channel_id=1, source_target_pairs={{0,4},{1,5},{2,6},{3,7},{4,0},{5,1},{6,2},{7,3},{8,12},{9,13},{10,... | collective-permute-start | bytes 258056 | tf_op jit(solution)/shard_map/ppermute | solution.py:476
  7.3 0.0 collective-permute-start.2
  7.3 0.0 collective-permute-start.3
  7.3 0.0 collective-permute-done.refs_1_
  7.3 0.5 %collective-permute-start.4 = (bf16[336,128]{1,0:T(8,128)(2,1)S(1)}, bf16[336,128]{1,0:T(8,128)(2,1)S(1)}, u32[]{:S(2)}, u32[]{:S(2)}) collective-permute-start(bf16[336,128]{1,0:T(8,128)(2,1)S(1)} %collective-permute-done.refs_1_), channel_id=1, source_target_pairs={{0,1},{1,0},{2,3},{3,2},{4,5},{5,4},{6,7},{7,6},{8,9},{9,8},{10,11... | collective-permute-start | bytes 258056 | tf_op jit(solution)/shard_map/ppermute | solution.py:476
  7.8 6.4 %collective-permute-done.1.refs_2_ = bf16[336,128]{1,0:T(8,128)(2,1)S(1)} collective-permute-done((bf16[336,128]{1,0:T(8,128)(2,1)S(1)}, bf16[336,128]{1,0:T(8,128)(2,1)S(1)}, u32[]{:S(2)}, u32[]{:S(2)}) %collective-permute-start.1) | collective-permute-done | bytes 86048 | tf_op jit(solution)/shard_map/ppermute | solution.py:476
  14.2 0.0 collective-permute-start.5
  14.2 0.0 collective-permute-done.2.refs_3_
  14.2 0.5 %collective-permute-start.6 = (bf16[336,128]{1,0:T(8,128)(2,1)S(1)}, bf16[336,128]{1,0:T(8,128)(2,1)S(1)}, u32[]{:S(2)}, u32[]{:S(2)}) collective-permute-start(bf16[336,128]{1,0:T(8,128)(2,1)S(1)} %collective-permute-done.2.refs_3_), channel_id=1, source_target_pairs={{0,1},{1,0},{2,3},{3,2},{4,5},{5,4},{6,7},{7,6},{8,9},{9,8},{10,11... | collective-permute-start | bytes 258056 | tf_op jit(solution)/shard_map/ppermute | solution.py:476
  14.8 0.0 copy-done.7
  14.8 0.1 fusion.4
  14.8 0.0 collective-permute-done.3.refs_4_
  14.8 0.0 collective-permute-done.4.refs_5_
  14.9 0.7 %collective-permute-done.5.refs_6_ = bf16[336,128]{1,0:T(8,128)(2,1)S(1)} collective-permute-done((bf16[336,128]{1,0:T(8,128)(2,1)S(1)}, bf16[336,128]{1,0:T(8,128)(2,1)S(1)}, u32[]{:S(2)}, u32[]{:S(2)}) %collective-permute-start.5) | collective-permute-done | bytes 86048 | tf_op jit(solution)/shard_map/ppermute | solution.py:476
  15.5 0.2 collective-permute-done.6.refs_7_
  15.7 0.1 shard_map.118
  15.8 1.4 %collective-permute-start.7 = (bf16[256,128]{1,0:T(8,128)(2,1)S(1)}, bf16[256,128]{1,0:T(8,128)(2,1)S(1)}, u32[]{:S(2)}, u32[]{:S(2)}) collective-permute-start(bf16[256,128]{1,0:T(8,128)(2,1)S(1)} %get-tuple-element.36), channel_id=1, source_target_pairs={{0,2},{1,3},{2,0},{3,1},{4,6},{5,7},{6,4},{7,5},{8,10},{9,11},{10,... | collective-permute-start | bytes 196616 | tf_op jit(solution)/shard_map/ppermute | solution.py:476
  17.2 0.0 copy-done
  17.2 0.0 copy-done.1
  17.2 0.0 copy-done.2
  17.2 0.0 copy-done.5
  17.2 2.9 %shard_map.119 = (bf16[2,16,128,128]{3,2,1,0:T(8,128)(2,1)S(1)}, f32[4,128,128]{2,1,0:T(8,128)S(1)}, f32[8,128]{1,0:T(8,128)S(1)}, f32[80,128]{1,0:T(8,128)S(1)}) custom-call(s32[4,16]{1,0:T(4,128)S(4)} %get-tuple-element.29.links_ref, s32[16]{0:T(128)S(4)} %get-tuple-element.30.rows_ref, s32[16]{0:T(128)S(4)} %get-tuple-element.37.image_ref, ...), custom_call_target="tpu_custom_call" | custom-call | flops 1207959552 | bytes 2097152 | tf_op jit(solution)/shard_map/pallas_call | solution.py:514
  20.1 0.0 copy-start.8
  20.1 0.1 collective-permute-done.7.refs_1_
  20.2 0.4 shard_map.120
  20.6 0.0 copy-start.3
  20.6 0.0 copy-start.4
  20.6 0.0 copy-start.6
  20.6 1.3 %collective-permute-start.8 = (bf16[336,128]{1,0:T(8,128)(2,1)S(1)}, bf16[336,128]{1,0:T(8,128)(2,1)S(1)}, u32[]{:S(2)}, u32[]{:S(2)}) collective-permute-start(bf16[336,128]{1,0:T(8,128)(2,1)S(1)} %get-tuple-element.42), channel_id=1, source_target_pairs={{0,2},{1,3},{2,0},{3,1},{4,6},{5,7},{6,4},{7,5},{8,10},{9,11},{10,... | collective-permute-start | bytes 258056 | tf_op jit(solution)/shard_map/ppermute | solution.py:476
  21.9 1.8 %collective-permute-start.9 = (bf16[336,128]{1,0:T(8,128)(2,1)S(1)}, bf16[336,128]{1,0:T(8,128)(2,1)S(1)}, u32[]{:S(2)}, u32[]{:S(2)}) collective-permute-start(bf16[336,128]{1,0:T(8,128)(2,1)S(1)} %get-tuple-element.43), channel_id=1, source_target_pairs={{0,4},{1,5},{2,6},{3,7},{4,0},{5,1},{6,2},{7,3},{8,12},{9,13},{10,... | collective-permute-start | bytes 258056 | tf_op jit(solution)/shard_map/ppermute | solution.py:476
  23.7 1.3 %collective-permute-start.10 = (bf16[336,128]{1,0:T(8,128)(2,1)S(1)}, bf16[336,128]{1,0:T(8,128)(2,1)S(1)}, u32[]{:S(2)}, u32[]{:S(2)}) collective-permute-start(bf16[336,128]{1,0:T(8,128)(2,1)S(1)} %get-tuple-element.44), channel_id=1, source_target_pairs={{0,6},{1,7},{2,4},{3,5},{4,2},{5,3},{6,0},{7,1},{8,14},{9,15},{10,... | collective-permute-start | bytes 258056 | tf_op jit(solution)/shard_map/ppermute | solution.py:476
  25.0 0.0 collective-permute-start.11
  25.0 0.9 %collective-permute-done.8.refs_1_ = bf16[336,128]{1,0:T(8,128)(2,1)S(1)} collective-permute-done((bf16[336,128]{1,0:T(8,128)(2,1)S(1)}, bf16[336,128]{1,0:T(8,128)(2,1)S(1)}, u32[]{:S(2)}, u32[]{:S(2)}) %collective-permute-start.8) | collective-permute-done | bytes 86048 | tf_op jit(solution)/shard_map/ppermute | solution.py:476
  26.0 0.0 collective-permute-start.12
  26.0 5.0 %collective-permute-done.9.refs_2_ = bf16[336,128]{1,0:T(8,128)(2,1)S(1)} collective-permute-done((bf16[336,128]{1,0:T(8,128)(2,1)S(1)}, bf16[336,128]{1,0:T(8,128)(2,1)S(1)}, u32[]{:S(2)}, u32[]{:S(2)}) %collective-permute-start.9) | collective-permute-done | bytes 86048 | tf_op jit(solution)/shard_map/ppermute | solution.py:476
  31.0 0.0 collective-permute-start.13
  31.0 0.0 collective-permute-done.10.refs_3_
  31.0 0.5 %collective-permute-start.14 = (bf16[336,128]{1,0:T(8,128)(2,1)S(1)}, bf16[336,128]{1,0:T(8,128)(2,1)S(1)}, u32[]{:S(2)}, u32[]{:S(2)}) collective-permute-start(bf16[336,128]{1,0:T(8,128)(2,1)S(1)} %collective-permute-done.10.refs_3_), channel_id=1, source_target_pairs={{0,1},{1,0},{2,3},{3,2},{4,5},{5,4},{6,7},{7,6},{8,9},{9,8},{10,11... | collective-permute-start | bytes 258056 | tf_op jit(solution)/shard_map/ppermute | solution.py:476
  31.5 0.0 copy-done.8
  31.5 0.1 fusion.5
  31.6 0.0 collective-permute-done.11.refs_4_
  31.6 0.0 collective-permute-done.12.refs_5_
  31.6 0.7 %collective-permute-done.13.refs_6_ = bf16[336,128]{1,0:T(8,128)(2,1)S(1)} collective-permute-done((bf16[336,128]{1,0:T(8,128)(2,1)S(1)}, bf16[336,128]{1,0:T(8,128)(2,1)S(1)}, u32[]{:S(2)}, u32[]{:S(2)}) %collective-permute-start.13) | collective-permute-done | bytes 86048 | tf_op jit(solution)/shard_map/ppermute | solution.py:476
  32.3 0.2 collective-permute-done.14.refs_7_
  32.4 0.1 shard_map.121
  32.5 1.4 %collective-permute-start.15 = (bf16[256,128]{1,0:T(8,128)(2,1)S(1)}, bf16[256,128]{1,0:T(8,128)(2,1)S(1)}, u32[]{:S(2)}, u32[]{:S(2)}) collective-permute-start(bf16[256,128]{1,0:T(8,128)(2,1)S(1)} %get-tuple-element.46), channel_id=1, source_target_pairs={{0,2},{1,3},{2,0},{3,1},{4,6},{5,7},{6,4},{7,5},{8,10},{9,11},{10,... | collective-permute-start | bytes 196616 | tf_op jit(solution)/shard_map/ppermute | solution.py:476
  33.9 0.0 copy-done.3
  33.9 0.0 copy-done.4
  33.9 0.0 copy-done.6
  33.9 3.5 %shard_map.122 = (bf16[2,16,128,128]{3,2,1,0:T(8,128)(2,1)}, f32[4,128,128]{2,1,0:T(8,128)S(1)}, f32[8,128]{1,0:T(8,128)S(1)}, f32[80,128]{1,0:T(8,128)S(1)}) custom-call(s32[4,16]{1,0:T(4,128)S(4)} %get-tuple-element.29.links_ref, s32[16]{0:T(128)S(4)} %get-tuple-element.30.rows_ref, s32[16]{0:T(128)S(4)} %get-tuple-element.37.image_ref, ...), custom_call_target="tpu_custom_call" | custom-call | flops 1207959552 | bytes 2097152 | tf_op jit(solution)/shard_map/pallas_call | solution.py:514
  37.4 0.0 collective-permute-done.15.refs_1_
  37.4 0.9 %shard_map.123 = bf16[2,16,128,128]{3,2,1,0:T(8,128)(2,1)} custom-call(s32[4,16]{1,0:T(4,128)S(4)} %get-tuple-element.29.links_ref, s32[16]{0:T(128)S(4)} %get-tuple-element.30.rows_ref, bf16[256,128]{1,0:T(8,128)(2,1)S(1)} %get-tuple-element.45.refs_0_, bf16[256,128]{1,0:T(8,128)(2,1)S(1)} %collective-permute-done.15.refs_1_, ...), custom_call_target="tpu_custom_call", output_to_operand_aliasing={{}: (10, {})} | custom-call | tf_op jit(solution)/shard_map/pallas_call | solution.py:527
Async XLA Ops:
  0.0 14.8 %copy-start.7 = (bf16[3,3,128,128]{3,2,1,0:T(8,128)(2,1)S(1)}, bf16[3,3,128,128]{3,2,1,0:T(8,128)(2,1)}, u32[]{:S(2)}) copy-start(bf16[3,3,128,128]{3,2,1,0:T(8,128)(2,1)} %param.18) | copy-start | bytes 884740
  1.6 15.6 %copy-start = (bf16[2,16,128,128]{3,2,1,0:T(8,128)(2,1)S(1)}, bf16[2,16,128,128]{3,2,1,0:T(8,128)(2,1)}, u32[]{:S(2)}) copy-start(bf16[2,16,128,128]{3,2,1,0:T(8,128)(2,1)} %refs_14_.1) | copy-start | bytes 3145732
  1.6 15.6 %copy-start.1 = (f32[128]{0:T(128)S(1)}, f32[128]{0:T(128)}, u32[]{:S(2)}) copy-start(f32[128]{0:T(128)} %param.16) | copy-start | bytes 1540
  1.6 15.6 %copy-start.2 = (f32[128]{0:T(128)S(1)}, f32[128]{0:T(128)}, u32[]{:S(2)}) copy-start(f32[128]{0:T(128)} %param.17) | copy-start | bytes 1540
  1.6 15.5 %copy-start.5 = (f32[128]{0:T(128)S(1)}, f32[128]{0:T(128)}, u32[]{:S(2)}) copy-start(f32[128]{0:T(128)} %param.19) | copy-start | bytes 1540
  1.6 5.7 %collective-permute-start = (bf16[336,128]{1,0:T(8,128)(2,1)S(1)}, bf16[336,128]{1,0:T(8,128)(2,1)S(1)}, u32[]{:S(2)}, u32[]{:S(2)}) collective-permute-start(bf16[336,128]{1,0:T(8,128)(2,1)S(1)} %get-tuple-element.32), channel_id=1, source_target_pairs={{0,2},{1,3},{2,0},{3,1},{4,6},{5,7},{6,4},{7,5},{8,10},{9,11},{10,... | collective-permute-start | bytes 258056 | tf_op jit(solution)/shard_map/ppermute | solution.py:476
  4.7 9.5 %collective-permute-start.1 = (bf16[336,128]{1,0:T(8,128)(2,1)S(1)}, bf16[336,128]{1,0:T(8,128)(2,1)S(1)}, u32[]{:S(2)}, u32[]{:S(2)}) collective-permute-start(bf16[336,128]{1,0:T(8,128)(2,1)S(1)} %get-tuple-element.33), channel_id=1, source_target_pairs={{0,4},{1,5},{2,6},{3,7},{4,0},{5,1},{6,2},{7,3},{8,12},{9,13},{10,... | collective-permute-start | bytes 258056 | tf_op jit(solution)/shard_map/ppermute | solution.py:476
  7.3 6.9 %collective-permute-start.2 = (bf16[336,128]{1,0:T(8,128)(2,1)S(1)}, bf16[336,128]{1,0:T(8,128)(2,1)S(1)}, u32[]{:S(2)}, u32[]{:S(2)}) collective-permute-start(bf16[336,128]{1,0:T(8,128)(2,1)S(1)} %get-tuple-element.34), channel_id=1, source_target_pairs={{0,6},{1,7},{2,4},{3,5},{4,2},{5,3},{6,0},{7,1},{8,14},{9,15},{10,... | collective-permute-start | bytes 258056 | tf_op jit(solution)/shard_map/ppermute | solution.py:476
  7.3 7.5 %collective-permute-start.3 = (bf16[336,128]{1,0:T(8,128)(2,1)S(1)}, bf16[336,128]{1,0:T(8,128)(2,1)S(1)}, u32[]{:S(2)}, u32[]{:S(2)}) collective-permute-start(bf16[336,128]{1,0:T(8,128)(2,1)S(1)} %get-tuple-element.31.refs_0_), channel_id=1, source_target_pairs={{0,1},{1,0},{2,3},{3,2},{4,5},{5,4},{6,7},{7,6},{8,9},{9,8},{10,11... | collective-permute-start | bytes 258056 | tf_op jit(solution)/shard_map/ppermute | solution.py:476
  7.3 7.5 %collective-permute-start.4 = (bf16[336,128]{1,0:T(8,128)(2,1)S(1)}, bf16[336,128]{1,0:T(8,128)(2,1)S(1)}, u32[]{:S(2)}, u32[]{:S(2)}) collective-permute-start(bf16[336,128]{1,0:T(8,128)(2,1)S(1)} %collective-permute-done.refs_1_), channel_id=1, source_target_pairs={{0,1},{1,0},{2,3},{3,2},{4,5},{5,4},{6,7},{7,6},{8,9},{9,8},{10,11... | collective-permute-start | bytes 258056 | tf_op jit(solution)/shard_map/ppermute | solution.py:476
  14.2 1.3 %collective-permute-start.5 = (bf16[336,128]{1,0:T(8,128)(2,1)S(1)}, bf16[336,128]{1,0:T(8,128)(2,1)S(1)}, u32[]{:S(2)}, u32[]{:S(2)}) collective-permute-start(bf16[336,128]{1,0:T(8,128)(2,1)S(1)} %collective-permute-done.1.refs_2_), channel_id=1, source_target_pairs={{0,1},{1,0},{2,3},{3,2},{4,5},{5,4},{6,7},{7,6},{8,9},{9,8},{10,11... | collective-permute-start | bytes 258056 | tf_op jit(solution)/shard_map/ppermute | solution.py:476
  14.2 1.4 %collective-permute-start.6 = (bf16[336,128]{1,0:T(8,128)(2,1)S(1)}, bf16[336,128]{1,0:T(8,128)(2,1)S(1)}, u32[]{:S(2)}, u32[]{:S(2)}) collective-permute-start(bf16[336,128]{1,0:T(8,128)(2,1)S(1)} %collective-permute-done.2.refs_3_), channel_id=1, source_target_pairs={{0,1},{1,0},{2,3},{3,2},{4,5},{5,4},{6,7},{7,6},{8,9},{9,8},{10,11... | collective-permute-start | bytes 258056 | tf_op jit(solution)/shard_map/ppermute | solution.py:476
  15.8 4.4 %collective-permute-start.7 = (bf16[256,128]{1,0:T(8,128)(2,1)S(1)}, bf16[256,128]{1,0:T(8,128)(2,1)S(1)}, u32[]{:S(2)}, u32[]{:S(2)}) collective-permute-start(bf16[256,128]{1,0:T(8,128)(2,1)S(1)} %get-tuple-element.36), channel_id=1, source_target_pairs={{0,2},{1,3},{2,0},{3,1},{4,6},{5,7},{6,4},{7,5},{8,10},{9,11},{10,... | collective-permute-start | bytes 196616 | tf_op jit(solution)/shard_map/ppermute | solution.py:476
  20.1 11.5 %copy-start.8 = (bf16[3,3,128,128]{3,2,1,0:T(8,128)(2,1)S(1)}, bf16[3,3,128,128]{3,2,1,0:T(8,128)(2,1)}, u32[]{:S(2)}) copy-start(bf16[3,3,128,128]{3,2,1,0:T(8,128)(2,1)} %param.22) | copy-start | bytes 884740
  20.6 13.4 %copy-start.3 = (f32[128]{0:T(128)S(1)}, f32[128]{0:T(128)}, u32[]{:S(2)}) copy-start(f32[128]{0:T(128)} %param.20) | copy-start | bytes 1540
  20.6 13.4 %copy-start.4 = (f32[128]{0:T(128)S(1)}, f32[128]{0:T(128)}, u32[]{:S(2)}) copy-start(f32[128]{0:T(128)} %param.21) | copy-start | bytes 1540
  20.6 13.3 %copy-start.6 = (f32[128]{0:T(128)S(1)}, f32[128]{0:T(128)}, u32[]{:S(2)}) copy-start(f32[128]{0:T(128)} %param.23) | copy-start | bytes 1540
  20.6 5.4 %collective-permute-start.8 = (bf16[336,128]{1,0:T(8,128)(2,1)S(1)}, bf16[336,128]{1,0:T(8,128)(2,1)S(1)}, u32[]{:S(2)}, u32[]{:S(2)}) collective-permute-start(bf16[336,128]{1,0:T(8,128)(2,1)S(1)} %get-tuple-element.42), channel_id=1, source_target_pairs={{0,2},{1,3},{2,0},{3,1},{4,6},{5,7},{6,4},{7,5},{8,10},{9,11},{10,... | collective-permute-start | bytes 258056 | tf_op jit(solution)/shard_map/ppermute | solution.py:476
  21.9 9.1 %collective-permute-start.9 = (bf16[336,128]{1,0:T(8,128)(2,1)S(1)}, bf16[336,128]{1,0:T(8,128)(2,1)S(1)}, u32[]{:S(2)}, u32[]{:S(2)}) collective-permute-start(bf16[336,128]{1,0:T(8,128)(2,1)S(1)} %get-tuple-element.43), channel_id=1, source_target_pairs={{0,4},{1,5},{2,6},{3,7},{4,0},{5,1},{6,2},{7,3},{8,12},{9,13},{10,... | collective-permute-start | bytes 258056 | tf_op jit(solution)/shard_map/ppermute | solution.py:476
  23.7 7.3 %collective-permute-start.10 = (bf16[336,128]{1,0:T(8,128)(2,1)S(1)}, bf16[336,128]{1,0:T(8,128)(2,1)S(1)}, u32[]{:S(2)}, u32[]{:S(2)}) collective-permute-start(bf16[336,128]{1,0:T(8,128)(2,1)S(1)} %get-tuple-element.44), channel_id=1, source_target_pairs={{0,6},{1,7},{2,4},{3,5},{4,2},{5,3},{6,0},{7,1},{8,14},{9,15},{10,... | collective-permute-start | bytes 258056 | tf_op jit(solution)/shard_map/ppermute | solution.py:476
  25.0 6.6 %collective-permute-start.11 = (bf16[336,128]{1,0:T(8,128)(2,1)S(1)}, bf16[336,128]{1,0:T(8,128)(2,1)S(1)}, u32[]{:S(2)}, u32[]{:S(2)}) collective-permute-start(bf16[336,128]{1,0:T(8,128)(2,1)S(1)} %get-tuple-element.41.refs_0_), channel_id=1, source_target_pairs={{0,1},{1,0},{2,3},{3,2},{4,5},{5,4},{6,7},{7,6},{8,9},{9,8},{10,11... | collective-permute-start | bytes 258056 | tf_op jit(solution)/shard_map/ppermute | solution.py:476
  26.0 5.6 %collective-permute-start.12 = (bf16[336,128]{1,0:T(8,128)(2,1)S(1)}, bf16[336,128]{1,0:T(8,128)(2,1)S(1)}, u32[]{:S(2)}, u32[]{:S(2)}) collective-permute-start(bf16[336,128]{1,0:T(8,128)(2,1)S(1)} %collective-permute-done.8.refs_1_), channel_id=1, source_target_pairs={{0,1},{1,0},{2,3},{3,2},{4,5},{5,4},{6,7},{7,6},{8,9},{9,8},{10,11... | collective-permute-start | bytes 258056 | tf_op jit(solution)/shard_map/ppermute | solution.py:476
  31.0 1.3 %collective-permute-start.13 = (bf16[336,128]{1,0:T(8,128)(2,1)S(1)}, bf16[336,128]{1,0:T(8,128)(2,1)S(1)}, u32[]{:S(2)}, u32[]{:S(2)}) collective-permute-start(bf16[336,128]{1,0:T(8,128)(2,1)S(1)} %collective-permute-done.9.refs_2_), channel_id=1, source_target_pairs={{0,1},{1,0},{2,3},{3,2},{4,5},{5,4},{6,7},{7,6},{8,9},{9,8},{10,11... | collective-permute-start | bytes 258056 | tf_op jit(solution)/shard_map/ppermute | solution.py:476
  31.0 1.4 %collective-permute-start.14 = (bf16[336,128]{1,0:T(8,128)(2,1)S(1)}, bf16[336,128]{1,0:T(8,128)(2,1)S(1)}, u32[]{:S(2)}, u32[]{:S(2)}) collective-permute-start(bf16[336,128]{1,0:T(8,128)(2,1)S(1)} %collective-permute-done.10.refs_3_), channel_id=1, source_target_pairs={{0,1},{1,0},{2,3},{3,2},{4,5},{5,4},{6,7},{7,6},{8,9},{9,8},{10,11... | collective-permute-start | bytes 258056 | tf_op jit(solution)/shard_map/ppermute | solution.py:476
  32.5 4.9 %collective-permute-start.15 = (bf16[256,128]{1,0:T(8,128)(2,1)S(1)}, bf16[256,128]{1,0:T(8,128)(2,1)S(1)}, u32[]{:S(2)}, u32[]{:S(2)}) collective-permute-start(bf16[256,128]{1,0:T(8,128)(2,1)S(1)} %get-tuple-element.46), channel_id=1, source_target_pairs={{0,2},{1,3},{2,0},{3,1},{4,6},{5,7},{6,4},{7,5},{8,10},{9,11},{10,... | collective-permute-start | bytes 196616 | tf_op jit(solution)/shard_map/ppermute | solution.py:476

commit v3 on v2

--- a/solution.py
+++ b/solution.py
@@ -81,22 +81,24 @@
 
 
 def column_sums(values_of, rows, valid):
+    rows = list(rows)
+    first = values_of(rows[0])
+    pivot = jnp.sum(fold_rows(first), axis=0, keepdims=True) * (1.0 / first.shape[0])
     pixels = jnp.int32(0)
-    total = None
+    total = spread = None
     for row in rows:
-        values = values_of(row)
+        apart = values_of(row) - pivot
         inside = row < valid
-        pixels = pixels + jnp.where(inside, values.shape[0], 0)
-        part = jnp.where(inside, fold_rows(values), 0.0)
+        pixels = pixels + jnp.where(inside, apart.shape[0], 0)
+        part = jnp.where(inside, fold_rows(apart), 0.0)
+        square = jnp.where(inside, fold_rows(apart * apart), 0.0)
         total = part if total is None else total + part
+        spread = square if spread is None else spread + square
     total = jnp.sum(total, axis=0, keepdims=True)
-    mean = total / jnp.maximum(pixels, 1).astype(f32)
-    spread = None
-    for row in rows:
-        apart = values_of(row) - mean
-        part = jnp.where(row < valid, fold_rows(apart * apart), 0.0)
-        spread = part if spread is None else spread + part
-    return pixels.astype(f32), total, jnp.sum(spread, axis=0, keepdims=True)
+    spread = jnp.sum(spread, axis=0, keepdims=True)
+    pixels = pixels.astype(f32)
+    spread = jnp.maximum(spread - total * (total / jnp.maximum(pixels, 1.0)), 0.0)
+    return pixels, total + pixels * pivot, spread
 
 
 def merge_sums(one, two):
@@ -133,7 +135,7 @@
 
 
 def edges_kernel(plan, links_hbm, rows_hbm, image_hbm, x_hbm, links_ref, rows_ref, image_ref, *refs):
-    buf_refs, (x_ref, sems) = refs[: plan.targets], refs[plan.targets :]
+    x_ref, buf_refs, sems = refs[0], refs[1:-1], refs[-1]
     tables = [
         pltpu.make_async_copy(source, target, sems.at[plan.count + place])
         for place, (source, target) in enumerate(
@@ -143,8 +145,7 @@
     copies = [pltpu.make_async_copy(x_hbm.at[tile], x_ref.at[tile], sems.at[tile]) for tile in range(plan.count)]
     for copy in tables[:1] + copies + tables[1:]:
         copy.start()
-    for copy in tables:
-        copy.wait()
+    tables[0].wait()
     own_rows = own_values(plan, rows_ref)
     sums, spreads, columns = [], [], []
     for tile in range(plan.count):
@@ -160,6 +161,8 @@
         return x_ref[tile, edge * (plan.rows - 1), window, :]
 
     fill_buffers(plan, pack_stats(plan, sums, spreads), edge_of, columns, buf_refs)
+    for copy in tables[1:]:
+        copy.wait()
 
 
 def group_total(values, group_width):
@@ -293,8 +296,10 @@
     ends_ref = residual_ref = None
     if last:
         (ends_ref, residual_ref), refs = refs[:2], refs[2:]
-    out_ref, partial_ref, norm_ref, side_ref, held_ref, wide = refs[:6]
-    refs = refs[6:]
+    if last:
+        out_ref, partial_ref, norm_ref, side_ref, rest_ref, held_ref, wide, tiles_ref, sems = refs
+    else:
+        tiles_ref, partial_ref, norm_ref, side_ref, held_ref, wide = refs
     count, rows, cols, channels = plan.count, plan.rows, plan.cols, plan.channels
     held = Held(plan, bufs, held_ref, "rest")
     means, inverses = image_norms(plan, rows_ref, image_ref, held.held)
@@ -336,7 +341,7 @@
                 wide[tile, (row + 1) // 2, :, at : at + channels] = values
 
         pairs = rows // 2
-        step = 2 if pairs % 2 == 0 else 1
+        step = 1
         gathered = None
         for pair in range(0, pairs, step):
             upper = wide[tile, pair : pair + step].reshape(step * cols, 2 * depth)
@@ -353,15 +358,17 @@
                     partial_ref[2 * tile + (row > 0)] = part
                     continue
                 part = jnp.where(row < valid, part, 0.0).astype(bf16)
-                if last:
-                    refs[0][tile, row] = part
-                else:
-                    out_ref[tile, row] = part
+                if last and tile == count - 1:
+                    rest_ref[row - 1] = part
+                    continue
+                tiles_ref[tile, row] = part
                 inner[row] = part.astype(f32)
             if last:
+                if not inner:
+                    continue
                 band = pl.ds(min(inner), len(inner))
-                sem = refs[1].at[tile * pairs + pair]
-                copy = pltpu.make_async_copy(refs[0].at[tile, band], out_ref.at[tile, band], sem)
+                sem = sems.at[tile * pairs + pair]
+                copy = pltpu.make_async_copy(tiles_ref.at[tile, band], out_ref.at[tile, band], sem)
                 copy.start()
                 copies.append(copy)
             else:
@@ -371,7 +378,7 @@
             norm_ref[(2 * count + tile) : (2 * count + tile) + 1, :] = gathered[1]
             norm_ref[(3 * count + tile) : (3 * count + tile) + 1, :] = gathered[2]
             for side, column in enumerate((0, cols - 1)):
-                picked = [out_ref[tile, row, column : column + 1, :].astype(f32) for row in range(1, rows - 1)]
+                picked = [tiles_ref[tile, row, column : column + 1, :].astype(f32) for row in range(1, rows - 1)]
                 at = 8 * count + (2 * tile + side) * rows
                 side_ref[at + 1 : at + rows - 1, :] = jnp.concatenate(picked, axis=0)
     for copy in copies:
@@ -384,7 +391,7 @@
     refs = refs[6:]
     count, rows, cols, channels = plan.count, plan.rows, plan.cols, plan.channels
     if last:
-        _, out_ref, halo, ends_ref, sems = refs
+        rest_ref, _, out_ref, halo, ends_ref, sems = refs
     else:
         ends_ref, buf_refs, halo = refs[0], refs[1:-1], refs[-1]
     first = lax.axis_index(AXIS) * count
@@ -395,6 +402,10 @@
             halo[place, plan.window(k), :] = halo_refs[k][at : at + plan.width, :]
     depth = 3 * channels
     copies, sums, spreads, columns = [], [], [], []
+    if last:
+        target = out_ref.at[count - 1, pl.ds(1, rows - 2)]
+        copies.append(pltpu.make_async_copy(rest_ref, target, sems.at[2 * count]))
+        copies[-1].start()
     for tile in range(count):
         valid = own_rows[tile]
         activate = halves(
@@ -509,19 +520,19 @@
         halo = spread(send)
         weights = paired_weights(kernel)
         gain, shift, offset = gain[None], shift[None], offset[None]
-        operands = arrays + [source, gain, shift, offset, weights] + ([ends, feature_tiles] if last else [])
+        operands = arrays + [source, gain, shift, offset, weights] + ([ends, features] if last else [])
         flops = 2 * count * rows * cols * 9 * channels * channels
-        tiles, partial, norm, side = pl.pallas_call(
+        tiles, partial, norm, side, *rest = pl.pallas_call(
             functools.partial(middle_kernel, plan, last),
-            out_shape=[tiles_shape, partial_shape, norm_shape, side_shape],
+            out_shape=[tiles_shape, partial_shape, norm_shape, side_shape] + [shape((rows - 2, cols, channels), bf16)] * last,
             in_specs=[SMEM] * 3 + [VMEM] * len(operands),
-            out_specs=[HBM if last else VMEM] + [VMEM] * 3,
+            out_specs=[HBM if last else VMEM] + [VMEM] * (3 + last),
             scratch_shapes=[held_scratch(plan, "rest"), pltpu.VMEM((count, rows // 2 + 1, cols, 6 * channels), bf16)]
             + ([pltpu.VMEM(feature_tiles.shape, bf16), pltpu.SemaphoreType.DMA((count * rows // 2,))] if last else []),
             compiler_params=params,
             cost_estimate=pl.CostEstimate(flops=flops, bytes_accessed=4 * feature_tiles.size, transcendentals=0),
         )(*scalars, *operands)
-        operands = halo + [partial, norm, side, gain, shift, weights]
+        operands = halo + [partial, norm, side, gain, shift, weights] + rest
         scratch = [pltpu.VMEM((2 * count, cols, channels), bf16)]
         if last:
             return pl.pallas_call(
@@ -530,7 +541,7 @@
                 in_specs=[SMEM] * 2 + [VMEM] * len(operands) + [HBM],
                 out_specs=HBM,
                 input_output_aliases={2 + len(operands): 0},
-                scratch_shapes=scratch + scratch + [pltpu.SemaphoreType.DMA((2 * count,))],
+                scratch_shapes=scratch + scratch + [pltpu.SemaphoreType.DMA((2 * count + 1,))],
                 compiler_params=params,
             )(*scalars[:2], *operands, tiles)
         ends, *bufs = pl.pallas_call(
@@ -547,15 +558,15 @@
     inputs = [pltpu.with_memory_space_constraint(array, pltpu.HBM) for array in (*tables, feature_tiles)]
     found = pl.pallas_call(
         functools.partial(edges_kernel, plan),
-        out_shape=[pltpu.SMEM(table.shape, jnp.int32) for table in tables] + buf_shape,
+        out_shape=[pltpu.SMEM(table.shape, jnp.int32) for table in tables] + [tiles_shape] + buf_shape,
         in_specs=[HBM] * 4,
-        out_specs=[SMEM] * 3 + [VMEM] * plan.targets,
-        scratch_shapes=[pltpu.VMEM(feature_tiles.shape, bf16), pltpu.SemaphoreType.DMA((count + 3,))],
+        out_specs=[SMEM] * 3 + [VMEM] * (1 + plan.targets),
+        scratch_shapes=[pltpu.SemaphoreType.DMA((count + 3,))],
         compiler_params=params,
         name="edges",
     )(*inputs)
-    scalars, bufs = found[:3], found[3:]
-    hidden, ends, bufs = stage(False, feature_tiles, None, bufs, gain_one, shift_one, kernel_one, offset_one)
+    scalars, features, bufs = found[:3], found[3], found[4:]
+    hidden, ends, bufs = stage(False, features, None, bufs, gain_one, shift_one, kernel_one, offset_one)
     return stage(True, hidden, ends, bufs, gain_two, shift_two, kernel_two, offset_two)
 
 

time: 38.5 us -> 37.9 us (0.984)
  Pallas kernels: 9.37 us -> 8.63 us
    pallas_call x2, Pallas kernels: 6.35 us -> 5.52 us  [stage(): pl.pallas_call(functools.partial(middle_kernel, plan, last), out_shape=[t...]
  transfers between devices with their start and end apart: 16 -> 16, of which waited for: 8 -> 9; matrix products, arithmetic and copies ran while one was open for 0% -> 0% of each run, Pallas kernels for 17% -> 15%
where the time goes in v3:
time: 37.9 us; the launch traced here: 37.8 us
  starting transfers between devices  14.5 us (38%)
  waiting for transfers between devices  14.3 us (38%)
  Pallas kernels  8.63 us (23%)
    ppermute x16, starting transfers between devices, swap(): return lax.ppermute(array, AXIS, [(i, i ^ distance) for i in range(size)])  14.5 us
    ppermute x16, waiting for transfers between devices, swap(): return lax.ppermute(array, AXIS, [(i, i ^ distance) for i in range(size)])  14.3 us
    pallas_call x2, Pallas kernels, stage(): pl.pallas_call(functools.partial(middle_kernel, plan, last), out_shape=[t...  5.52 us
    pallas_call x1, Pallas kernels, shards(): pl.pallas_call(functools.partial(edges_kernel, plan), out_shape=[pltpu.SM...  1.67 us
    pallas_call x1, Pallas kernels, stage(): pl.pallas_call(functools.partial(ends_kernel, plan, last), out_shape=tile...  0.95 us
  transfers between devices with their start and end apart: 16, of which 9 were waited for; matrix products, arithmetic and copies ran while one was open for 0% of the time, Pallas kernels for 15%

profile of v3, /device:TPU:0, one launch (start us, length us, event | category | flops | bytes accessed | tf_op | source)
XLA Modules:
  0.0 37.8 jit_solution(4260896183309508025)
XLA Ops:
  0.0 0.0 copy-start.6
  0.0 1.7 %edges.1 = (s32[4,16]{1,0:T(4,128)S(4)}, s32[16]{0:T(128)S(4)}, s32[16]{0:T(128)S(4)}, bf16[2,16,128,128]{3,2,1,0:T(8,128)(2,1)S(1)}, bf16[336,128]{1,0:T(8,128)...) custom-call(s32[4,16]{1,0:T(4,128)} %bitcast.23, s32[16]{0:T(128)} %rows_hbm.1, ...), custom_call_target="tpu_custom_call" | custom-call | tf_op jit(solution)/shard_map/edges/pallas_call | solution.py:559
  1.7 0.0 copy-start
  1.7 0.0 copy-start.1
  1.7 0.0 copy-start.4
  1.7 3.1 %collective-permute-start = (bf16[336,128]{1,0:T(8,128)(2,1)S(1)}, bf16[336,128]{1,0:T(8,128)(2,1)S(1)}, u32[]{:S(2)}, u32[]{:S(2)}) collective-permute-start(bf16[336,128]{1,0:T(8,128)(2,1)S(1)} %get-tuple-element.34), channel_id=1, source_target_pairs={{0,2},{1,3},{2,0},{3,1},{4,6},{5,7},{6,4},{7,5},{8,10},{9,11},{10,... | collective-permute-start | bytes 258056 | tf_op jit(solution)/shard_map/ppermute | solution.py:487
  4.8 2.6 %collective-permute-start.1 = (bf16[336,128]{1,0:T(8,128)(2,1)S(1)}, bf16[336,128]{1,0:T(8,128)(2,1)S(1)}, u32[]{:S(2)}, u32[]{:S(2)}) collective-permute-start(bf16[336,128]{1,0:T(8,128)(2,1)S(1)} %get-tuple-element.35), channel_id=1, source_target_pairs={{0,4},{1,5},{2,6},{3,7},{4,0},{5,1},{6,2},{7,3},{8,12},{9,13},{10,... | collective-permute-start | bytes 258056 | tf_op jit(solution)/shard_map/ppermute | solution.py:487
  7.4 0.0 collective-permute-start.2
  7.4 0.0 collective-permute-start.3
  7.4 0.0 collective-permute-done.refs_1_
  7.4 0.5 %collective-permute-start.4 = (bf16[336,128]{1,0:T(8,128)(2,1)S(1)}, bf16[336,128]{1,0:T(8,128)(2,1)S(1)}, u32[]{:S(2)}, u32[]{:S(2)}) collective-permute-start(bf16[336,128]{1,0:T(8,128)(2,1)S(1)} %collective-permute-done.refs_1_), channel_id=1, source_target_pairs={{0,1},{1,0},{2,3},{3,2},{4,5},{5,4},{6,7},{7,6},{8,9},{9,8},{10,11... | collective-permute-start | bytes 258056 | tf_op jit(solution)/shard_map/ppermute | solution.py:487
  7.9 6.4 %collective-permute-done.1.refs_2_ = bf16[336,128]{1,0:T(8,128)(2,1)S(1)} collective-permute-done((bf16[336,128]{1,0:T(8,128)(2,1)S(1)}, bf16[336,128]{1,0:T(8,128)(2,1)S(1)}, u32[]{:S(2)}, u32[]{:S(2)}) %collective-permute-start.1) | collective-permute-done | bytes 86048 | tf_op jit(solution)/shard_map/ppermute | solution.py:487
  14.3 0.0 collective-permute-start.5
  14.3 0.0 collective-permute-done.2.refs_3_
  14.3 0.5 %collective-permute-start.6 = (bf16[336,128]{1,0:T(8,128)(2,1)S(1)}, bf16[336,128]{1,0:T(8,128)(2,1)S(1)}, u32[]{:S(2)}, u32[]{:S(2)}) collective-permute-start(bf16[336,128]{1,0:T(8,128)(2,1)S(1)} %collective-permute-done.2.refs_3_), channel_id=1, source_target_pairs={{0,1},{1,0},{2,3},{3,2},{4,5},{5,4},{6,7},{7,6},{8,9},{9,8},{10,11... | collective-permute-start | bytes 258056 | tf_op jit(solution)/shard_map/ppermute | solution.py:487
  14.8 0.0 copy-done.6
  14.8 0.1 fusion.4
  14.9 0.0 collective-permute-done.3.refs_4_
  14.9 0.0 collective-permute-done.4.refs_5_
  15.0 0.7 %collective-permute-done.5.refs_6_ = bf16[336,128]{1,0:T(8,128)(2,1)S(1)} collective-permute-done((bf16[336,128]{1,0:T(8,128)(2,1)S(1)}, bf16[336,128]{1,0:T(8,128)(2,1)S(1)}, u32[]{:S(2)}, u32[]{:S(2)}) %collective-permute-start.5) | collective-permute-done | bytes 86048 | tf_op jit(solution)/shard_map/ppermute | solution.py:487
  15.6 0.2 collective-permute-done.6.refs_7_
  15.8 0.1 shard_map.118
  15.8 1.4 %collective-permute-start.7 = (bf16[256,128]{1,0:T(8,128)(2,1)S(1)}, bf16[256,128]{1,0:T(8,128)(2,1)S(1)}, u32[]{:S(2)}, u32[]{:S(2)}) collective-permute-start(bf16[256,128]{1,0:T(8,128)(2,1)S(1)} %get-tuple-element.38), channel_id=1, source_target_pairs={{0,2},{1,3},{2,0},{3,1},{4,6},{5,7},{6,4},{7,5},{8,10},{9,11},{10,... | collective-permute-start | bytes 196616 | tf_op jit(solution)/shard_map/ppermute | solution.py:487
  17.2 0.0 copy-done
  17.2 0.0 copy-done.1
  17.2 0.0 copy-done.4
  17.2 2.7 %shard_map.119 = (bf16[2,16,128,128]{3,2,1,0:T(8,128)(2,1)S(1)}, f32[4,128,128]{2,1,0:T(8,128)S(1)}, f32[8,128]{1,0:T(8,128)S(1)}, f32[80,128]{1,0:T(8,128)S(1)}) custom-call(s32[4,16]{1,0:T(4,128)S(4)} %get-tuple-element.31.links_ref, s32[16]{0:T(128)S(4)} %get-tuple-element.32.rows_ref, s32[16]{0:T(128)S(4)} %get-tuple-element.39.image_ref, ...), custom_call_target="tpu_custom_call" | custom-call | flops 1207959552 | bytes 2097152 | tf_op jit(solution)/shard_map/pallas_call | solution.py:525
  20.0 0.0 copy-start.7
  20.0 0.3 collective-permute-done.7.refs_1_
  20.3 0.4 shard_map.120
  20.6 0.0 copy-start.2
  20.6 0.0 copy-start.3
  20.6 0.0 copy-start.5
  20.7 1.3 %collective-permute-start.8 = (bf16[336,128]{1,0:T(8,128)(2,1)S(1)}, bf16[336,128]{1,0:T(8,128)(2,1)S(1)}, u32[]{:S(2)}, u32[]{:S(2)}) collective-permute-start(bf16[336,128]{1,0:T(8,128)(2,1)S(1)} %get-tuple-element.45), channel_id=1, source_target_pairs={{0,2},{1,3},{2,0},{3,1},{4,6},{5,7},{6,4},{7,5},{8,10},{9,11},{10,... | collective-permute-start | bytes 258056 | tf_op jit(solution)/shard_map/ppermute | solution.py:487
  22.0 1.8 %collective-permute-start.9 = (bf16[336,128]{1,0:T(8,128)(2,1)S(1)}, bf16[336,128]{1,0:T(8,128)(2,1)S(1)}, u32[]{:S(2)}, u32[]{:S(2)}) collective-permute-start(bf16[336,128]{1,0:T(8,128)(2,1)S(1)} %get-tuple-element.46), channel_id=1, source_target_pairs={{0,4},{1,5},{2,6},{3,7},{4,0},{5,1},{6,2},{7,3},{8,12},{9,13},{10,... | collective-permute-start | bytes 258056 | tf_op jit(solution)/shard_map/ppermute | solution.py:487
  23.8 1.3 %collective-permute-start.10 = (bf16[336,128]{1,0:T(8,128)(2,1)S(1)}, bf16[336,128]{1,0:T(8,128)(2,1)S(1)}, u32[]{:S(2)}, u32[]{:S(2)}) collective-permute-start(bf16[336,128]{1,0:T(8,128)(2,1)S(1)} %get-tuple-element.47), channel_id=1, source_target_pairs={{0,6},{1,7},{2,4},{3,5},{4,2},{5,3},{6,0},{7,1},{8,14},{9,15},{10,... | collective-permute-start | bytes 258056 | tf_op jit(solution)/shard_map/ppermute | solution.py:487
  25.1 0.0 collective-permute-start.11
  25.1 0.9 %collective-permute-done.8.refs_1_ = bf16[336,128]{1,0:T(8,128)(2,1)S(1)} collective-permute-done((bf16[336,128]{1,0:T(8,128)(2,1)S(1)}, bf16[336,128]{1,0:T(8,128)(2,1)S(1)}, u32[]{:S(2)}, u32[]{:S(2)}) %collective-permute-start.8) | collective-permute-done | bytes 86048 | tf_op jit(solution)/shard_map/ppermute | solution.py:487
  26.1 0.0 collective-permute-start.12
  26.1 4.8 %collective-permute-done.9.refs_2_ = bf16[336,128]{1,0:T(8,128)(2,1)S(1)} collective-permute-done((bf16[336,128]{1,0:T(8,128)(2,1)S(1)}, bf16[336,128]{1,0:T(8,128)(2,1)S(1)}, u32[]{:S(2)}, u32[]{:S(2)}) %collective-permute-start.9) | collective-permute-done | bytes 86048 | tf_op jit(solution)/shard_map/ppermute | solution.py:487
  30.9 0.0 collective-permute-start.13
  30.9 0.0 collective-permute-done.10.refs_3_
  30.9 0.5 %collective-permute-start.14 = (bf16[336,128]{1,0:T(8,128)(2,1)S(1)}, bf16[336,128]{1,0:T(8,128)(2,1)S(1)}, u32[]{:S(2)}, u32[]{:S(2)}) collective-permute-start(bf16[336,128]{1,0:T(8,128)(2,1)S(1)} %collective-permute-done.10.refs_3_), channel_id=1, source_target_pairs={{0,1},{1,0},{2,3},{3,2},{4,5},{5,4},{6,7},{7,6},{8,9},{9,8},{10,11... | collective-permute-start | bytes 258056 | tf_op jit(solution)/shard_map/ppermute | solution.py:487
  31.4 0.0 copy-done.7
  31.4 0.1 fusion.5
  31.5 0.0 collective-permute-done.11.refs_4_
  31.5 0.0 collective-permute-done.12.refs_5_
  31.5 0.7 %collective-permute-done.13.refs_6_ = bf16[336,128]{1,0:T(8,128)(2,1)S(1)} collective-permute-done((bf16[336,128]{1,0:T(8,128)(2,1)S(1)}, bf16[336,128]{1,0:T(8,128)(2,1)S(1)}, u32[]{:S(2)}, u32[]{:S(2)}) %collective-permute-start.13) | collective-permute-done | bytes 86048 | tf_op jit(solution)/shard_map/ppermute | solution.py:487
  32.2 0.2 collective-permute-done.14.refs_7_
  32.3 0.1 shard_map.121
  32.4 1.4 %collective-permute-start.15 = (bf16[256,128]{1,0:T(8,128)(2,1)S(1)}, bf16[256,128]{1,0:T(8,128)(2,1)S(1)}, u32[]{:S(2)}, u32[]{:S(2)}) collective-permute-start(bf16[256,128]{1,0:T(8,128)(2,1)S(1)} %get-tuple-element.49), channel_id=1, source_target_pairs={{0,2},{1,3},{2,0},{3,1},{4,6},{5,7},{6,4},{7,5},{8,10},{9,11},{10,... | collective-permute-start | bytes 196616 | tf_op jit(solution)/shard_map/ppermute | solution.py:487
  33.8 0.0 copy-done.2
  33.8 0.0 copy-done.3
  33.8 0.0 copy-done.5
  33.8 2.8 %shard_map.122 = (bf16[2,16,128,128]{3,2,1,0:T(8,128)(2,1)}, f32[4,128,128]{2,1,0:T(8,128)S(1)}, f32[8,128]{1,0:T(8,128)S(1)}, f32[80,128]{1,0:T(8,128)S(1)}, bf16[14,128,128]{2,1,0:T(8,128)(2,1)S(1)}) custom-call(s32[4,16]{1,0:T(4,128)S(4)} %get-tuple-element.31.links_ref, s32[16]{0:T(128)S(4)} %get-tuple-element.32.rows_ref, ...), custom_call_target="tpu_custom_call" | custom-call | flops 1207959552 | bytes 2097152 | tf_op jit(solution)/shard_map/pallas_call | solution.py:525
  36.6 0.2 collective-permute-done.15.refs_1_
  36.8 0.9 %shard_map.123 = bf16[2,16,128,128]{3,2,1,0:T(8,128)(2,1)} custom-call(s32[4,16]{1,0:T(4,128)S(4)} %get-tuple-element.31.links_ref, s32[16]{0:T(128)S(4)} %get-tuple-element.32.rows_ref, bf16[256,128]{1,0:T(8,128)(2,1)S(1)} %get-tuple-element.48.refs_0_, bf16[256,128]{1,0:T(8,128)(2,1)S(1)} %collective-permute-done.15.refs_1_, ...), custom_call_target="tpu_custom_call", output_to_operand_aliasing={{}: (11, {})} | custom-call | tf_op jit(solution)/shard_map/pallas_call | solution.py:538
Async XLA Ops:
  0.0 14.8 %copy-start.6 = (bf16[3,3,128,128]{3,2,1,0:T(8,128)(2,1)S(1)}, bf16[3,3,128,128]{3,2,1,0:T(8,128)(2,1)}, u32[]{:S(2)}) copy-start(bf16[3,3,128,128]{3,2,1,0:T(8,128)(2,1)} %param.18) | copy-start | bytes 884740
  1.7 15.6 %copy-start = (f32[128]{0:T(128)S(1)}, f32[128]{0:T(128)}, u32[]{:S(2)}) copy-start(f32[128]{0:T(128)} %param.16) | copy-start | bytes 1540
  1.7 15.6 %copy-start.1 = (f32[128]{0:T(128)S(1)}, f32[128]{0:T(128)}, u32[]{:S(2)}) copy-start(f32[128]{0:T(128)} %param.17) | copy-start | bytes 1540
  1.7 15.5 %copy-start.4 = (f32[128]{0:T(128)S(1)}, f32[128]{0:T(128)}, u32[]{:S(2)}) copy-start(f32[128]{0:T(128)} %param.19) | copy-start | bytes 1540
  1.7 5.7 %collective-permute-start = (bf16[336,128]{1,0:T(8,128)(2,1)S(1)}, bf16[336,128]{1,0:T(8,128)(2,1)S(1)}, u32[]{:S(2)}, u32[]{:S(2)}) collective-permute-start(bf16[336,128]{1,0:T(8,128)(2,1)S(1)} %get-tuple-element.34), channel_id=1, source_target_pairs={{0,2},{1,3},{2,0},{3,1},{4,6},{5,7},{6,4},{7,5},{8,10},{9,11},{10,... | collective-permute-start | bytes 258056 | tf_op jit(solution)/shard_map/ppermute | solution.py:487
  4.8 9.5 %collective-permute-start.1 = (bf16[336,128]{1,0:T(8,128)(2,1)S(1)}, bf16[336,128]{1,0:T(8,128)(2,1)S(1)}, u32[]{:S(2)}, u32[]{:S(2)}) collective-permute-start(bf16[336,128]{1,0:T(8,128)(2,1)S(1)} %get-tuple-element.35), channel_id=1, source_target_pairs={{0,4},{1,5},{2,6},{3,7},{4,0},{5,1},{6,2},{7,3},{8,12},{9,13},{10,... | collective-permute-start | bytes 258056 | tf_op jit(solution)/shard_map/ppermute | solution.py:487
  7.4 6.9 %collective-permute-start.2 = (bf16[336,128]{1,0:T(8,128)(2,1)S(1)}, bf16[336,128]{1,0:T(8,128)(2,1)S(1)}, u32[]{:S(2)}, u32[]{:S(2)}) collective-permute-start(bf16[336,128]{1,0:T(8,128)(2,1)S(1)} %get-tuple-element.36), channel_id=1, source_target_pairs={{0,6},{1,7},{2,4},{3,5},{4,2},{5,3},{6,0},{7,1},{8,14},{9,15},{10,... | collective-permute-start | bytes 258056 | tf_op jit(solution)/shard_map/ppermute | solution.py:487
  7.4 7.5 %collective-permute-start.3 = (bf16[336,128]{1,0:T(8,128)(2,1)S(1)}, bf16[336,128]{1,0:T(8,128)(2,1)S(1)}, u32[]{:S(2)}, u32[]{:S(2)}) collective-permute-start(bf16[336,128]{1,0:T(8,128)(2,1)S(1)} %get-tuple-element.33.refs_0_), channel_id=1, source_target_pairs={{0,1},{1,0},{2,3},{3,2},{4,5},{5,4},{6,7},{7,6},{8,9},{9,8},{10,11... | collective-permute-start | bytes 258056 | tf_op jit(solution)/shard_map/ppermute | solution.py:487
  7.4 7.5 %collective-permute-start.4 = (bf16[336,128]{1,0:T(8,128)(2,1)S(1)}, bf16[336,128]{1,0:T(8,128)(2,1)S(1)}, u32[]{:S(2)}, u32[]{:S(2)}) collective-permute-start(bf16[336,128]{1,0:T(8,128)(2,1)S(1)} %collective-permute-done.refs_1_), channel_id=1, source_target_pairs={{0,1},{1,0},{2,3},{3,2},{4,5},{5,4},{6,7},{7,6},{8,9},{9,8},{10,11... | collective-permute-start | bytes 258056 | tf_op jit(solution)/shard_map/ppermute | solution.py:487
  14.3 1.3 %collective-permute-start.5 = (bf16[336,128]{1,0:T(8,128)(2,1)S(1)}, bf16[336,128]{1,0:T(8,128)(2,1)S(1)}, u32[]{:S(2)}, u32[]{:S(2)}) collective-permute-start(bf16[336,128]{1,0:T(8,128)(2,1)S(1)} %collective-permute-done.1.refs_2_), channel_id=1, source_target_pairs={{0,1},{1,0},{2,3},{3,2},{4,5},{5,4},{6,7},{7,6},{8,9},{9,8},{10,11... | collective-permute-start | bytes 258056 | tf_op jit(solution)/shard_map/ppermute | solution.py:487
  14.3 1.4 %collective-permute-start.6 = (bf16[336,128]{1,0:T(8,128)(2,1)S(1)}, bf16[336,128]{1,0:T(8,128)(2,1)S(1)}, u32[]{:S(2)}, u32[]{:S(2)}) collective-permute-start(bf16[336,128]{1,0:T(8,128)(2,1)S(1)} %collective-permute-done.2.refs_3_), channel_id=1, source_target_pairs={{0,1},{1,0},{2,3},{3,2},{4,5},{5,4},{6,7},{7,6},{8,9},{9,8},{10,11... | collective-permute-start | bytes 258056 | tf_op jit(solution)/shard_map/ppermute | solution.py:487
  15.8 4.4 %collective-permute-start.7 = (bf16[256,128]{1,0:T(8,128)(2,1)S(1)}, bf16[256,128]{1,0:T(8,128)(2,1)S(1)}, u32[]{:S(2)}, u32[]{:S(2)}) collective-permute-start(bf16[256,128]{1,0:T(8,128)(2,1)S(1)} %get-tuple-element.38), channel_id=1, source_target_pairs={{0,2},{1,3},{2,0},{3,1},{4,6},{5,7},{6,4},{7,5},{8,10},{9,11},{10,... | collective-permute-start | bytes 196616 | tf_op jit(solution)/shard_map/ppermute | solution.py:487
  20.0 11.4 %copy-start.7 = (bf16[3,3,128,128]{3,2,1,0:T(8,128)(2,1)S(1)}, bf16[3,3,128,128]{3,2,1,0:T(8,128)(2,1)}, u32[]{:S(2)}) copy-start(bf16[3,3,128,128]{3,2,1,0:T(8,128)(2,1)} %param.22) | copy-start | bytes 884740
  20.6 13.2 %copy-start.2 = (f32[128]{0:T(128)S(1)}, f32[128]{0:T(128)}, u32[]{:S(2)}) copy-start(f32[128]{0:T(128)} %param.20) | copy-start | bytes 1540
  20.6 13.2 %copy-start.3 = (f32[128]{0:T(128)S(1)}, f32[128]{0:T(128)}, u32[]{:S(2)}) copy-start(f32[128]{0:T(128)} %param.21) | copy-start | bytes 1540
  20.6 13.2 %copy-start.5 = (f32[128]{0:T(128)S(1)}, f32[128]{0:T(128)}, u32[]{:S(2)}) copy-start(f32[128]{0:T(128)} %param.23) | copy-start | bytes 1540
  20.7 5.4 %collective-permute-start.8 = (bf16[336,128]{1,0:T(8,128)(2,1)S(1)}, bf16[336,128]{1,0:T(8,128)(2,1)S(1)}, u32[]{:S(2)}, u32[]{:S(2)}) collective-permute-start(bf16[336,128]{1,0:T(8,128)(2,1)S(1)} %get-tuple-element.45), channel_id=1, source_target_pairs={{0,2},{1,3},{2,0},{3,1},{4,6},{5,7},{6,4},{7,5},{8,10},{9,11},{10,... | collective-permute-start | bytes 258056 | tf_op jit(solution)/shard_map/ppermute | solution.py:487
  22.0 8.9 %collective-permute-start.9 = (bf16[336,128]{1,0:T(8,128)(2,1)S(1)}, bf16[336,128]{1,0:T(8,128)(2,1)S(1)}, u32[]{:S(2)}, u32[]{:S(2)}) collective-permute-start(bf16[336,128]{1,0:T(8,128)(2,1)S(1)} %get-tuple-element.46), channel_id=1, source_target_pairs={{0,4},{1,5},{2,6},{3,7},{4,0},{5,1},{6,2},{7,3},{8,12},{9,13},{10,... | collective-permute-start | bytes 258056 | tf_op jit(solution)/shard_map/ppermute | solution.py:487
  23.8 7.1 %collective-permute-start.10 = (bf16[336,128]{1,0:T(8,128)(2,1)S(1)}, bf16[336,128]{1,0:T(8,128)(2,1)S(1)}, u32[]{:S(2)}, u32[]{:S(2)}) collective-permute-start(bf16[336,128]{1,0:T(8,128)(2,1)S(1)} %get-tuple-element.47), channel_id=1, source_target_pairs={{0,6},{1,7},{2,4},{3,5},{4,2},{5,3},{6,0},{7,1},{8,14},{9,15},{10,... | collective-permute-start | bytes 258056 | tf_op jit(solution)/shard_map/ppermute | solution.py:487
  25.1 6.4 %collective-permute-start.11 = (bf16[336,128]{1,0:T(8,128)(2,1)S(1)}, bf16[336,128]{1,0:T(8,128)(2,1)S(1)}, u32[]{:S(2)}, u32[]{:S(2)}) collective-permute-start(bf16[336,128]{1,0:T(8,128)(2,1)S(1)} %get-tuple-element.44.refs_0_), channel_id=1, source_target_pairs={{0,1},{1,0},{2,3},{3,2},{4,5},{5,4},{6,7},{7,6},{8,9},{9,8},{10,11... | collective-permute-start | bytes 258056 | tf_op jit(solution)/shard_map/ppermute | solution.py:487
  26.1 5.5 %collective-permute-start.12 = (bf16[336,128]{1,0:T(8,128)(2,1)S(1)}, bf16[336,128]{1,0:T(8,128)(2,1)S(1)}, u32[]{:S(2)}, u32[]{:S(2)}) collective-permute-start(bf16[336,128]{1,0:T(8,128)(2,1)S(1)} %collective-permute-done.8.refs_1_), channel_id=1, source_target_pairs={{0,1},{1,0},{2,3},{3,2},{4,5},{5,4},{6,7},{7,6},{8,9},{9,8},{10,11... | collective-permute-start | bytes 258056 | tf_op jit(solution)/shard_map/ppermute | solution.py:487
  30.9 1.3 %collective-permute-start.13 = (bf16[336,128]{1,0:T(8,128)(2,1)S(1)}, bf16[336,128]{1,0:T(8,128)(2,1)S(1)}, u32[]{:S(2)}, u32[]{:S(2)}) collective-permute-start(bf16[336,128]{1,0:T(8,128)(2,1)S(1)} %collective-permute-done.9.refs_2_), channel_id=1, source_target_pairs={{0,1},{1,0},{2,3},{3,2},{4,5},{5,4},{6,7},{7,6},{8,9},{9,8},{10,11... | collective-permute-start | bytes 258056 | tf_op jit(solution)/shard_map/ppermute | solution.py:487
  30.9 1.4 %collective-permute-start.14 = (bf16[336,128]{1,0:T(8,128)(2,1)S(1)}, bf16[336,128]{1,0:T(8,128)(2,1)S(1)}, u32[]{:S(2)}, u32[]{:S(2)}) collective-permute-start(bf16[336,128]{1,0:T(8,128)(2,1)S(1)} %collective-permute-done.10.refs_3_), channel_id=1, source_target_pairs={{0,1},{1,0},{2,3},{3,2},{4,5},{5,4},{6,7},{7,6},{8,9},{9,8},{10,11... | collective-permute-start | bytes 258056 | tf_op jit(solution)/shard_map/ppermute | solution.py:487
  32.4 4.4 %collective-permute-start.15 = (bf16[256,128]{1,0:T(8,128)(2,1)S(1)}, bf16[256,128]{1,0:T(8,128)(2,1)S(1)}, u32[]{:S(2)}, u32[]{:S(2)}) collective-permute-start(bf16[256,128]{1,0:T(8,128)(2,1)S(1)} %get-tuple-element.49), channel_id=1, source_target_pairs={{0,2},{1,3},{2,0},{3,1},{4,6},{5,7},{6,4},{7,5},{8,10},{9,11},{10,... | collective-permute-start | bytes 196616 | tf_op jit(solution)/shard_map/ppermute | solution.py:487

commit v4 on v3

--- a/solution.py
+++ b/solution.py
@@ -80,18 +80,25 @@
     return values.reshape(-1, 8, values.shape[-1]).sum(axis=0)
 
 
-def column_sums(values_of, rows, valid):
-    rows = list(rows)
-    first = values_of(rows[0])
-    pivot = jnp.sum(fold_rows(first), axis=0, keepdims=True) * (1.0 / first.shape[0])
+def mean_of(values):
+    return jnp.sum(fold_rows(values), axis=0, keepdims=True) * (1.0 / values.shape[0])
+
+
+def row_sums(values_of, rows, pivot):
+    found = []
+    for row in rows:
+        apart = values_of(row) - pivot
+        found.append((row, fold_rows(apart), fold_rows(apart * apart)))
+    return found
+
+
+def masked_sums(width, pivot, found, valid):
     pixels = jnp.int32(0)
     total = spread = None
-    for row in rows:
-        apart = values_of(row) - pivot
+    for row, part, square in found:
         inside = row < valid
-        pixels = pixels + jnp.where(inside, apart.shape[0], 0)
-        part = jnp.where(inside, fold_rows(apart), 0.0)
-        square = jnp.where(inside, fold_rows(apart * apart), 0.0)
+        pixels = pixels + jnp.where(inside, width, 0)
+        part, square = jnp.where(inside, part, 0.0), jnp.where(inside, square, 0.0)
         total = part if total is None else total + part
         spread = square if spread is None else spread + square
     total = jnp.sum(total, axis=0, keepdims=True)
@@ -99,6 +106,13 @@
     pixels = pixels.astype(f32)
     spread = jnp.maximum(spread - total * (total / jnp.maximum(pixels, 1.0)), 0.0)
     return pixels, total + pixels * pivot, spread
+
+
+def column_sums(values_of, rows, valid):
+    rows = list(rows)
+    first = values_of(rows[0])
+    pivot = mean_of(first)
+    return masked_sums(first.shape[0], pivot, row_sums(values_of, rows, pivot), valid)
 
 
 def merge_sums(one, two):
@@ -137,25 +151,41 @@
 def edges_kernel(plan, links_hbm, rows_hbm, image_hbm, x_hbm, links_ref, rows_ref, image_ref, *refs):
     x_ref, buf_refs, sems = refs[0], refs[1:-1], refs[-1]
     tables = [
-        pltpu.make_async_copy(source, target, sems.at[plan.count + place])
+        pltpu.make_async_copy(source, target, sems.at[place])
         for place, (source, target) in enumerate(
             ((rows_hbm, rows_ref), (links_hbm, links_ref), (image_hbm, image_ref))
         )
     ]
-    copies = [pltpu.make_async_copy(x_hbm.at[tile], x_ref.at[tile], sems.at[tile]) for tile in range(plan.count)]
-    for copy in tables[:1] + copies + tables[1:]:
+    bands = 4
+    height = plan.rows // bands
+    copies = {}
+    for tile in range(plan.count):
+        for band in range(bands):
+            window = pl.ds(band * height, height)
+            sem = sems.at[3 + tile * bands + band]
+            copies[tile, band] = pltpu.make_async_copy(x_hbm.at[tile, window], x_ref.at[tile, window], sem)
+    for copy in [tables[0], *copies.values(), *tables[1:]]:
         copy.start()
-    tables[0].wait()
-    own_rows = own_values(plan, rows_ref)
-    sums, spreads, columns = [], [], []
+    found, columns = [], []
     for tile in range(plan.count):
-        copies[tile].wait()
-        _, total, spread = column_sums(lambda row: x_ref[tile, row].astype(f32), range(plan.rows), own_rows[tile])
-        sums.append(total)
-        spreads.append(spread)
+        pieces = []
+        for band in range(bands):
+            copies[tile, band].wait()
+            rows = range(band * height, (band + 1) * height)
+            if band == 0:
+                pivot = mean_of(x_ref[tile, 0].astype(f32))
+            pieces += row_sums(lambda row: x_ref[tile, row].astype(f32), rows, pivot)
+        found.append((plan.cols, pivot, pieces))
         for column in (0, plan.cols - 1):
             picked = [x_ref[tile, row, column : column + 1, :].astype(f32) for row in range(plan.rows)]
             columns.append(jnp.concatenate(picked, axis=0).astype(bf16))
+    tables[0].wait()
+    own_rows = own_values(plan, rows_ref)
+    sums, spreads = [], []
+    for tile in range(plan.count):
+        _, total, spread = masked_sums(*found[tile], own_rows[tile])
+        sums.append(total)
+        spreads.append(spread)
 
     def edge_of(tile, edge, window):
         return x_ref[tile, edge * (plan.rows - 1), window, :]
@@ -561,7 +591,7 @@
         out_shape=[pltpu.SMEM(table.shape, jnp.int32) for table in tables] + [tiles_shape] + buf_shape,
         in_specs=[HBM] * 4,
         out_specs=[SMEM] * 3 + [VMEM] * (1 + plan.targets),
-        scratch_shapes=[pltpu.SemaphoreType.DMA((count + 3,))],
+        scratch_shapes=[pltpu.SemaphoreType.DMA((3 + 4 * count,))],
         compiler_params=params,
         name="edges",
     )(*inputs)

time: 37.9 us -> 37.9 us (level)
  no operation moved by 1% of the time
where the time goes in v4:
time: 37.9 us; the launch traced here: 37.8 us
  starting transfers between devices  14.5 us (38%)
  waiting for transfers between devices  14.3 us (38%)
  Pallas kernels  8.6 us (23%)
    ppermute x16, starting transfers between devices, swap(): return lax.ppermute(array, AXIS, [(i, i ^ distance) for i in range(size)])  14.5 us
    ppermute x16, waiting for transfers between devices, swap(): return lax.ppermute(array, AXIS, [(i, i ^ distance) for i in range(size)])  14.3 us
    pallas_call x2, Pallas kernels, stage(): pl.pallas_call(functools.partial(middle_kernel, plan, last), out_shape=[t...  5.52 us
    pallas_call x1, Pallas kernels, shards(): pl.pallas_call(functools.partial(edges_kernel, plan), out_shape=[pltpu.SM...  1.64 us
    pallas_call x1, Pallas kernels, stage(): pl.pallas_call(functools.partial(ends_kernel, plan, last), out_shape=tile...  0.95 us
  transfers between devices with their start and end apart: 16, of which 9 were waited for; matrix products, arithmetic and copies ran while one was open for 0% of the time, Pallas kernels for 15%

profile of v4, /device:TPU:0, one launch (start us, length us, event | category | flops | bytes accessed | tf_op | source)
XLA Modules:
  0.0 37.8 jit_solution(15921263305888029643)
XLA Ops:
  0.0 0.0 copy-start.6
  0.0 1.6 %edges.1 = (s32[4,16]{1,0:T(4,128)S(4)}, s32[16]{0:T(128)S(4)}, s32[16]{0:T(128)S(4)}, bf16[2,16,128,128]{3,2,1,0:T(8,128)(2,1)S(1)}, bf16[336,128]{1,0:T(8,128)...) custom-call(s32[4,16]{1,0:T(4,128)} %bitcast.23, s32[16]{0:T(128)} %rows_hbm.1, ...), custom_call_target="tpu_custom_call" | custom-call | tf_op jit(solution)/shard_map/edges/pallas_call | solution.py:589
  1.7 0.0 copy-start
  1.7 0.0 copy-start.1
  1.7 0.0 copy-start.4
  1.7 3.1 %collective-permute-start = (bf16[336,128]{1,0:T(8,128)(2,1)S(1)}, bf16[336,128]{1,0:T(8,128)(2,1)S(1)}, u32[]{:S(2)}, u32[]{:S(2)}) collective-permute-start(bf16[336,128]{1,0:T(8,128)(2,1)S(1)} %get-tuple-element.34), channel_id=1, source_target_pairs={{0,2},{1,3},{2,0},{3,1},{4,6},{5,7},{6,4},{7,5},{8,10},{9,11},{10,... | collective-permute-start | bytes 258056 | tf_op jit(solution)/shard_map/ppermute | solution.py:517
  4.8 2.6 %collective-permute-start.1 = (bf16[336,128]{1,0:T(8,128)(2,1)S(1)}, bf16[336,128]{1,0:T(8,128)(2,1)S(1)}, u32[]{:S(2)}, u32[]{:S(2)}) collective-permute-start(bf16[336,128]{1,0:T(8,128)(2,1)S(1)} %get-tuple-element.35), channel_id=1, source_target_pairs={{0,4},{1,5},{2,6},{3,7},{4,0},{5,1},{6,2},{7,3},{8,12},{9,13},{10,... | collective-permute-start | bytes 258056 | tf_op jit(solution)/shard_map/ppermute | solution.py:517
  7.4 0.0 collective-permute-start.2
  7.4 0.0 collective-permute-start.3
  7.4 0.0 collective-permute-done.refs_1_
  7.4 0.5 %collective-permute-start.4 = (bf16[336,128]{1,0:T(8,128)(2,1)S(1)}, bf16[336,128]{1,0:T(8,128)(2,1)S(1)}, u32[]{:S(2)}, u32[]{:S(2)}) collective-permute-start(bf16[336,128]{1,0:T(8,128)(2,1)S(1)} %collective-permute-done.refs_1_), channel_id=1, source_target_pairs={{0,1},{1,0},{2,3},{3,2},{4,5},{5,4},{6,7},{7,6},{8,9},{9,8},{10,11... | collective-permute-start | bytes 258056 | tf_op jit(solution)/shard_map/ppermute | solution.py:517
  7.9 6.4 %collective-permute-done.1.refs_2_ = bf16[336,128]{1,0:T(8,128)(2,1)S(1)} collective-permute-done((bf16[336,128]{1,0:T(8,128)(2,1)S(1)}, bf16[336,128]{1,0:T(8,128)(2,1)S(1)}, u32[]{:S(2)}, u32[]{:S(2)}) %collective-permute-start.1) | collective-permute-done | bytes 86048 | tf_op jit(solution)/shard_map/ppermute | solution.py:517
  14.3 0.0 collective-permute-start.5
  14.3 0.0 collective-permute-done.2.refs_3_
  14.3 0.5 %collective-permute-start.6 = (bf16[336,128]{1,0:T(8,128)(2,1)S(1)}, bf16[336,128]{1,0:T(8,128)(2,1)S(1)}, u32[]{:S(2)}, u32[]{:S(2)}) collective-permute-start(bf16[336,128]{1,0:T(8,128)(2,1)S(1)} %collective-permute-done.2.refs_3_), channel_id=1, source_target_pairs={{0,1},{1,0},{2,3},{3,2},{4,5},{5,4},{6,7},{7,6},{8,9},{9,8},{10,11... | collective-permute-start | bytes 258056 | tf_op jit(solution)/shard_map/ppermute | solution.py:517
  14.8 0.0 copy-done.6
  14.8 0.1 fusion.4
  14.9 0.0 collective-permute-done.3.refs_4_
  14.9 0.0 collective-permute-done.4.refs_5_
  14.9 0.7 %collective-permute-done.5.refs_6_ = bf16[336,128]{1,0:T(8,128)(2,1)S(1)} collective-permute-done((bf16[336,128]{1,0:T(8,128)(2,1)S(1)}, bf16[336,128]{1,0:T(8,128)(2,1)S(1)}, u32[]{:S(2)}, u32[]{:S(2)}) %collective-permute-start.5) | collective-permute-done | bytes 86048 | tf_op jit(solution)/shard_map/ppermute | solution.py:517
  15.6 0.2 collective-permute-done.6.refs_7_
  15.7 0.1 shard_map.118
  15.8 1.4 %collective-permute-start.7 = (bf16[256,128]{1,0:T(8,128)(2,1)S(1)}, bf16[256,128]{1,0:T(8,128)(2,1)S(1)}, u32[]{:S(2)}, u32[]{:S(2)}) collective-permute-start(bf16[256,128]{1,0:T(8,128)(2,1)S(1)} %get-tuple-element.38), channel_id=1, source_target_pairs={{0,2},{1,3},{2,0},{3,1},{4,6},{5,7},{6,4},{7,5},{8,10},{9,11},{10,... | collective-permute-start | bytes 196616 | tf_op jit(solution)/shard_map/ppermute | solution.py:517
  17.2 0.0 copy-done
  17.2 0.0 copy-done.1
  17.2 0.0 copy-done.4
  17.2 2.7 %shard_map.119 = (bf16[2,16,128,128]{3,2,1,0:T(8,128)(2,1)S(1)}, f32[4,128,128]{2,1,0:T(8,128)S(1)}, f32[8,128]{1,0:T(8,128)S(1)}, f32[80,128]{1,0:T(8,128)S(1)}) custom-call(s32[4,16]{1,0:T(4,128)S(4)} %get-tuple-element.31.links_ref, s32[16]{0:T(128)S(4)} %get-tuple-element.32.rows_ref, s32[16]{0:T(128)S(4)} %get-tuple-element.39.image_ref, ...), custom_call_target="tpu_custom_call" | custom-call | flops 1207959552 | bytes 2097152 | tf_op jit(solution)/shard_map/pallas_call | solution.py:555
  20.0 0.0 copy-start.7
  20.0 0.3 collective-permute-done.7.refs_1_
  20.2 0.4 shard_map.120
  20.6 0.0 copy-start.2
  20.6 0.0 copy-start.3
  20.6 0.0 copy-start.5
  20.6 1.3 %collective-permute-start.8 = (bf16[336,128]{1,0:T(8,128)(2,1)S(1)}, bf16[336,128]{1,0:T(8,128)(2,1)S(1)}, u32[]{:S(2)}, u32[]{:S(2)}) collective-permute-start(bf16[336,128]{1,0:T(8,128)(2,1)S(1)} %get-tuple-element.45), channel_id=1, source_target_pairs={{0,2},{1,3},{2,0},{3,1},{4,6},{5,7},{6,4},{7,5},{8,10},{9,11},{10,... | collective-permute-start | bytes 258056 | tf_op jit(solution)/shard_map/ppermute | solution.py:517
  21.9 1.8 %collective-permute-start.9 = (bf16[336,128]{1,0:T(8,128)(2,1)S(1)}, bf16[336,128]{1,0:T(8,128)(2,1)S(1)}, u32[]{:S(2)}, u32[]{:S(2)}) collective-permute-start(bf16[336,128]{1,0:T(8,128)(2,1)S(1)} %get-tuple-element.46), channel_id=1, source_target_pairs={{0,4},{1,5},{2,6},{3,7},{4,0},{5,1},{6,2},{7,3},{8,12},{9,13},{10,... | collective-permute-start | bytes 258056 | tf_op jit(solution)/shard_map/ppermute | solution.py:517
  23.7 1.3 %collective-permute-start.10 = (bf16[336,128]{1,0:T(8,128)(2,1)S(1)}, bf16[336,128]{1,0:T(8,128)(2,1)S(1)}, u32[]{:S(2)}, u32[]{:S(2)}) collective-permute-start(bf16[336,128]{1,0:T(8,128)(2,1)S(1)} %get-tuple-element.47), channel_id=1, source_target_pairs={{0,6},{1,7},{2,4},{3,5},{4,2},{5,3},{6,0},{7,1},{8,14},{9,15},{10,... | collective-permute-start | bytes 258056 | tf_op jit(solution)/shard_map/ppermute | solution.py:517
  25.1 0.0 collective-permute-start.11
  25.1 0.9 %collective-permute-done.8.refs_1_ = bf16[336,128]{1,0:T(8,128)(2,1)S(1)} collective-permute-done((bf16[336,128]{1,0:T(8,128)(2,1)S(1)}, bf16[336,128]{1,0:T(8,128)(2,1)S(1)}, u32[]{:S(2)}, u32[]{:S(2)}) %collective-permute-start.8) | collective-permute-done | bytes 86048 | tf_op jit(solution)/shard_map/ppermute | solution.py:517
  26.0 0.0 collective-permute-start.12
  26.0 4.8 %collective-permute-done.9.refs_2_ = bf16[336,128]{1,0:T(8,128)(2,1)S(1)} collective-permute-done((bf16[336,128]{1,0:T(8,128)(2,1)S(1)}, bf16[336,128]{1,0:T(8,128)(2,1)S(1)}, u32[]{:S(2)}, u32[]{:S(2)}) %collective-permute-start.9) | collective-permute-done | bytes 86048 | tf_op jit(solution)/shard_map/ppermute | solution.py:517
  30.9 0.0 collective-permute-start.13
  30.9 0.0 collective-permute-done.10.refs_3_
  30.9 0.5 %collective-permute-start.14 = (bf16[336,128]{1,0:T(8,128)(2,1)S(1)}, bf16[336,128]{1,0:T(8,128)(2,1)S(1)}, u32[]{:S(2)}, u32[]{:S(2)}) collective-permute-start(bf16[336,128]{1,0:T(8,128)(2,1)S(1)} %collective-permute-done.10.refs_3_), channel_id=1, source_target_pairs={{0,1},{1,0},{2,3},{3,2},{4,5},{5,4},{6,7},{7,6},{8,9},{9,8},{10,11... | collective-permute-start | bytes 258056 | tf_op jit(solution)/shard_map/ppermute | solution.py:517
  31.4 0.0 copy-done.7
  31.4 0.1 fusion.5
  31.5 0.0 collective-permute-done.11.refs_4_
  31.5 0.0 collective-permute-done.12.refs_5_
  31.5 0.7 %collective-permute-done.13.refs_6_ = bf16[336,128]{1,0:T(8,128)(2,1)S(1)} collective-permute-done((bf16[336,128]{1,0:T(8,128)(2,1)S(1)}, bf16[336,128]{1,0:T(8,128)(2,1)S(1)}, u32[]{:S(2)}, u32[]{:S(2)}) %collective-permute-start.13) | collective-permute-done | bytes 86048 | tf_op jit(solution)/shard_map/ppermute | solution.py:517
  32.2 0.2 collective-permute-done.14.refs_7_
  32.3 0.1 shard_map.121
  32.4 1.4 %collective-permute-start.15 = (bf16[256,128]{1,0:T(8,128)(2,1)S(1)}, bf16[256,128]{1,0:T(8,128)(2,1)S(1)}, u32[]{:S(2)}, u32[]{:S(2)}) collective-permute-start(bf16[256,128]{1,0:T(8,128)(2,1)S(1)} %get-tuple-element.49), channel_id=1, source_target_pairs={{0,2},{1,3},{2,0},{3,1},{4,6},{5,7},{6,4},{7,5},{8,10},{9,11},{10,... | collective-permute-start | bytes 196616 | tf_op jit(solution)/shard_map/ppermute | solution.py:517
  33.8 0.0 copy-done.2
  33.8 0.0 copy-done.3
  33.8 0.0 copy-done.5
  33.8 2.8 %shard_map.122 = (bf16[2,16,128,128]{3,2,1,0:T(8,128)(2,1)}, f32[4,128,128]{2,1,0:T(8,128)S(1)}, f32[8,128]{1,0:T(8,128)S(1)}, f32[80,128]{1,0:T(8,128)S(1)}, bf16[14,128,128]{2,1,0:T(8,128)(2,1)S(1)}) custom-call(s32[4,16]{1,0:T(4,128)S(4)} %get-tuple-element.31.links_ref, s32[16]{0:T(128)S(4)} %get-tuple-element.32.rows_ref, ...), custom_call_target="tpu_custom_call" | custom-call | flops 1207959552 | bytes 2097152 | tf_op jit(solution)/shard_map/pallas_call | solution.py:555
  36.6 0.2 collective-permute-done.15.refs_1_
  36.8 0.9 %shard_map.123 = bf16[2,16,128,128]{3,2,1,0:T(8,128)(2,1)} custom-call(s32[4,16]{1,0:T(4,128)S(4)} %get-tuple-element.31.links_ref, s32[16]{0:T(128)S(4)} %get-tuple-element.32.rows_ref, bf16[256,128]{1,0:T(8,128)(2,1)S(1)} %get-tuple-element.48.refs_0_, bf16[256,128]{1,0:T(8,128)(2,1)S(1)} %collective-permute-done.15.refs_1_, ...), custom_call_target="tpu_custom_call", output_to_operand_aliasing={{}: (11, {})} | custom-call | tf_op jit(solution)/shard_map/pallas_call | solution.py:568
Async XLA Ops:
  0.0 14.8 %copy-start.6 = (bf16[3,3,128,128]{3,2,1,0:T(8,128)(2,1)S(1)}, bf16[3,3,128,128]{3,2,1,0:T(8,128)(2,1)}, u32[]{:S(2)}) copy-start(bf16[3,3,128,128]{3,2,1,0:T(8,128)(2,1)} %param.18) | copy-start | bytes 884740
  1.7 15.6 %copy-start = (f32[128]{0:T(128)S(1)}, f32[128]{0:T(128)}, u32[]{:S(2)}) copy-start(f32[128]{0:T(128)} %param.16) | copy-start | bytes 1540
  1.7 15.6 %copy-start.1 = (f32[128]{0:T(128)S(1)}, f32[128]{0:T(128)}, u32[]{:S(2)}) copy-start(f32[128]{0:T(128)} %param.17) | copy-start | bytes 1540
  1.7 15.5 %copy-start.4 = (f32[128]{0:T(128)S(1)}, f32[128]{0:T(128)}, u32[]{:S(2)}) copy-start(f32[128]{0:T(128)} %param.19) | copy-start | bytes 1540
  1.7 5.7 %collective-permute-start = (bf16[336,128]{1,0:T(8,128)(2,1)S(1)}, bf16[336,128]{1,0:T(8,128)(2,1)S(1)}, u32[]{:S(2)}, u32[]{:S(2)}) collective-permute-start(bf16[336,128]{1,0:T(8,128)(2,1)S(1)} %get-tuple-element.34), channel_id=1, source_target_pairs={{0,2},{1,3},{2,0},{3,1},{4,6},{5,7},{6,4},{7,5},{8,10},{9,11},{10,... | collective-permute-start | bytes 258056 | tf_op jit(solution)/shard_map/ppermute | solution.py:517
  4.8 9.5 %collective-permute-start.1 = (bf16[336,128]{1,0:T(8,128)(2,1)S(1)}, bf16[336,128]{1,0:T(8,128)(2,1)S(1)}, u32[]{:S(2)}, u32[]{:S(2)}) collective-permute-start(bf16[336,128]{1,0:T(8,128)(2,1)S(1)} %get-tuple-element.35), channel_id=1, source_target_pairs={{0,4},{1,5},{2,6},{3,7},{4,0},{5,1},{6,2},{7,3},{8,12},{9,13},{10,... | collective-permute-start | bytes 258056 | tf_op jit(solution)/shard_map/ppermute | solution.py:517
  7.4 6.9 %collective-permute-start.2 = (bf16[336,128]{1,0:T(8,128)(2,1)S(1)}, bf16[336,128]{1,0:T(8,128)(2,1)S(1)}, u32[]{:S(2)}, u32[]{:S(2)}) collective-permute-start(bf16[336,128]{1,0:T(8,128)(2,1)S(1)} %get-tuple-element.36), channel_id=1, source_target_pairs={{0,6},{1,7},{2,4},{3,5},{4,2},{5,3},{6,0},{7,1},{8,14},{9,15},{10,... | collective-permute-start | bytes 258056 | tf_op jit(solution)/shard_map/ppermute | solution.py:517
  7.4 7.5 %collective-permute-start.3 = (bf16[336,128]{1,0:T(8,128)(2,1)S(1)}, bf16[336,128]{1,0:T(8,128)(2,1)S(1)}, u32[]{:S(2)}, u32[]{:S(2)}) collective-permute-start(bf16[336,128]{1,0:T(8,128)(2,1)S(1)} %get-tuple-element.33.refs_0_), channel_id=1, source_target_pairs={{0,1},{1,0},{2,3},{3,2},{4,5},{5,4},{6,7},{7,6},{8,9},{9,8},{10,11... | collective-permute-start | bytes 258056 | tf_op jit(solution)/shard_map/ppermute | solution.py:517
  7.4 7.5 %collective-permute-start.4 = (bf16[336,128]{1,0:T(8,128)(2,1)S(1)}, bf16[336,128]{1,0:T(8,128)(2,1)S(1)}, u32[]{:S(2)}, u32[]{:S(2)}) collective-permute-start(bf16[336,128]{1,0:T(8,128)(2,1)S(1)} %collective-permute-done.refs_1_), channel_id=1, source_target_pairs={{0,1},{1,0},{2,3},{3,2},{4,5},{5,4},{6,7},{7,6},{8,9},{9,8},{10,11... | collective-permute-start | bytes 258056 | tf_op jit(solution)/shard_map/ppermute | solution.py:517
  14.3 1.3 %collective-permute-start.5 = (bf16[336,128]{1,0:T(8,128)(2,1)S(1)}, bf16[336,128]{1,0:T(8,128)(2,1)S(1)}, u32[]{:S(2)}, u32[]{:S(2)}) collective-permute-start(bf16[336,128]{1,0:T(8,128)(2,1)S(1)} %collective-permute-done.1.refs_2_), channel_id=1, source_target_pairs={{0,1},{1,0},{2,3},{3,2},{4,5},{5,4},{6,7},{7,6},{8,9},{9,8},{10,11... | collective-permute-start | bytes 258056 | tf_op jit(solution)/shard_map/ppermute | solution.py:517
  14.3 1.4 %collective-permute-start.6 = (bf16[336,128]{1,0:T(8,128)(2,1)S(1)}, bf16[336,128]{1,0:T(8,128)(2,1)S(1)}, u32[]{:S(2)}, u32[]{:S(2)}) collective-permute-start(bf16[336,128]{1,0:T(8,128)(2,1)S(1)} %collective-permute-done.2.refs_3_), channel_id=1, source_target_pairs={{0,1},{1,0},{2,3},{3,2},{4,5},{5,4},{6,7},{7,6},{8,9},{9,8},{10,11... | collective-permute-start | bytes 258056 | tf_op jit(solution)/shard_map/ppermute | solution.py:517
  15.8 4.4 %collective-permute-start.7 = (bf16[256,128]{1,0:T(8,128)(2,1)S(1)}, bf16[256,128]{1,0:T(8,128)(2,1)S(1)}, u32[]{:S(2)}, u32[]{:S(2)}) collective-permute-start(bf16[256,128]{1,0:T(8,128)(2,1)S(1)} %get-tuple-element.38), channel_id=1, source_target_pairs={{0,2},{1,3},{2,0},{3,1},{4,6},{5,7},{6,4},{7,5},{8,10},{9,11},{10,... | collective-permute-start | bytes 196616 | tf_op jit(solution)/shard_map/ppermute | solution.py:517
  20.0 11.4 %copy-start.7 = (bf16[3,3,128,128]{3,2,1,0:T(8,128)(2,1)S(1)}, bf16[3,3,128,128]{3,2,1,0:T(8,128)(2,1)}, u32[]{:S(2)}) copy-start(bf16[3,3,128,128]{3,2,1,0:T(8,128)(2,1)} %param.22) | copy-start | bytes 884740
  20.6 13.2 %copy-start.2 = (f32[128]{0:T(128)S(1)}, f32[128]{0:T(128)}, u32[]{:S(2)}) copy-start(f32[128]{0:T(128)} %param.20) | copy-start | bytes 1540
  20.6 13.2 %copy-start.3 = (f32[128]{0:T(128)S(1)}, f32[128]{0:T(128)}, u32[]{:S(2)}) copy-start(f32[128]{0:T(128)} %param.21) | copy-start | bytes 1540
  20.6 13.2 %copy-start.5 = (f32[128]{0:T(128)S(1)}, f32[128]{0:T(128)}, u32[]{:S(2)}) copy-start(f32[128]{0:T(128)} %param.23) | copy-start | bytes 1540
  20.6 5.4 %collective-permute-start.8 = (bf16[336,128]{1,0:T(8,128)(2,1)S(1)}, bf16[336,128]{1,0:T(8,128)(2,1)S(1)}, u32[]{:S(2)}, u32[]{:S(2)}) collective-permute-start(bf16[336,128]{1,0:T(8,128)(2,1)S(1)} %get-tuple-element.45), channel_id=1, source_target_pairs={{0,2},{1,3},{2,0},{3,1},{4,6},{5,7},{6,4},{7,5},{8,10},{9,11},{10,... | collective-permute-start | bytes 258056 | tf_op jit(solution)/shard_map/ppermute | solution.py:517
  21.9 8.9 %collective-permute-start.9 = (bf16[336,128]{1,0:T(8,128)(2,1)S(1)}, bf16[336,128]{1,0:T(8,128)(2,1)S(1)}, u32[]{:S(2)}, u32[]{:S(2)}) collective-permute-start(bf16[336,128]{1,0:T(8,128)(2,1)S(1)} %get-tuple-element.46), channel_id=1, source_target_pairs={{0,4},{1,5},{2,6},{3,7},{4,0},{5,1},{6,2},{7,3},{8,12},{9,13},{10,... | collective-permute-start | bytes 258056 | tf_op jit(solution)/shard_map/ppermute | solution.py:517
  23.7 7.1 %collective-permute-start.10 = (bf16[336,128]{1,0:T(8,128)(2,1)S(1)}, bf16[336,128]{1,0:T(8,128)(2,1)S(1)}, u32[]{:S(2)}, u32[]{:S(2)}) collective-permute-start(bf16[336,128]{1,0:T(8,128)(2,1)S(1)} %get-tuple-element.47), channel_id=1, source_target_pairs={{0,6},{1,7},{2,4},{3,5},{4,2},{5,3},{6,0},{7,1},{8,14},{9,15},{10,... | collective-permute-start | bytes 258056 | tf_op jit(solution)/shard_map/ppermute | solution.py:517
  25.1 6.4 %collective-permute-start.11 = (bf16[336,128]{1,0:T(8,128)(2,1)S(1)}, bf16[336,128]{1,0:T(8,128)(2,1)S(1)}, u32[]{:S(2)}, u32[]{:S(2)}) collective-permute-start(bf16[336,128]{1,0:T(8,128)(2,1)S(1)} %get-tuple-element.44.refs_0_), channel_id=1, source_target_pairs={{0,1},{1,0},{2,3},{3,2},{4,5},{5,4},{6,7},{7,6},{8,9},{9,8},{10,11... | collective-permute-start | bytes 258056 | tf_op jit(solution)/shard_map/ppermute | solution.py:517
  26.0 5.5 %collective-permute-start.12 = (bf16[336,128]{1,0:T(8,128)(2,1)S(1)}, bf16[336,128]{1,0:T(8,128)(2,1)S(1)}, u32[]{:S(2)}, u32[]{:S(2)}) collective-permute-start(bf16[336,128]{1,0:T(8,128)(2,1)S(1)} %collective-permute-done.8.refs_1_), channel_id=1, source_target_pairs={{0,1},{1,0},{2,3},{3,2},{4,5},{5,4},{6,7},{7,6},{8,9},{9,8},{10,11... | collective-permute-start | bytes 258056 | tf_op jit(solution)/shard_map/ppermute | solution.py:517
  30.9 1.3 %collective-permute-start.13 = (bf16[336,128]{1,0:T(8,128)(2,1)S(1)}, bf16[336,128]{1,0:T(8,128)(2,1)S(1)}, u32[]{:S(2)}, u32[]{:S(2)}) collective-permute-start(bf16[336,128]{1,0:T(8,128)(2,1)S(1)} %collective-permute-done.9.refs_2_), channel_id=1, source_target_pairs={{0,1},{1,0},{2,3},{3,2},{4,5},{5,4},{6,7},{7,6},{8,9},{9,8},{10,11... | collective-permute-start | bytes 258056 | tf_op jit(solution)/shard_map/ppermute | solution.py:517
  30.9 1.4 %collective-permute-start.14 = (bf16[336,128]{1,0:T(8,128)(2,1)S(1)}, bf16[336,128]{1,0:T(8,128)(2,1)S(1)}, u32[]{:S(2)}, u32[]{:S(2)}) collective-permute-start(bf16[336,128]{1,0:T(8,128)(2,1)S(1)} %collective-permute-done.10.refs_3_), channel_id=1, source_target_pairs={{0,1},{1,0},{2,3},{3,2},{4,5},{5,4},{6,7},{7,6},{8,9},{9,8},{10,11... | collective-permute-start | bytes 258056 | tf_op jit(solution)/shard_map/ppermute | solution.py:517
  32.4 4.4 %collective-permute-start.15 = (bf16[256,128]{1,0:T(8,128)(2,1)S(1)}, bf16[256,128]{1,0:T(8,128)(2,1)S(1)}, u32[]{:S(2)}, u32[]{:S(2)}) collective-permute-start(bf16[256,128]{1,0:T(8,128)(2,1)S(1)} %get-tuple-element.49), channel_id=1, source_target_pairs={{0,2},{1,3},{2,0},{3,1},{4,6},{5,7},{6,4},{7,5},{8,10},{9,11},{10,... | collective-permute-start | bytes 196616 | tf_op jit(solution)/shard_map/ppermute | solution.py:517

commit v5 on v4

--- a/solution.py
+++ b/solution.py
@@ -526,7 +526,10 @@
         if not plan.direct:
             return [lax.all_gather(bufs[0], AXIS)]
         own = spread(bufs)
-        return own + [swap(array, 1) for array in own]
+        other = []
+        for array in own:
+            other.append(swap(array, 1))
+        return own + other
 
     def shape(dims, dtype=f32):
         return jax.ShapeDtypeStruct(dims, dtype)

time: 37.9 us -> 37.9 us (level)
  no operation moved by 1% of the time
where the time goes in v5:
time: 37.9 us; the launch traced here: 37.8 us
  starting transfers between devices  14.5 us (38%)
  waiting for transfers between devices  14.3 us (38%)
  Pallas kernels  8.6 us (23%)
    ppermute x16, starting transfers between devices, swap(): return lax.ppermute(array, AXIS, [(i, i ^ distance) for i in range(size)])  14.5 us
    ppermute x16, waiting for transfers between devices, swap(): return lax.ppermute(array, AXIS, [(i, i ^ distance) for i in range(size)])  14.3 us
    pallas_call x2, Pallas kernels, stage(): pl.pallas_call(functools.partial(middle_kernel, plan, last), out_shape=[t...  5.52 us
    pallas_call x1, Pallas kernels, shards(): pl.pallas_call(functools.partial(edges_kernel, plan), out_shape=[pltpu.SM...  1.64 us
    pallas_call x1, Pallas kernels, stage(): pl.pallas_call(functools.partial(ends_kernel, plan, last), out_shape=tile...  0.95 us
  transfers between devices with their start and end apart: 16, of which 9 were waited for; matrix products, arithmetic and copies ran while one was open for 0% of the time, Pallas kernels for 15%

profile of v5, /device:TPU:0, one launch (start us, length us, event | category | flops | bytes accessed | tf_op | source)
XLA Modules:
  0.0 37.8 jit_solution(15921263305888029643)
XLA Ops:
  0.0 0.0 copy-start.6
  0.0 1.6 %edges.1 = (s32[4,16]{1,0:T(4,128)S(4)}, s32[16]{0:T(128)S(4)}, s32[16]{0:T(128)S(4)}, bf16[2,16,128,128]{3,2,1,0:T(8,128)(2,1)S(1)}, bf16[336,128]{1,0:T(8,128)...) custom-call(s32[4,16]{1,0:T(4,128)} %bitcast.23, s32[16]{0:T(128)} %rows_hbm.1, ...), custom_call_target="tpu_custom_call" | custom-call | tf_op jit(solution)/shard_map/edges/pallas_call | solution.py:592
  1.7 0.0 copy-start
  1.7 0.0 copy-start.1
  1.7 0.0 copy-start.4
  1.7 3.1 %collective-permute-start = (bf16[336,128]{1,0:T(8,128)(2,1)S(1)}, bf16[336,128]{1,0:T(8,128)(2,1)S(1)}, u32[]{:S(2)}, u32[]{:S(2)}) collective-permute-start(bf16[336,128]{1,0:T(8,128)(2,1)S(1)} %get-tuple-element.34), channel_id=1, source_target_pairs={{0,2},{1,3},{2,0},{3,1},{4,6},{5,7},{6,4},{7,5},{8,10},{9,11},{10,... | collective-permute-start | bytes 258056 | tf_op jit(solution)/shard_map/ppermute | solution.py:517
  4.8 2.6 %collective-permute-start.1 = (bf16[336,128]{1,0:T(8,128)(2,1)S(1)}, bf16[336,128]{1,0:T(8,128)(2,1)S(1)}, u32[]{:S(2)}, u32[]{:S(2)}) collective-permute-start(bf16[336,128]{1,0:T(8,128)(2,1)S(1)} %get-tuple-element.35), channel_id=1, source_target_pairs={{0,4},{1,5},{2,6},{3,7},{4,0},{5,1},{6,2},{7,3},{8,12},{9,13},{10,... | collective-permute-start | bytes 258056 | tf_op jit(solution)/shard_map/ppermute | solution.py:517
  7.4 0.0 collective-permute-start.2
  7.4 0.0 collective-permute-start.3
  7.4 0.0 collective-permute-done.refs_1_
  7.4 0.5 %collective-permute-start.4 = (bf16[336,128]{1,0:T(8,128)(2,1)S(1)}, bf16[336,128]{1,0:T(8,128)(2,1)S(1)}, u32[]{:S(2)}, u32[]{:S(2)}) collective-permute-start(bf16[336,128]{1,0:T(8,128)(2,1)S(1)} %collective-permute-done.refs_1_), channel_id=1, source_target_pairs={{0,1},{1,0},{2,3},{3,2},{4,5},{5,4},{6,7},{7,6},{8,9},{9,8},{10,11... | collective-permute-start | bytes 258056 | tf_op jit(solution)/shard_map/ppermute | solution.py:517
  7.9 6.4 %collective-permute-done.1.refs_2_ = bf16[336,128]{1,0:T(8,128)(2,1)S(1)} collective-permute-done((bf16[336,128]{1,0:T(8,128)(2,1)S(1)}, bf16[336,128]{1,0:T(8,128)(2,1)S(1)}, u32[]{:S(2)}, u32[]{:S(2)}) %collective-permute-start.1) | collective-permute-done | bytes 86048 | tf_op jit(solution)/shard_map/ppermute | solution.py:517
  14.3 0.0 collective-permute-start.5
  14.3 0.0 collective-permute-done.2.refs_3_
  14.3 0.5 %collective-permute-start.6 = (bf16[336,128]{1,0:T(8,128)(2,1)S(1)}, bf16[336,128]{1,0:T(8,128)(2,1)S(1)}, u32[]{:S(2)}, u32[]{:S(2)}) collective-permute-start(bf16[336,128]{1,0:T(8,128)(2,1)S(1)} %collective-permute-done.2.refs_3_), channel_id=1, source_target_pairs={{0,1},{1,0},{2,3},{3,2},{4,5},{5,4},{6,7},{7,6},{8,9},{9,8},{10,11... | collective-permute-start | bytes 258056 | tf_op jit(solution)/shard_map/ppermute | solution.py:517
  14.8 0.0 copy-done.6
  14.8 0.1 fusion.4
  14.9 0.0 collective-permute-done.3.refs_4_
  14.9 0.0 collective-permute-done.4.refs_5_
  14.9 0.7 %collective-permute-done.5.refs_6_ = bf16[336,128]{1,0:T(8,128)(2,1)S(1)} collective-permute-done((bf16[336,128]{1,0:T(8,128)(2,1)S(1)}, bf16[336,128]{1,0:T(8,128)(2,1)S(1)}, u32[]{:S(2)}, u32[]{:S(2)}) %collective-permute-start.5) | collective-permute-done | bytes 86048 | tf_op jit(solution)/shard_map/ppermute | solution.py:517
  15.6 0.2 collective-permute-done.6.refs_7_
  15.7 0.1 shard_map.118
  15.8 1.4 %collective-permute-start.7 = (bf16[256,128]{1,0:T(8,128)(2,1)S(1)}, bf16[256,128]{1,0:T(8,128)(2,1)S(1)}, u32[]{:S(2)}, u32[]{:S(2)}) collective-permute-start(bf16[256,128]{1,0:T(8,128)(2,1)S(1)} %get-tuple-element.38), channel_id=1, source_target_pairs={{0,2},{1,3},{2,0},{3,1},{4,6},{5,7},{6,4},{7,5},{8,10},{9,11},{10,... | collective-permute-start | bytes 196616 | tf_op jit(solution)/shard_map/ppermute | solution.py:517
  17.2 0.0 copy-done
  17.2 0.0 copy-done.1
  17.2 0.0 copy-done.4
  17.2 2.7 %shard_map.119 = (bf16[2,16,128,128]{3,2,1,0:T(8,128)(2,1)S(1)}, f32[4,128,128]{2,1,0:T(8,128)S(1)}, f32[8,128]{1,0:T(8,128)S(1)}, f32[80,128]{1,0:T(8,128)S(1)}) custom-call(s32[4,16]{1,0:T(4,128)S(4)} %get-tuple-element.31.links_ref, s32[16]{0:T(128)S(4)} %get-tuple-element.32.rows_ref, s32[16]{0:T(128)S(4)} %get-tuple-element.39.image_ref, ...), custom_call_target="tpu_custom_call" | custom-call | flops 1207959552 | bytes 2097152 | tf_op jit(solution)/shard_map/pallas_call | solution.py:558
  20.0 0.0 copy-start.7
  20.0 0.3 collective-permute-done.7.refs_1_
  20.2 0.4 shard_map.120
  20.6 0.0 copy-start.2
  20.6 0.0 copy-start.3
  20.6 0.0 copy-start.5
  20.6 1.3 %collective-permute-start.8 = (bf16[336,128]{1,0:T(8,128)(2,1)S(1)}, bf16[336,128]{1,0:T(8,128)(2,1)S(1)}, u32[]{:S(2)}, u32[]{:S(2)}) collective-permute-start(bf16[336,128]{1,0:T(8,128)(2,1)S(1)} %get-tuple-element.45), channel_id=1, source_target_pairs={{0,2},{1,3},{2,0},{3,1},{4,6},{5,7},{6,4},{7,5},{8,10},{9,11},{10,... | collective-permute-start | bytes 258056 | tf_op jit(solution)/shard_map/ppermute | solution.py:517
  21.9 1.8 %collective-permute-start.9 = (bf16[336,128]{1,0:T(8,128)(2,1)S(1)}, bf16[336,128]{1,0:T(8,128)(2,1)S(1)}, u32[]{:S(2)}, u32[]{:S(2)}) collective-permute-start(bf16[336,128]{1,0:T(8,128)(2,1)S(1)} %get-tuple-element.46), channel_id=1, source_target_pairs={{0,4},{1,5},{2,6},{3,7},{4,0},{5,1},{6,2},{7,3},{8,12},{9,13},{10,... | collective-permute-start | bytes 258056 | tf_op jit(solution)/shard_map/ppermute | solution.py:517
  23.7 1.3 %collective-permute-start.10 = (bf16[336,128]{1,0:T(8,128)(2,1)S(1)}, bf16[336,128]{1,0:T(8,128)(2,1)S(1)}, u32[]{:S(2)}, u32[]{:S(2)}) collective-permute-start(bf16[336,128]{1,0:T(8,128)(2,1)S(1)} %get-tuple-element.47), channel_id=1, source_target_pairs={{0,6},{1,7},{2,4},{3,5},{4,2},{5,3},{6,0},{7,1},{8,14},{9,15},{10,... | collective-permute-start | bytes 258056 | tf_op jit(solution)/shard_map/ppermute | solution.py:517
  25.1 0.0 collective-permute-start.11
  25.1 0.9 %collective-permute-done.8.refs_1_ = bf16[336,128]{1,0:T(8,128)(2,1)S(1)} collective-permute-done((bf16[336,128]{1,0:T(8,128)(2,1)S(1)}, bf16[336,128]{1,0:T(8,128)(2,1)S(1)}, u32[]{:S(2)}, u32[]{:S(2)}) %collective-permute-start.8) | collective-permute-done | bytes 86048 | tf_op jit(solution)/shard_map/ppermute | solution.py:517
  26.0 0.0 collective-permute-start.12
  26.0 4.8 %collective-permute-done.9.refs_2_ = bf16[336,128]{1,0:T(8,128)(2,1)S(1)} collective-permute-done((bf16[336,128]{1,0:T(8,128)(2,1)S(1)}, bf16[336,128]{1,0:T(8,128)(2,1)S(1)}, u32[]{:S(2)}, u32[]{:S(2)}) %collective-permute-start.9) | collective-permute-done | bytes 86048 | tf_op jit(solution)/shard_map/ppermute | solution.py:517
  30.9 0.0 collective-permute-start.13
  30.9 0.0 collective-permute-done.10.refs_3_
  30.9 0.5 %collective-permute-start.14 = (bf16[336,128]{1,0:T(8,128)(2,1)S(1)}, bf16[336,128]{1,0:T(8,128)(2,1)S(1)}, u32[]{:S(2)}, u32[]{:S(2)}) collective-permute-start(bf16[336,128]{1,0:T(8,128)(2,1)S(1)} %collective-permute-done.10.refs_3_), channel_id=1, source_target_pairs={{0,1},{1,0},{2,3},{3,2},{4,5},{5,4},{6,7},{7,6},{8,9},{9,8},{10,11... | collective-permute-start | bytes 258056 | tf_op jit(solution)/shard_map/ppermute | solution.py:517
  31.4 0.0 copy-done.7
  31.4 0.1 fusion.5
  31.5 0.0 collective-permute-done.11.refs_4_
  31.5 0.0 collective-permute-done.12.refs_5_
  31.5 0.7 %collective-permute-done.13.refs_6_ = bf16[336,128]{1,0:T(8,128)(2,1)S(1)} collective-permute-done((bf16[336,128]{1,0:T(8,128)(2,1)S(1)}, bf16[336,128]{1,0:T(8,128)(2,1)S(1)}, u32[]{:S(2)}, u32[]{:S(2)}) %collective-permute-start.13) | collective-permute-done | bytes 86048 | tf_op jit(solution)/shard_map/ppermute | solution.py:517
  32.2 0.2 collective-permute-done.14.refs_7_
  32.3 0.1 shard_map.121
  32.4 1.4 %collective-permute-start.15 = (bf16[256,128]{1,0:T(8,128)(2,1)S(1)}, bf16[256,128]{1,0:T(8,128)(2,1)S(1)}, u32[]{:S(2)}, u32[]{:S(2)}) collective-permute-start(bf16[256,128]{1,0:T(8,128)(2,1)S(1)} %get-tuple-element.49), channel_id=1, source_target_pairs={{0,2},{1,3},{2,0},{3,1},{4,6},{5,7},{6,4},{7,5},{8,10},{9,11},{10,... | collective-permute-start | bytes 196616 | tf_op jit(solution)/shard_map/ppermute | solution.py:517
  33.8 0.0 copy-done.2
  33.8 0.0 copy-done.3
  33.8 0.0 copy-done.5
  33.8 2.8 %shard_map.122 = (bf16[2,16,128,128]{3,2,1,0:T(8,128)(2,1)}, f32[4,128,128]{2,1,0:T(8,128)S(1)}, f32[8,128]{1,0:T(8,128)S(1)}, f32[80,128]{1,0:T(8,128)S(1)}, bf16[14,128,128]{2,1,0:T(8,128)(2,1)S(1)}) custom-call(s32[4,16]{1,0:T(4,128)S(4)} %get-tuple-element.31.links_ref, s32[16]{0:T(128)S(4)} %get-tuple-element.32.rows_ref, ...), custom_call_target="tpu_custom_call" | custom-call | flops 1207959552 | bytes 2097152 | tf_op jit(solution)/shard_map/pallas_call | solution.py:558
  36.6 0.2 collective-permute-done.15.refs_1_
  36.8 0.9 %shard_map.123 = bf16[2,16,128,128]{3,2,1,0:T(8,128)(2,1)} custom-call(s32[4,16]{1,0:T(4,128)S(4)} %get-tuple-element.31.links_ref, s32[16]{0:T(128)S(4)} %get-tuple-element.32.rows_ref, bf16[256,128]{1,0:T(8,128)(2,1)S(1)} %get-tuple-element.48.refs_0_, bf16[256,128]{1,0:T(8,128)(2,1)S(1)} %collective-permute-done.15.refs_1_, ...), custom_call_target="tpu_custom_call", output_to_operand_aliasing={{}: (11, {})} | custom-call | tf_op jit(solution)/shard_map/pallas_call | solution.py:571
Async XLA Ops:
  0.0 14.8 %copy-start.6 = (bf16[3,3,128,128]{3,2,1,0:T(8,128)(2,1)S(1)}, bf16[3,3,128,128]{3,2,1,0:T(8,128)(2,1)}, u32[]{:S(2)}) copy-start(bf16[3,3,128,128]{3,2,1,0:T(8,128)(2,1)} %param.18) | copy-start | bytes 884740
  1.7 15.6 %copy-start = (f32[128]{0:T(128)S(1)}, f32[128]{0:T(128)}, u32[]{:S(2)}) copy-start(f32[128]{0:T(128)} %param.16) | copy-start | bytes 1540
  1.7 15.6 %copy-start.1 = (f32[128]{0:T(128)S(1)}, f32[128]{0:T(128)}, u32[]{:S(2)}) copy-start(f32[128]{0:T(128)} %param.17) | copy-start | bytes 1540
  1.7 15.5 %copy-start.4 = (f32[128]{0:T(128)S(1)}, f32[128]{0:T(128)}, u32[]{:S(2)}) copy-start(f32[128]{0:T(128)} %param.19) | copy-start | bytes 1540
  1.7 5.7 %collective-permute-start = (bf16[336,128]{1,0:T(8,128)(2,1)S(1)}, bf16[336,128]{1,0:T(8,128)(2,1)S(1)}, u32[]{:S(2)}, u32[]{:S(2)}) collective-permute-start(bf16[336,128]{1,0:T(8,128)(2,1)S(1)} %get-tuple-element.34), channel_id=1, source_target_pairs={{0,2},{1,3},{2,0},{3,1},{4,6},{5,7},{6,4},{7,5},{8,10},{9,11},{10,... | collective-permute-start | bytes 258056 | tf_op jit(solution)/shard_map/ppermute | solution.py:517
  4.8 9.5 %collective-permute-start.1 = (bf16[336,128]{1,0:T(8,128)(2,1)S(1)}, bf16[336,128]{1,0:T(8,128)(2,1)S(1)}, u32[]{:S(2)}, u32[]{:S(2)}) collective-permute-start(bf16[336,128]{1,0:T(8,128)(2,1)S(1)} %get-tuple-element.35), channel_id=1, source_target_pairs={{0,4},{1,5},{2,6},{3,7},{4,0},{5,1},{6,2},{7,3},{8,12},{9,13},{10,... | collective-permute-start | bytes 258056 | tf_op jit(solution)/shard_map/ppermute | solution.py:517
  7.4 6.9 %collective-permute-start.2 = (bf16[336,128]{1,0:T(8,128)(2,1)S(1)}, bf16[336,128]{1,0:T(8,128)(2,1)S(1)}, u32[]{:S(2)}, u32[]{:S(2)}) collective-permute-start(bf16[336,128]{1,0:T(8,128)(2,1)S(1)} %get-tuple-element.36), channel_id=1, source_target_pairs={{0,6},{1,7},{2,4},{3,5},{4,2},{5,3},{6,0},{7,1},{8,14},{9,15},{10,... | collective-permute-start | bytes 258056 | tf_op jit(solution)/shard_map/ppermute | solution.py:517
  7.4 7.5 %collective-permute-start.3 = (bf16[336,128]{1,0:T(8,128)(2,1)S(1)}, bf16[336,128]{1,0:T(8,128)(2,1)S(1)}, u32[]{:S(2)}, u32[]{:S(2)}) collective-permute-start(bf16[336,128]{1,0:T(8,128)(2,1)S(1)} %get-tuple-element.33.refs_0_), channel_id=1, source_target_pairs={{0,1},{1,0},{2,3},{3,2},{4,5},{5,4},{6,7},{7,6},{8,9},{9,8},{10,11... | collective-permute-start | bytes 258056 | tf_op jit(solution)/shard_map/ppermute | solution.py:517
  7.4 7.5 %collective-permute-start.4 = (bf16[336,128]{1,0:T(8,128)(2,1)S(1)}, bf16[336,128]{1,0:T(8,128)(2,1)S(1)}, u32[]{:S(2)}, u32[]{:S(2)}) collective-permute-start(bf16[336,128]{1,0:T(8,128)(2,1)S(1)} %collective-permute-done.refs_1_), channel_id=1, source_target_pairs={{0,1},{1,0},{2,3},{3,2},{4,5},{5,4},{6,7},{7,6},{8,9},{9,8},{10,11... | collective-permute-start | bytes 258056 | tf_op jit(solution)/shard_map/ppermute | solution.py:517
  14.3 1.3 %collective-permute-start.5 = (bf16[336,128]{1,0:T(8,128)(2,1)S(1)}, bf16[336,128]{1,0:T(8,128)(2,1)S(1)}, u32[]{:S(2)}, u32[]{:S(2)}) collective-permute-start(bf16[336,128]{1,0:T(8,128)(2,1)S(1)} %collective-permute-done.1.refs_2_), channel_id=1, source_target_pairs={{0,1},{1,0},{2,3},{3,2},{4,5},{5,4},{6,7},{7,6},{8,9},{9,8},{10,11... | collective-permute-start | bytes 258056 | tf_op jit(solution)/shard_map/ppermute | solution.py:517
  14.3 1.4 %collective-permute-start.6 = (bf16[336,128]{1,0:T(8,128)(2,1)S(1)}, bf16[336,128]{1,0:T(8,128)(2,1)S(1)}, u32[]{:S(2)}, u32[]{:S(2)}) collective-permute-start(bf16[336,128]{1,0:T(8,128)(2,1)S(1)} %collective-permute-done.2.refs_3_), channel_id=1, source_target_pairs={{0,1},{1,0},{2,3},{3,2},{4,5},{5,4},{6,7},{7,6},{8,9},{9,8},{10,11... | collective-permute-start | bytes 258056 | tf_op jit(solution)/shard_map/ppermute | solution.py:517
  15.8 4.4 %collective-permute-start.7 = (bf16[256,128]{1,0:T(8,128)(2,1)S(1)}, bf16[256,128]{1,0:T(8,128)(2,1)S(1)}, u32[]{:S(2)}, u32[]{:S(2)}) collective-permute-start(bf16[256,128]{1,0:T(8,128)(2,1)S(1)} %get-tuple-element.38), channel_id=1, source_target_pairs={{0,2},{1,3},{2,0},{3,1},{4,6},{5,7},{6,4},{7,5},{8,10},{9,11},{10,... | collective-permute-start | bytes 196616 | tf_op jit(solution)/shard_map/ppermute | solution.py:517
  20.0 11.4 %copy-start.7 = (bf16[3,3,128,128]{3,2,1,0:T(8,128)(2,1)S(1)}, bf16[3,3,128,128]{3,2,1,0:T(8,128)(2,1)}, u32[]{:S(2)}) copy-start(bf16[3,3,128,128]{3,2,1,0:T(8,128)(2,1)} %param.22) | copy-start | bytes 884740
  20.6 13.2 %copy-start.2 = (f32[128]{0:T(128)S(1)}, f32[128]{0:T(128)}, u32[]{:S(2)}) copy-start(f32[128]{0:T(128)} %param.20) | copy-start | bytes 1540
  20.6 13.2 %copy-start.3 = (f32[128]{0:T(128)S(1)}, f32[128]{0:T(128)}, u32[]{:S(2)}) copy-start(f32[128]{0:T(128)} %param.21) | copy-start | bytes 1540
  20.6 13.2 %copy-start.5 = (f32[128]{0:T(128)S(1)}, f32[128]{0:T(128)}, u32[]{:S(2)}) copy-start(f32[128]{0:T(128)} %param.23) | copy-start | bytes 1540
  20.6 5.4 %collective-permute-start.8 = (bf16[336,128]{1,0:T(8,128)(2,1)S(1)}, bf16[336,128]{1,0:T(8,128)(2,1)S(1)}, u32[]{:S(2)}, u32[]{:S(2)}) collective-permute-start(bf16[336,128]{1,0:T(8,128)(2,1)S(1)} %get-tuple-element.45), channel_id=1, source_target_pairs={{0,2},{1,3},{2,0},{3,1},{4,6},{5,7},{6,4},{7,5},{8,10},{9,11},{10,... | collective-permute-start | bytes 258056 | tf_op jit(solution)/shard_map/ppermute | solution.py:517
  21.9 8.9 %collective-permute-start.9 = (bf16[336,128]{1,0:T(8,128)(2,1)S(1)}, bf16[336,128]{1,0:T(8,128)(2,1)S(1)}, u32[]{:S(2)}, u32[]{:S(2)}) collective-permute-start(bf16[336,128]{1,0:T(8,128)(2,1)S(1)} %get-tuple-element.46), channel_id=1, source_target_pairs={{0,4},{1,5},{2,6},{3,7},{4,0},{5,1},{6,2},{7,3},{8,12},{9,13},{10,... | collective-permute-start | bytes 258056 | tf_op jit(solution)/shard_map/ppermute | solution.py:517
  23.7 7.1 %collective-permute-start.10 = (bf16[336,128]{1,0:T(8,128)(2,1)S(1)}, bf16[336,128]{1,0:T(8,128)(2,1)S(1)}, u32[]{:S(2)}, u32[]{:S(2)}) collective-permute-start(bf16[336,128]{1,0:T(8,128)(2,1)S(1)} %get-tuple-element.47), channel_id=1, source_target_pairs={{0,6},{1,7},{2,4},{3,5},{4,2},{5,3},{6,0},{7,1},{8,14},{9,15},{10,... | collective-permute-start | bytes 258056 | tf_op jit(solution)/shard_map/ppermute | solution.py:517
  25.1 6.4 %collective-permute-start.11 = (bf16[336,128]{1,0:T(8,128)(2,1)S(1)}, bf16[336,128]{1,0:T(8,128)(2,1)S(1)}, u32[]{:S(2)}, u32[]{:S(2)}) collective-permute-start(bf16[336,128]{1,0:T(8,128)(2,1)S(1)} %get-tuple-element.44.refs_0_), channel_id=1, source_target_pairs={{0,1},{1,0},{2,3},{3,2},{4,5},{5,4},{6,7},{7,6},{8,9},{9,8},{10,11... | collective-permute-start | bytes 258056 | tf_op jit(solution)/shard_map/ppermute | solution.py:517
  26.0 5.5 %collective-permute-start.12 = (bf16[336,128]{1,0:T(8,128)(2,1)S(1)}, bf16[336,128]{1,0:T(8,128)(2,1)S(1)}, u32[]{:S(2)}, u32[]{:S(2)}) collective-permute-start(bf16[336,128]{1,0:T(8,128)(2,1)S(1)} %collective-permute-done.8.refs_1_), channel_id=1, source_target_pairs={{0,1},{1,0},{2,3},{3,2},{4,5},{5,4},{6,7},{7,6},{8,9},{9,8},{10,11... | collective-permute-start | bytes 258056 | tf_op jit(solution)/shard_map/ppermute | solution.py:517
  30.9 1.3 %collective-permute-start.13 = (bf16[336,128]{1,0:T(8,128)(2,1)S(1)}, bf16[336,128]{1,0:T(8,128)(2,1)S(1)}, u32[]{:S(2)}, u32[]{:S(2)}) collective-permute-start(bf16[336,128]{1,0:T(8,128)(2,1)S(1)} %collective-permute-done.9.refs_2_), channel_id=1, source_target_pairs={{0,1},{1,0},{2,3},{3,2},{4,5},{5,4},{6,7},{7,6},{8,9},{9,8},{10,11... | collective-permute-start | bytes 258056 | tf_op jit(solution)/shard_map/ppermute | solution.py:517
  30.9 1.4 %collective-permute-start.14 = (bf16[336,128]{1,0:T(8,128)(2,1)S(1)}, bf16[336,128]{1,0:T(8,128)(2,1)S(1)}, u32[]{:S(2)}, u32[]{:S(2)}) collective-permute-start(bf16[336,128]{1,0:T(8,128)(2,1)S(1)} %collective-permute-done.10.refs_3_), channel_id=1, source_target_pairs={{0,1},{1,0},{2,3},{3,2},{4,5},{5,4},{6,7},{7,6},{8,9},{9,8},{10,11... | collective-permute-start | bytes 258056 | tf_op jit(solution)/shard_map/ppermute | solution.py:517
  32.4 4.4 %collective-permute-start.15 = (bf16[256,128]{1,0:T(8,128)(2,1)S(1)}, bf16[256,128]{1,0:T(8,128)(2,1)S(1)}, u32[]{:S(2)}, u32[]{:S(2)}) collective-permute-start(bf16[256,128]{1,0:T(8,128)(2,1)S(1)} %get-tuple-element.49), channel_id=1, source_target_pairs={{0,2},{1,3},{2,0},{3,1},{4,6},{5,7},{6,4},{7,5},{8,10},{9,11},{10,... | collective-permute-start | bytes 196616 | tf_op jit(solution)/shard_map/ppermute | solution.py:517
